TPU v7x, 256 devices: a 4x2x16 block of a 4x16x16 slice. The times are simulated.
256 devices in a mesh: grp: 2 (over y), gx: 16 (over z), gy: 4 (over x), gz: 2 (over core).
Axes of the slice: x: 4, y: 2, z: 16, core: 2. Of those that a mesh axis runs over, the one named last changes fastest.
The devices are a block of a 4x16x16 slice.
Arguments:
- observed: float32 [16384, 4, 256], P(('grp', 'gx', 'gy', 'gz')), parts along dimension 0, may hold values from -12 to 12
- predicted: float32 [16384, 4, 256], P(('grp', 'gx', 'gy', 'gz')), parts along dimension 0, may hold values from -6 to 6
- coherence_mask: int32 [16384, 256], P(('grp', 'gx', 'gy', 'gz')), parts along dimension 0, may hold values 0 or 1
- block_count: int32 [16384], P(('grp', 'gx', 'gy', 'gz')), parts along dimension 0, may hold values from 64 to 256
- block_owner: int32 [16384, 1], P(('grp', 'gx', 'gy', 'gz')), parts along dimension 0, may hold values from 0 to 63; in each aligned block of 64 rows (0 to 63, 64 to 127, ...) at most 4 rows name the same one
- block_matrix_choice: int32 [16384], P(('grp', 'gx', 'gy', 'gz')), parts along dimension 0, may hold values from 0 to 31
- block_patch: int32 [16384], P(('grp', 'gx', 'gy', 'gz')), parts along dimension 0, may hold values from 0 to 31
- look_vector: float32 [4, 3], replicated, may hold values from -1 to 1
- interp_weights: bfloat16 [32, 256, 128], replicated, may hold values from -0.375 to 0.375
- depth_kernel: float32 [64], P(('grp', 'gz')), parts along dimension 0, may hold values from 0.2 to 1
- stiffness: float32 [64, 512, 512], P(('grp', 'gz'), 'gx', 'gy'), parts along dimension 0, may hold values from 0.25 to 4
Outputs:
- adjoint_field: float32 [3, 64, 512, 512], P(None, ('grp', 'gz'), 'gx', 'gy'), parts along dimension 1
- cg_residual: float32 [3, 64, 512, 512], P(None, ('grp', 'gz'), 'gx', 'gy'), parts along dimension 1
There are 2 independent parts, one for each index of `grp`. A program takes and returns all parts, laid end to end along the dimension named above; an argument that names none is the same for every part. Nothing has to cross between parts.
Inputs may be any that keep to these rules, and one draw needn't show every extreme that they name: `block_owner`: the blocks of one device name no column tile more than 4 times; in some devices one tile is named exactly 4 times.
All inputs are finite; a program needn't handle non-finite values. No bound on the sum of `coherence_mask` on one device may be relied on, other than what follows from the above.
Results may differ from a plain program's by a relative error of at most 0.0029.
Values sent between devices are 32-bit elements; how exact they have to be, the bound alone decides.
No kernel may reach another device: no remote copies, remote signals or barrier semaphores. Data moves between devices by JAX's collectives and lax.ppermute only.
A program may use at most 64 MiB of HBM per device.

v0:
```python
import functools

import jax
import jax.numpy as jnp
from jax import lax
from jax.experimental import pallas as pl
from jax.experimental.pallas import tpu as pltpu
from jax.sharding import PartitionSpec as P

EPOCHS = 4
PATCH_X = 8
PATCH_Y = 16
CAP = 4
LANES = 128
EPS = 1e-06
SHIFT = 8.0
REACH = 4
EDGE = 8
F32 = jnp.float32
VMEM = pl.BlockSpec(memory_space=pltpu.VMEM)
SMEM = pl.BlockSpec(memory_space=pltpu.SMEM)


def block_sums_kernel(owner_ref, patch_ref, coeffs_ref, choice_ref, weights_ref, out_ref, sums_ref, used_ref):
    step = pl.program_id(0)
    blocks = owner_ref.shape[0]
    tables = weights_ref.shape[0]
    owners = out_ref.shape[1]
    choice = choice_ref[...]
    coeffs = coeffs_ref[...]

    @pl.when(step == 0)
    def _():
        sums_ref[...] = jnp.zeros_like(sums_ref)

    total = sums_ref[...]
    for t in range(tables):
        product = jnp.dot(coeffs, weights_ref[t], preferred_element_type=F32)
        total = jnp.where(choice == step * tables + t, product, total)
    sums_ref[...] = total

    @pl.when(step == pl.num_programs(0) - 1)
    def _():
        out_ref[...] = jnp.zeros_like(out_ref)
        lane = lax.broadcasted_iota(jnp.int32, (1, LANES), 1)

        def clear(o, carry):
            used_ref[o] = 0
            return carry

        lax.fori_loop(0, owners, clear, 0)

        def put(b, carry):
            o = owner_ref[b]
            r = used_ref[o]
            used_ref[o] = r + 1
            for c in range(3):
                out_ref[r * 3 + c, pl.ds(o, 1), :] = sums_ref[pl.ds(c * blocks + b, 1), :]
            ids = out_ref[3 * CAP, pl.ds(o, 1), :]
            out_ref[3 * CAP, pl.ds(o, 1), :] = jnp.where(lane == r, patch_ref[b].astype(F32), ids)
            return carry

        lax.fori_loop(0, blocks, put, 0)


def block_sums(owner, patch, coeffs, choice, weights, owners):
    tables, pixels, cells = weights.shape
    blocks = owner.shape[0]
    steps = 8
    per = tables // steps
    return pl.pallas_call(
        block_sums_kernel,
        grid=(steps,),
        out_shape=jax.ShapeDtypeStruct((3 * CAP + 1, owners, cells), F32),
        in_specs=[
            SMEM,
            SMEM,
            pl.BlockSpec((3 * blocks, pixels), lambda i: (0, 0)),
            pl.BlockSpec((3 * blocks, LANES), lambda i: (0, 0)),
            pl.BlockSpec((per, pixels, cells), lambda i: (i, 0, 0)),
        ],
        out_specs=pl.BlockSpec((3 * CAP + 1, owners, cells), lambda i: (0, 0, 0)),
        scratch_shapes=[pltpu.VMEM((3 * blocks, cells), F32), pltpu.SMEM((owners,), jnp.int32)],
        name="block_sums",
    )(owner, patch, coeffs, choice, weights)


def swap_granules(tile, size):
    count = tile.shape[0]
    lanes = tile.shape[1]
    row = lax.broadcasted_iota(jnp.int32, tile.shape, 0)
    granule = lax.broadcasted_iota(jnp.int32, tile.shape, 1) // size
    k = 1
    while k < count:
        low = (row & k) == 0
        same = low == ((granule & k) == 0)
        up = pltpu.roll(pltpu.roll(tile, count - k, 0), k * size, 1)
        down = pltpu.roll(pltpu.roll(tile, k, 0), lanes - k * size, 1)
        tile = jnp.where(same, tile, jnp.where(low, up, down))
        k *= 2
    return tile


def place_kernel(got_ref, out_ref):
    sources, cells = got_ref.shape[1:]
    local_x, local_y = out_ref.shape[1:]
    places_x, places_y = local_x // PATCH_X, local_y // PATCH_Y
    places = places_x * places_y
    place = lax.broadcasted_iota(jnp.int32, (sources, places), 1).astype(F32)
    ids = got_ref[3 * CAP]
    total = jnp.zeros((places, 3 * cells), F32)
    for r in range(CAP):
        hot = (ids[:, r : r + 1] == place).astype(F32)
        total += lax.dot_general(
            hot,
            jnp.concatenate([got_ref[3 * r + c] for c in range(3)], axis=1),
            (((0,), (0,)), ((), ())),
            precision=lax.Precision.HIGHEST,
            preferred_element_type=F32,
        )
    for c in range(3):
        for i in range(places_x):
            tile = total[i * places_y : (i + 1) * places_y, c * cells : (c + 1) * cells]
            out_ref[c, i * PATCH_X : (i + 1) * PATCH_X, :] = swap_granules(tile, PATCH_Y)


def place(got, local_x, local_y):
    return pl.pallas_call(
        place_kernel,
        out_shape=jax.ShapeDtypeStruct((3, local_x, local_y), F32),
        in_specs=[VMEM],
        out_specs=VMEM,
        name="place",
    )(got)


def lane_steps(own, side):
    lane = lax.broadcasted_iota(jnp.int32, own.shape, 1)
    last, first = lane == LANES - 1, lane == 0
    a0, a1 = pltpu.roll(own, LANES - 1, 1), pltpu.roll(side, LANES - 1, 1)
    b0, b1 = pltpu.roll(own, 1, 1), pltpu.roll(side, 1, 1)
    ahead = (jnp.where(last, a1, a0), jnp.where(last, a0, a1))
    behind = (jnp.where(first, b1, b0), jnp.where(first, b0, b1))
    return ahead, behind


def powers_kernel(
    at_ref, depth_ref, beyond_ref, own_ref, left_ref, right_ref, stiff_ref, stiff_side_ref, stiff_beyond_ref,
    tally_ref, one_ref, two_ref, three_ref, row_ref, flat, keep, diag, w1, w2, div,
):
    layers, rows = stiff_ref.shape[0], stiff_ref.shape[1]
    local_x = one_ref.shape[2]
    upper = at_ref[0] == 1
    sign = jnp.where(upper, -1.0, 1.0).astype(F32)
    tall = own_ref.shape[1]

    def layer_of(z):
        return jnp.where(upper, layers - 1 - z, z)

    def depth(z):
        inner = depth_ref[layer_of(jnp.clip(z, 0, layers - 1))]
        outer = beyond_ref[layer_of(jnp.clip(z - layers, 0, layers - 1))]
        return jnp.where(z < 0, 0.0, jnp.where(z < layers, inner, outer))

    lane = lax.broadcasted_iota(jnp.int32, (tall, LANES), 1)
    line = lax.broadcasted_iota(jnp.int32, (tall, LANES), 0)
    outside_x = ((line < EDGE) & (at_ref[1] == 1)) | ((line >= tall - EDGE) & (at_ref[2] == 1))
    half = lane < LANES // 2
    outside_y = (half & (at_ref[4] == 1)) | (jnp.logical_not(half) & (at_ref[3] == 1))
    in0 = jnp.where(outside_x, 0.0, 1.0)
    in1 = jnp.where(outside_x | outside_y, 0.0, 1.0)
    inside = (in0, in1)

    def tiles(c):
        return own_ref[c], jnp.where(half, right_ref[c], left_ref[c])

    def down(v):
        return pltpu.roll(v, tall - 1, 0)

    def up(v):
        return pltpu.roll(v, 1, 0)

    s = [tiles(0), tiles(1), tuple(sign * v for v in tiles(2))]
    moved = [lane_steps(*v) for v in s]
    grad = tuple(
        inside[t] * 0.5 * (down(s[0][t]) - up(s[0][t]) + moved[1][0][t] - moved[1][1][t]) for t in range(2)
    )
    grad_moved = lane_steps(*grad)
    for t in range(2):
        around = [down(s[c][t]) + up(s[c][t]) + moved[c][0][t] + moved[c][1][t] for c in range(3)]
        keep[t] = inside[t]
        for c in range(3):
            flat[t, c] = s[c][t]
        flat[t, 3] = inside[t] * (-around[0] - 0.25 * (down(grad[t]) - up(grad[t])))
        flat[t, 4] = inside[t] * (-around[1] - 0.25 * (grad_moved[0][t] - grad_moved[1][t]))
        flat[t, 5] = inside[t] * (-around[2])
        flat[t, 6] = inside[t] * (-0.25) * (down(s[2][t]) - up(s[2][t]))
        flat[t, 7] = inside[t] * (-0.25) * (moved[2][0][t] - moved[2][1][t])
        flat[t, 8] = inside[t] * (-0.5) * grad[t]

    first = EDGE - REACH
    body = pl.ds(EDGE, rows)
    ahead_x, behind_x = pl.ds(EDGE + 1, rows), pl.ds(EDGE - 1, rows)
    flat_rows = pl.ds(first, rows)

    def apply_first(z, carry):
        d = depth(z)
        before, after = depth(z - 1), depth(z + 1)
        slope = 0.5 * (after - before)
        slope_after = 0.5 * (depth(z + 2) - d)
        slope_before = jnp.where(z > 0, 0.5 * (d - depth(z - 2)), 0.0)
        bend = 0.5 * (slope_after - slope_before)
        sides = before + after
        z_in = layer_of(jnp.minimum(z, layers - 1))
        z_out = jnp.clip(jnp.where(upper, REACH - 1 - (z - layers), z - layers), 0, REACH - 1)
        for t in range(2):
            inner = (stiff_ref if t == 0 else stiff_side_ref)[z_in]
            stiff = jnp.where(z < layers, inner, stiff_beyond_ref[t, z_out])
            centre = stiff + (6.0 - SHIFT)
            diag[z, t] = centre
            for c in range(3):
                v = flat[t, c, flat_rows, :]
                rest = flat[t, 3 + c, flat_rows, :]
                cross = flat[t, 6 + c, flat_rows, :]
                own_part = sides if c < 2 else sides + 0.5 * bend
                w1[c, z + 1, t, body, :] = d * (centre * v + rest) - own_part * v + slope * cross
        return carry

    for c in range(3):
        for t in range(2):
            w1[c, 0, t] = jnp.zeros_like(w1[c, 0, t])
            w2[c, 0, t] = jnp.zeros_like(w2[c, 0, t])
    for t in range(2):
        div[0, t] = jnp.zeros_like(div[0, t])
    lax.fori_loop(0, layers + REACH, apply_first, 0)

    def spread(w, z):
        ahead, behind = lane_steps(w[1, z, 0, body, :], w[1, z, 1, body, :])
        for t in range(2):
            total = w[0, z, t, ahead_x, :] - w[0, z, t, behind_x, :] + ahead[t] - behind[t]
            total += w[2, z + 1, t, body, :] - w[2, z - 1, t, body, :]
            div[z, t, body, :] = keep[t, flat_rows, :] * total

    def spread_first(z, carry):
        spread(w1, z + 1)
        return carry

    lax.fori_loop(0, layers + REACH - 1, spread_first, 0)

    def apply_second(z, carry):
        ahead, behind = lane_steps(div[z + 1, 0, body, :], div[z + 1, 1, body, :])
        for c in range(3):
            yp, ym = lane_steps(w1[c, z + 1, 0, body, :], w1[c, z + 1, 1, body, :])
            for t in range(2):
                around = w1[c, z + 1, t, ahead_x, :] + w1[c, z + 1, t, behind_x, :] + yp[t] + ym[t]
                around += w1[c, z, t, body, :] + w1[c, z + 2, t, body, :]
                if c == 0:
                    slope = div[z + 1, t, ahead_x, :] - div[z + 1, t, behind_x, :]
                elif c == 1:
                    slope = ahead[t] - behind[t]
                else:
                    slope = div[z + 2, t, body, :] - div[z, t, body, :]
                value = diag[z, t] * w1[c, z + 1, t, body, :] - around - 0.125 * slope
                w2[c, z + 1, t, body, :] = keep[t, flat_rows, :] * value
        return carry

    lax.fori_loop(0, layers + REACH - 2, apply_second, 0)

    def spread_second(z, carry):
        spread(w2, z + 1)
        return carry

    lax.fori_loop(0, layers + REACH // 4, spread_second, 0)

    lo = EDGE + REACH
    mid = pl.ds(lo, local_x)
    mid_ahead, mid_behind = pl.ds(lo + 1, local_x), pl.ds(lo - 1, local_x)
    narrow = lax.broadcasted_iota(jnp.int32, (local_x, LANES), 1)
    at_last, at_first = narrow == LANES - 1, narrow == 0

    def sides_of(own, side):
        ahead = jnp.where(at_last, pltpu.roll(side, LANES - 1, 1), pltpu.roll(own, LANES - 1, 1))
        behind = jnp.where(at_first, pltpu.roll(side, 1, 1), pltpu.roll(own, 1, 1))
        return ahead, behind

    def fold(v):
        out = v[0:8]
        for k in range(8, local_x, 8):
            out += v[k : k + 8]
        return out

    def apply_third(z, sums):
        sums = list(sums)
        d = depth(z)
        z_out = layer_of(z)
        ahead, behind = sides_of(div[z + 1, 0, mid, :], div[z + 1, 1, mid, :])
        for c in range(3):
            centre = w2[c, z + 1, 0, mid, :]
            yp, ym = sides_of(centre, w2[c, z + 1, 1, mid, :])
            around = w2[c, z + 1, 0, mid_ahead, :] + w2[c, z + 1, 0, mid_behind, :] + yp + ym
            around += w2[c, z, 0, mid, :] + w2[c, z + 2, 0, mid, :]
            if c == 0:
                slope = div[z + 1, 0, mid_ahead, :] - div[z + 1, 0, mid_behind, :]
            elif c == 1:
                slope = ahead - behind
            else:
                slope = div[z + 2, 0, mid, :] - div[z, 0, mid, :]
            third = diag[z, 0, pl.ds(REACH, local_x), :] * centre - around - 0.125 * slope
            begin = d * flat[0, c, pl.ds(EDGE, local_x), :]
            once = w1[c, z + 1, 0, mid, :]
            factor = sign if c == 2 else None
            for ref, value in ((one_ref, once), (two_ref, centre), (three_ref, third)):
                ref[c, z_out] = value if factor is None else factor * value
            pairs = ((begin, begin), (begin, once), (once, once), (once, centre), (centre, centre), (centre, third))
            for k, (a, b) in enumerate(pairs):
                sums[k] = sums[k] + fold(a * b)
        return tuple(sums)

    zero = jnp.zeros((8, LANES), F32)
    sums = lax.fori_loop(0, layers, apply_third, (zero,) * 6)
    spot = lax.broadcasted_iota(jnp.int32, (1, row_ref.shape[1]), 1)
    row = jnp.zeros((1, row_ref.shape[1]), F32)
    for k in range(6):
        row = jnp.where(spot == k, jnp.sum(sums[k]), row)
    for k in range(2):
        row = jnp.where(spot == 6 + k, tally_ref[k], row)
    row_ref[...] = jnp.broadcast_to(row, row_ref.shape)


def powers(at, depth, beyond, own, left, right, stiff, stiff_side, stiff_beyond, tally, copies):
    layers, rows, lanes = stiff.shape
    tall = own.shape[1]
    local_x = tall - 2 * EDGE
    field = jax.ShapeDtypeStruct((3, layers, local_x, lanes), F32)
    deep = rows + 2 * EDGE
    return pl.pallas_call(
        powers_kernel,
        out_shape=(field, field, field, jax.ShapeDtypeStruct((copies, 16), F32)),
        in_specs=[SMEM] * 3 + [VMEM] * 6 + [SMEM],
        out_specs=(VMEM,) * 4,
        scratch_shapes=[
            pltpu.VMEM((2, 9, tall, lanes), F32),
            pltpu.VMEM((2, tall, lanes), F32),
            pltpu.VMEM((layers + REACH, 2, rows, lanes), F32),
            pltpu.VMEM((3, layers + REACH + 1, 2, deep, lanes), F32),
            pltpu.VMEM((3, layers + REACH - 1, 2, deep, lanes), F32),
            pltpu.VMEM((layers + REACH, 2, deep, lanes), F32),
        ],
        name="powers",
    )(at, depth, beyond, own, left, right, stiff, stiff_side, stiff_beyond, tally)


def step_factors(nu):
    def inner(a, b):
        total = None
        for i, u in enumerate(a):
            for j, v in enumerate(b):
                term = u * v * nu[i + j]
                total = term if total is None else total + term
        return total

    def applied(a):
        out = [SHIFT * u for u in a] + [jnp.zeros_like(nu[0])]
        for i, u in enumerate(a):
            out[i + 1] = out[i + 1] + u
        return out

    def plus(a, factor, b):
        size = max(len(a), len(b))
        out = []
        for i in range(size):
            if i >= len(b):
                out.append(a[i])
            elif i >= len(a):
                out.append(factor * b[i])
            else:
                out.append(a[i] + factor * b[i])
        return out

    one = jnp.ones_like(nu[0])
    resid, along = [one], [one]
    found = [jnp.zeros_like(one)]
    now = nu[0]
    for step in range(3):
        image = applied(along)
        alpha = now / inner(along, image)
        found = plus(found, alpha, along)
        resid = plus(resid, -alpha, image)
        if step < 2:
            new = inner(resid, resid)
            along = plus(resid, new / now, along)
            now = new
    return found, resid


def finish_kernel(depth_ref, got_ref, surface_ref, one_ref, two_ref, three_ref, field_ref, resid_ref):
    block = one_ref.shape[1]
    step = pl.program_id(0)
    totals = jnp.sum(got_ref[...], axis=0, keepdims=True)
    values = [totals[:, k : k + 1] for k in range(8)]
    found, resid = step_factors(values[:6])
    scale = lax.rsqrt(values[6] / (EPOCHS * values[7]) + EPS)
    found = [scale * v for v in found]
    resid = [scale * v for v in resid]
    for z in range(block):
        d = depth_ref[step * block + z]
        for c in range(3):
            begin = d * surface_ref[c]
            once, twice = one_ref[c, z], two_ref[c, z]
            field_ref[c, z] = found[0] * begin + found[1] * once + found[2] * twice
            resid_ref[c, z] = resid[0] * begin + resid[1] * once + resid[2] * twice + resid[3] * three_ref[c, z]


def finish(depth, got, surface, one, two, three):
    layers = one.shape[1]
    block = 4
    spec = pl.BlockSpec((3, block) + one.shape[2:], lambda i: (0, i, 0, 0))
    field = jax.ShapeDtypeStruct(one.shape, F32)
    return pl.pallas_call(
        finish_kernel,
        grid=(layers // block,),
        out_shape=(field, field),
        in_specs=[
            SMEM,
            pl.BlockSpec(got.shape, lambda i: (0, 0)),
            pl.BlockSpec(surface.shape, lambda i: (0, 0, 0)),
            spec,
            spec,
            spec,
        ],
        out_specs=(spec, spec),
        name="finish",
    )(depth, got, surface, one, two, three)


def from_below(value, axis):
    count = lax.axis_size(axis)
    return lax.ppermute(value, axis, [(i, i + 1) for i in range(count - 1)])


def from_above(value, axis):
    count = lax.axis_size(axis)
    return lax.ppermute(value, axis, [(i + 1, i) for i in range(count - 1)])


def from_partner(value, axis):
    return lax.ppermute(value, axis, [(0, 1), (1, 0)])


def beside(left, right):
    lane = lax.broadcasted_iota(jnp.int32, left.shape, left.ndim - 1)
    return jnp.where(lane < LANES // 2, right, left)


def per_device(
    observed,
    predicted,
    coherence_mask,
    block_count,
    block_owner,
    block_matrix_choice,
    block_patch,
    look_vector,
    interp_weights,
    depth_kernel,
    stiffness,
):
    blocks, _, pixels = observed.shape
    layers, local_x, local_y = stiffness.shape
    owners = lax.axis_size("gx") * lax.axis_size("gy")
    copies = owners * lax.axis_size("gz")
    gx, gy, gz = (lax.axis_index(a) for a in ("gx", "gy", "gz"))

    tall = jnp.concatenate(
        [
            from_below(stiffness[:, local_x - REACH :, :], "gx"),
            stiffness,
            from_above(stiffness[:, :REACH, :], "gx"),
        ],
        axis=1,
    )
    stiff_side = beside(from_below(tall, "gy"), from_above(tall, "gy"))
    start = jnp.where(gz == 0, layers - REACH, 0)
    stiff_beyond = from_partner(
        jnp.stack([lax.dynamic_slice_in_dim(v, start, REACH, axis=0) for v in (tall, stiff_side)]), "gz"
    )
    depth_beyond = from_partner(depth_kernel, "gz")

    column = lax.broadcasted_iota(jnp.int32, (blocks, pixels), 1)
    valid = coherence_mask.astype(F32) * (column < block_count[:, None]).astype(F32)
    resid = (predicted - observed) * valid[:, None, :]
    tally = jnp.stack([jnp.sum(resid * resid), jnp.sum(valid)])
    coeffs = jnp.stack(
        [sum(look_vector[e, c] * resid[:, e, :] for e in range(EPOCHS)) for c in range(3)]
    ).astype(jnp.bfloat16)
    choice = jnp.broadcast_to(block_matrix_choice[None, :, None], (3, blocks, LANES))
    sums = block_sums(
        block_owner[:, 0],
        block_patch,
        coeffs.reshape(3 * blocks, pixels),
        choice.reshape(3 * blocks, LANES),
        interp_weights,
        owners,
    )
    got = lax.all_to_all(sums, ("gx", "gy"), split_axis=1, concat_axis=1, tiled=True)
    part = place(got, local_x, local_y)
    surface = part + from_partner(part, "gz")
    own = jnp.concatenate(
        [
            from_below(surface[:, local_x - EDGE :, :], "gx"),
            surface,
            from_above(surface[:, :EDGE, :], "gx"),
        ],
        axis=1,
    )
    left, right = from_below(own, "gy"), from_above(own, "gy")
    at = jnp.stack(
        [
            gz,
            (gx == 0).astype(jnp.int32),
            (gx == lax.axis_size("gx") - 1).astype(jnp.int32),
            (gy == 0).astype(jnp.int32),
            (gy == lax.axis_size("gy") - 1).astype(jnp.int32),
        ]
    )
    one, two, three, rows = powers(
        at, depth_kernel, depth_beyond, own, left, right, tall, stiff_side, stiff_beyond, tally, copies
    )
    rows = lax.all_to_all(rows, ("gx", "gy", "gz"), split_axis=0, concat_axis=0, tiled=True)
    return finish(depth_kernel, rows, surface, one, two, three)


def solution(mesh):
    in_specs = (
        P(("grp", "gx", "gy", "gz"), None, None),
        P(("grp", "gx", "gy", "gz"), None, None),
        P(("grp", "gx", "gy", "gz"), None),
        P(("grp", "gx", "gy", "gz")),
        P(("grp", "gx", "gy", "gz"), None),
        P(("grp", "gx", "gy", "gz")),
        P(("grp", "gx", "gy", "gz")),
        P(),
        P(),
        P(("grp", "gz")),
        P(("grp", "gz"), "gx", "gy"),
    )
    out_specs = (P(None, ("grp", "gz"), "gx", "gy"), P(None, ("grp", "gz"), "gx", "gy"))
    return jax.shard_map(
        per_device, mesh=mesh, in_specs=in_specs, out_specs=out_specs, check_vma=False
    )
```

profile of v0, /device:TPU:33, one launch (start us, length us, event | category | flops | bytes accessed | tf_op | source)
XLA Modules:
  0.0 165.3 jit_solution(11076989754108563082)
XLA Ops:
  0.6 0.7 broadcast_in_dim.12
  1.3 0.1 broadcast_in_dim.13
  1.4 1.8 %fusion.8 = (f32[1,1]{1,0:T(1,128)}, f32[1,1]{1,0:T(1,128)}, f32[1,1]{1,0:T(1,128)}, f32[1,1]{1,0:T(1,128)}, f32[1,1]{1,0:T(1,128)}, /*index=5*/f32[1,1]{1,0:T(1...) fusion(f32[4,3]{1,0:T(4,128)} %param.18), kind=kLoop, calls=%fused_computation.23 | loop fusion | bytes 96 | tf_op jit(solution)/shard_map/slice | solution.py:494
  3.2 1.6 fusion.5
  4.8 1.7 %multiply_reduce_fusion = (f32[]{:T(128)}, f32[64,4,256]{2,0,1:T(8,128)S(1)}) fusion(f32[64,256]{1,0:T(8,128)S(1)} %get-tuple-element.13, f32[64,4,256]{2,1,0:T(4,128)} %param.11, f32[64,4,256]{2,1,0:T(4,128)} %param.12), kind=kLoop, calls=%fused_computation.3 | loop fusion | flops 262143 | bytes 851972 | tf_op jit(solution)/shard_map/reduce_sum | solution.py:492
  6.5 2.5 %fusion.3 = bf16[1,64,256]{2,1,0:T(8,128)(2,1)S(1)} fusion(f32[64,4,256]{2,0,1:T(8,128)S(1)} %get-tuple-element.11, f32[]{:T(128)} %bitcast.19, f32[]{:T(128)} %bitcast.18, f32[]{:T(128)} %bitcast.17, f32[]{:T(128)} %bitcast.16), kind=kLoop, calls=%fused_computation.17 | loop fusion | flops 131072 | bytes 294928 | tf_op jit(solution)/shard_map/add | solution.py:494
  9.0 5.2 %fusion.1 = (bf16[1,64,256]{2,1,0:T(8,128)(2,1)S(1)}, bf16[1,64,256]{2,1,0:T(8,128)(2,1)S(1)}) fusion(f32[64,4,256]{2,0,1:T(8,128)S(1)} %get-tuple-element.11, f32[]{:T(128)} %bitcast.9, f32[]{:T(128)} %bitcast.8, f32[]{:T(128)} %bitcast.7, f32[]{:T(128)} %bitcast.6, f32[]{:T(128)} %bitcast.14, f32[]{:T(128)} %bitcast.13, f32[]{:T(128)} %bitcast.12, f32[]{:T(128)} %bitcast.11), kind=kLoop, calls=%fused_computation.15 | loop fusion | flops 262144 | bytes 327712 | tf_op jit(solution)/shard_map/add | solution.py:494
  14.3 0.7 pad_maximum_fusion.2
  14.9 0.7 broadcast_in_dim.14.choice_ref
  15.6 7.4 %block_sums.1 = f32[13,64,128]{2,1,0:T(8,128)} custom-call(s32[64]{0:T(128)} %bitcast.38, s32[64]{0:T(128)} %patch_ref.1, bf16[192,256]{1,0:T(8,128)(2,1)} %bitcast.35, s32[192,128]{1,0:T(8,128)} %broadcast_in_dim.14.choice_ref, bf16[32,256,128]{2,1,0:T(8,128)(2,1)} %weights_ref.1), custom_call_target="tpu_custom_call" | custom-call | tf_op jit(solution)/shard_map/block_sums/pallas_call | solution.py:71
  23.0 2.1 %copy.23 = f32[13,64,128]{2,0,1:T(8,128)} copy(f32[13,64,128]{2,1,0:T(8,128)} %block_sums.1) | data formatting | bytes 851968 | tf_op jit(solution)/shard_map/block_sums/pallas_call | solution.py:71
  25.1 29.6 %all-to-all-start = ((f32[13,64,128]{2,0,1:T(8,128)}), f32[13,64,128]{2,0,1:T(8,128)S(1)}, u32[]{:S(2)}, u32[]{:S(2)}) async-start(f32[13,64,128]{2,0,1:T(8,128)} %copy.23), calls=%async_computation | async-start | bytes 1048576 | tf_op jit(solution)/shard_map/all_to_all | solution.py:505
  54.7 2.1 %collective-permute-start.6 = (f32[16,4,128]{2,1,0:T(4,128)S(1)}, f32[16,4,128]{2,1,0:T(4,128)S(1)}, u32[]{:S(2)}, u32[]{:S(2)}) collective-permute-start(f32[16,4,128]{2,1,0:T(4,128)S(1)} %get-tuple-element.14), channel_id=1, source_target_pairs={{0,8},{8,16},{16,24},{24,32},{32,40},{40,48},{48,56},{56,64},{64,7... | collective-permute-start | bytes 98312 | tf_op jit(solution)/shard_map/ppermute | solution.py:438
  56.8 1.3 collective-permute-start.7
  58.1 9.7 %collective-permute-done.6 = f32[16,4,128]{2,1,0:T(4,128)S(1)} collective-permute-done((f32[16,4,128]{2,1,0:T(4,128)S(1)}, f32[16,4,128]{2,1,0:T(4,128)S(1)}, u32[]{:S(2)}, u32[]{:S(2)}) %collective-permute-start.6) | collective-permute-done | bytes 32800 | tf_op jit(solution)/shard_map/ppermute | solution.py:438
  67.9 6.7 %collective-permute-done.7 = f32[16,4,128]{2,1,0:T(4,128)S(1)} collective-permute-done((f32[16,4,128]{2,1,0:T(4,128)S(1)}, f32[16,4,128]{2,1,0:T(4,128)S(1)}, u32[]{:S(2)}, u32[]{:S(2)}) %collective-permute-start.7) | collective-permute-done | bytes 32800 | tf_op jit(solution)/shard_map/ppermute | solution.py:443
  74.6 0.0 copy-start.1
  74.7 2.9 %collective-permute-start.9 = (f32[16,40,128]{2,1,0:T(8,128)S(1)}, f32[16,40,128]{2,1,0:T(8,128)S(1)}, u32[]{:S(2)}, u32[]{:S(2)}) collective-permute-start(f32[16,40,128]{2,1,0:T(8,128)S(1)} %pad_maximum_fusion.stiff_ref), channel_id=1, source_target_pairs={{0,2},{2,4},{4,6},{1,3},{3,5},{5,7},{8,10},{10,12},{12,14},{9,11},... | collective-permute-start | bytes 983048 | tf_op jit(solution)/shard_map/ppermute | solution.py:438
  77.5 1.3 collective-permute-start.8
  78.8 3.6 %collective-permute-start = (f32[16]{0:T(128)S(1)}, f32[16]{0:T(128)S(1)}, u32[]{:S(2)}, u32[]{:S(2)}) collective-permute-start(f32[16]{0:T(128)S(1)} %copy-done.8), channel_id=1, source_target_pairs={{0,1},{1,0},{2,3},{3,2},{4,5},{5,4},{6,7},{7,6},{8,9},{9,8},{10,11... | collective-permute-start | bytes 200 | tf_op jit(solution)/shard_map/ppermute | solution.py:447
  82.5 0.0 collective-permute-done.9
  82.5 3.4 %collective-permute-done.8 = f32[16,40,128]{2,1,0:T(8,128)S(1)} collective-permute-done((f32[16,40,128]{2,1,0:T(8,128)S(1)}, f32[16,40,128]{2,1,0:T(8,128)S(1)}, u32[]{:S(2)}, u32[]{:S(2)}) %collective-permute-start.8) | collective-permute-done | bytes 327712 | tf_op jit(solution)/shard_map/ppermute | solution.py:443
  85.9 0.0 all-to-all-done
  85.9 0.9 copy.24.got_ref
  86.8 2.3 %place.1 = f32[3,32,128]{2,1,0:T(8,128)} custom-call(f32[13,64,128]{2,1,0:T(8,128)} %copy.24.got_ref), custom_call_target="tpu_custom_call" | custom-call | tf_op jit(solution)/shard_map/place/pallas_call | solution.py:128
  89.1 4.2 %collective-permute-start.1 = (f32[3,32,128]{2,1,0:T(8,128)}, f32[3,32,128]{2,1,0:T(8,128)S(1)}, u32[]{:S(2)}, u32[]{:S(2)}) collective-permute-start(f32[3,32,128]{2,1,0:T(8,128)} %place.1), channel_id=1, source_target_pairs={{0,1},{1,0},{2,3},{3,2},{4,5},{5,4},{6,7},{7,6},{8,9},{9,8},{10,11... | collective-permute-start | bytes 147464 | tf_op jit(solution)/shard_map/ppermute | solution.py:447
  93.4 1.1 collective-permute-done.1
  94.5 0.8 add.122.surface_ref
  95.3 3.1 %collective-permute-start.2 = (f32[3,8,128]{2,1,0:T(8,128)S(1)}, f32[3,8,128]{2,1,0:T(8,128)S(1)}, u32[]{:S(2)}, u32[]{:S(2)}) collective-permute-start(f32[3,8,128]{2,1,0:T(8,128)S(1)} %get-tuple-element.18), channel_id=1, source_target_pairs={{0,8},{8,16},{16,24},{24,32},{32,40},{40,48},{48,56},{56,64},{64,7... | collective-permute-start | bytes 36872 | tf_op jit(solution)/shard_map/ppermute | solution.py:438
  98.4 1.3 collective-permute-start.3
  99.7 0.8 collective-permute-start.10
  100.5 0.0 collective-permute-done.2
  100.5 2.4 %collective-permute-done.3 = f32[3,8,128]{2,1,0:T(8,128)S(1)} collective-permute-done((f32[3,8,128]{2,1,0:T(8,128)S(1)}, f32[3,8,128]{2,1,0:T(8,128)S(1)}, u32[]{:S(2)}, u32[]{:S(2)}) %collective-permute-start.3) | collective-permute-done | bytes 12320 | tf_op jit(solution)/shard_map/ppermute | solution.py:443
  102.9 1.3 collective-permute-start.5
  104.2 4.0 %collective-permute-start.4 = (f32[3,48,128]{2,1,0:T(8,128)S(1)}, f32[3,48,128]{2,1,0:T(8,128)S(1)}, u32[]{:S(2)}, u32[]{:S(2)}) collective-permute-start(f32[3,48,128]{2,1,0:T(8,128)S(1)} %pad_maximum_fusion.3.own_ref), channel_id=1, source_target_pairs={{0,2},{2,4},{4,6},{1,3},{3,5},{5,7},{8,10},{10,12},{12,14},{9,11},... | collective-permute-start | bytes 221192 | tf_op jit(solution)/shard_map/ppermute | solution.py:438
  108.3 1.9 %pad_maximum_fusion.4.tally_ref = f32[2]{0:T(128)} fusion(f32[1]{0:T(128)} %bitcast.25, f32[1]{0:T(128)} %bitcast.24), kind=kLoop, calls=%fused_computation.18 | loop fusion | flops 2 | bytes 16 | tf_op jit(solution)/shard_map/stack | solution.py:492
  110.2 0.6 stack.64.at_ref
  110.8 0.0 collective-permute-done.beyond_ref
  110.8 0.0 collective-permute-done.10.stiff_beyond_ref
  110.8 0.0 copy-start.5
  110.8 0.0 collective-permute-done.4.left_ref
  110.8 0.5 copy-done.9
  111.4 0.1 copy-done.5
  111.4 0.0 copy-done.6
  111.5 0.6 copy-done.7
  112.1 12.8 %powers.1 = (f32[3,16,32,128]{3,2,1,0:T(8,128)}, f32[3,16,32,128]{3,2,1,0:T(8,128)}, f32[3,16,32,128]{3,2,1,0:T(8,128)}, f32[128,16]{1,0:T(8,128)}) custom-call(s32[5]{0:T(128)} %stack.64.at_ref, f32[16]{0:T(128)} %depth_ref.3, f32[16]{0:T(128)} %copy-done.9, f32[3,48,128]{2,1,0:T(8,128)} %copy-done.4, f32[3,48,128]{2,1,0:T(8,128)} %copy-done.7, ...), custom_call_target="tpu_custom_call" | custom-call | tf_op jit(solution)/shard_map/powers/pallas_call | solution.py:336
  124.9 35.8 %all_to_all.16 = f32[128,1,16]{2,1,0:T(1,128)} all-to-all(f32[128,1,16]{2,1,0:T(1,128)} %bitcast.37), channel_id=1, replica_groups=mesh['grp'=2,'gx'=16,'gy'=4,'gz'=2] {'gx','gy','gz'}, dimensions={0} | all-to-all | bytes 16384 | tf_op jit(solution)/shard_map/all_to_all | solution.py:529
  160.7 4.7 %finish.1 = (f32[3,16,32,128]{3,2,1,0:T(8,128)}, f32[3,16,32,128]{3,2,1,0:T(8,128)}) custom-call(f32[16]{0:T(128)} %depth_ref.3, f32[128,16]{1,0:T(8,128)} %bitcast.36, f32[3,32,128]{2,1,0:T(8,128)} %copy-done.2, f32[3,16,32,128]{3,2,1,0:T(8,128)} %get-tuple-element.7.one_ref, f32[3,16,32,128]{3,2,1,0:T(8,128)} %get-tuple-element.8.two_ref, ...), custom_call_target="tpu_custom_call" | custom-call | tf_op jit(solution)/shard_map/finish/pallas_call | solution.py:419
  (24 shorter events, 0.2 us)
Async XLA Ops:
  15.6 39.0 %copy-start.3 = (f32[16,32,128]{2,1,0:T(8,128)S(1)}, f32[16,32,128]{2,1,0:T(8,128)}, u32[]{:S(2)}) copy-start(f32[16,32,128]{2,1,0:T(8,128)} %param.21) | copy-start | bytes 786436
  15.6 63.2 %copy-start.8 = (f32[16]{0:T(128)S(1)}, f32[16]{0:T(128)}, u32[]{:S(2)}) copy-start(f32[16]{0:T(128)} %depth_ref.3) | copy-start | bytes 196
  25.1 60.8 %all-to-all-start = ((f32[13,64,128]{2,0,1:T(8,128)}), f32[13,64,128]{2,0,1:T(8,128)S(1)}, u32[]{:S(2)}, u32[]{:S(2)}) async-start(f32[13,64,128]{2,0,1:T(8,128)} %copy.23), calls=%async_computation | async-start | bytes 1048576 | tf_op jit(solution)/shard_map/all_to_all | solution.py:505
  54.7 13.1 %collective-permute-start.6 = (f32[16,4,128]{2,1,0:T(4,128)S(1)}, f32[16,4,128]{2,1,0:T(4,128)S(1)}, u32[]{:S(2)}, u32[]{:S(2)}) collective-permute-start(f32[16,4,128]{2,1,0:T(4,128)S(1)} %get-tuple-element.14), channel_id=1, source_target_pairs={{0,8},{8,16},{16,24},{24,32},{32,40},{40,48},{48,56},{56,64},{64,7... | collective-permute-start | bytes 98312 | tf_op jit(solution)/shard_map/ppermute | solution.py:438
  56.8 17.8 %collective-permute-start.7 = (f32[16,4,128]{2,1,0:T(4,128)S(1)}, f32[16,4,128]{2,1,0:T(4,128)S(1)}, u32[]{:S(2)}, u32[]{:S(2)}) collective-permute-start(f32[16,4,128]{2,1,0:T(4,128)S(1)} %get-tuple-element.15), channel_id=1, source_target_pairs={{8,0},{16,8},{24,16},{32,24},{40,32},{48,40},{56,48},{64,56},{72,6... | collective-permute-start | bytes 98312 | tf_op jit(solution)/shard_map/ppermute | solution.py:443
  74.6 36.2 %copy-start.1 = (f32[16,40,128]{2,1,0:T(8,128)}, f32[16,40,128]{2,1,0:T(8,128)S(1)}, u32[]{:S(2)}) copy-start(f32[16,40,128]{2,1,0:T(8,128)S(1)} %pad_maximum_fusion.stiff_ref) | copy-start | bytes 983044
  74.7 7.8 %collective-permute-start.9 = (f32[16,40,128]{2,1,0:T(8,128)S(1)}, f32[16,40,128]{2,1,0:T(8,128)S(1)}, u32[]{:S(2)}, u32[]{:S(2)}) collective-permute-start(f32[16,40,128]{2,1,0:T(8,128)S(1)} %pad_maximum_fusion.stiff_ref), channel_id=1, source_target_pairs={{0,2},{2,4},{4,6},{1,3},{3,5},{5,7},{8,10},{10,12},{12,14},{9,11},... | collective-permute-start | bytes 983048 | tf_op jit(solution)/shard_map/ppermute | solution.py:438
  77.5 8.3 %collective-permute-start.8 = (f32[16,40,128]{2,1,0:T(8,128)S(1)}, f32[16,40,128]{2,1,0:T(8,128)S(1)}, u32[]{:S(2)}, u32[]{:S(2)}) collective-permute-start(f32[16,40,128]{2,1,0:T(8,128)S(1)} %pad_maximum_fusion.stiff_ref), channel_id=1, source_target_pairs={{2,0},{4,2},{6,4},{3,1},{5,3},{7,5},{10,8},{12,10},{14,12},{11,9},... | collective-permute-start | bytes 983048 | tf_op jit(solution)/shard_map/ppermute | solution.py:443
  78.8 31.9 %collective-permute-start = (f32[16]{0:T(128)S(1)}, f32[16]{0:T(128)S(1)}, u32[]{:S(2)}, u32[]{:S(2)}) collective-permute-start(f32[16]{0:T(128)S(1)} %copy-done.8), channel_id=1, source_target_pairs={{0,1},{1,0},{2,3},{3,2},{4,5},{5,4},{6,7},{7,6},{8,9},{9,8},{10,11... | collective-permute-start | bytes 200 | tf_op jit(solution)/shard_map/ppermute | solution.py:447
  85.9 24.9 %copy-start = (f32[16,40,128]{2,1,0:T(8,128)}, f32[16,40,128]{2,1,0:T(8,128)S(1)}, u32[]{:S(2)}) copy-start(f32[16,40,128]{2,1,0:T(8,128)S(1)} %broadcast_select_fusion.stiff_side_ref) | copy-start | bytes 983044
  89.1 5.3 %collective-permute-start.1 = (f32[3,32,128]{2,1,0:T(8,128)}, f32[3,32,128]{2,1,0:T(8,128)S(1)}, u32[]{:S(2)}, u32[]{:S(2)}) collective-permute-start(f32[3,32,128]{2,1,0:T(8,128)} %place.1), channel_id=1, source_target_pairs={{0,1},{1,0},{2,3},{3,2},{4,5},{5,4},{6,7},{7,6},{8,9},{9,8},{10,11... | collective-permute-start | bytes 147464 | tf_op jit(solution)/shard_map/ppermute | solution.py:447
  95.3 65.4 %copy-start.2 = (f32[3,32,128]{2,1,0:T(8,128)}, f32[3,32,128]{2,1,0:T(8,128)S(1)}, u32[]{:S(2)}) copy-start(f32[3,32,128]{2,1,0:T(8,128)S(1)} %add.122.surface_ref) | copy-start | bytes 147460
  95.3 5.2 %collective-permute-start.2 = (f32[3,8,128]{2,1,0:T(8,128)S(1)}, f32[3,8,128]{2,1,0:T(8,128)S(1)}, u32[]{:S(2)}, u32[]{:S(2)}) collective-permute-start(f32[3,8,128]{2,1,0:T(8,128)S(1)} %get-tuple-element.18), channel_id=1, source_target_pairs={{0,8},{8,16},{16,24},{24,32},{32,40},{40,48},{48,56},{56,64},{64,7... | collective-permute-start | bytes 36872 | tf_op jit(solution)/shard_map/ppermute | solution.py:438
  98.4 4.5 %collective-permute-start.3 = (f32[3,8,128]{2,1,0:T(8,128)S(1)}, f32[3,8,128]{2,1,0:T(8,128)S(1)}, u32[]{:S(2)}, u32[]{:S(2)}) collective-permute-start(f32[3,8,128]{2,1,0:T(8,128)S(1)} %get-tuple-element.19), channel_id=1, source_target_pairs={{8,0},{16,8},{24,16},{32,24},{40,32},{48,40},{56,48},{64,56},{72,6... | collective-permute-start | bytes 36872 | tf_op jit(solution)/shard_map/ppermute | solution.py:443
  99.7 11.0 %collective-permute-start.10 = (f32[2,4,40,128]{3,2,1,0:T(8,128)S(1)}, f32[2,4,40,128]{3,2,1,0:T(8,128)S(1)}, u32[]{:S(2)}, u32[]{:S(2)}) collective-permute-start(f32[2,4,40,128]{3,2,1,0:T(8,128)S(1)} %pad_maximum_fusion.1), channel_id=1, source_target_pairs={{0,1},{1,0},{2,3},{3,2},{4,5},{5,4},{6,7},{7,6},{8,9},{9,8},{10,11... | collective-permute-start | bytes 491528 | tf_op jit(solution)/shard_map/ppermute | solution.py:447
  102.9 8.0 %copy-start.4 = (f32[3,48,128]{2,1,0:T(8,128)}, f32[3,48,128]{2,1,0:T(8,128)S(1)}, u32[]{:S(2)}) copy-start(f32[3,48,128]{2,1,0:T(8,128)S(1)} %pad_maximum_fusion.3.own_ref) | copy-start | bytes 221188
  102.9 7.9 %collective-permute-start.5 = (f32[3,48,128]{2,1,0:T(8,128)S(1)}, f32[3,48,128]{2,1,0:T(8,128)S(1)}, u32[]{:S(2)}, u32[]{:S(2)}) collective-permute-start(f32[3,48,128]{2,1,0:T(8,128)S(1)} %pad_maximum_fusion.3.own_ref), channel_id=1, source_target_pairs={{2,0},{4,2},{6,4},{3,1},{5,3},{7,5},{10,8},{12,10},{14,12},{11,9},... | collective-permute-start | bytes 221192 | tf_op jit(solution)/shard_map/ppermute | solution.py:443
  104.2 6.6 %collective-permute-start.4 = (f32[3,48,128]{2,1,0:T(8,128)S(1)}, f32[3,48,128]{2,1,0:T(8,128)S(1)}, u32[]{:S(2)}, u32[]{:S(2)}) collective-permute-start(f32[3,48,128]{2,1,0:T(8,128)S(1)} %pad_maximum_fusion.3.own_ref), channel_id=1, source_target_pairs={{0,2},{2,4},{4,6},{1,3},{3,5},{5,7},{8,10},{10,12},{12,14},{9,11},... | collective-permute-start | bytes 221192 | tf_op jit(solution)/shard_map/ppermute | solution.py:438
  110.8 0.6 copy-start.9
  110.8 0.7 copy-start.5
  110.8 0.7 copy-start.6
  111.5 0.6 copy-start.7
where the time goes:
time: 166 us; the launch traced here: 165 us
  starting transfers between devices  55.5 us (33%)
  blocking collectives  35.8 us (22%)
  Pallas kernels  27.2 us (16%)
  waiting for transfers between devices  23.3 us (14%)
  other arithmetic  14.5 us (9%)
  local copies, waits for them, and re-layouts  8.12 us (5%)
    all_to_all x1, blocking collectives, per_device(): lax.all_to_all(rows, ('gx', 'gy', 'gz'), split_axis=0, concat_axis=0, til...  35.8 us
    all_to_all x1, starting transfers between devices, per_device(): lax.all_to_all(sums, ('gx', 'gy'), split_axis=1, concat_axis=1, tiled=True)  29.6 us
    pallas_call x1, Pallas kernels, powers(): pl.pallas_call(powers_kernel, out_shape=(field, field, field, jax.ShapeDt...  12.8 us
    ppermute x4, waiting for transfers between devices, from_above(): return lax.ppermute(value, axis, [(i + 1, i) for i in range(count - 1)])  12.5 us
    ppermute x4, starting transfers between devices, from_below(): return lax.ppermute(value, axis, [(i, i + 1) for i in range(count - 1)])  12.1 us
    ppermute x4, waiting for transfers between devices, from_below(): return lax.ppermute(value, axis, [(i, i + 1) for i in range(count - 1)])  9.75 us
    ppermute x3, starting transfers between devices, from_partner(): return lax.ppermute(value, axis, [(0, 1), (1, 0)])  8.59 us
    add x2, other arithmetic, per_device(): sum((look_vector[e, c] * resid[:, e, :] for e in range(EPOCHS)))  7.72 us
  transfers between devices with their start and end apart: 12, of which 5 were waited for; matrix products, arithmetic and copies ran while one was open for 3% of the time, Pallas kernels for 1%

commit v1 on v0

--- a/solution.py
+++ b/solution.py
@@ -1,4 +1,5 @@
 import functools
+import math
 
 import jax
 import jax.numpy as jnp
@@ -16,73 +17,142 @@
 SHIFT = 8.0
 REACH = 4
 EDGE = 8
+ROW = 16
+PIECES = 4
 F32 = jnp.float32
 VMEM = pl.BlockSpec(memory_space=pltpu.VMEM)
 SMEM = pl.BlockSpec(memory_space=pltpu.SMEM)
 
 
-def block_sums_kernel(owner_ref, patch_ref, coeffs_ref, choice_ref, weights_ref, out_ref, sums_ref, used_ref):
-    step = pl.program_id(0)
+def column(ref, first, count, lanes):
+    row = lax.broadcasted_iota(jnp.int32, (count, lanes), 0)
+    out = jnp.full((count, lanes), ref[first], jnp.int32)
+    for i in range(1, count):
+        out = jnp.where(row == i, ref[first + i], out)
+    return out
+
+
+def project_kernel(count_ref, look_ref, observed_ref, predicted_ref, mask_ref, coeffs_ref, tally_ref):
+    blocks, _, pixels = observed_ref.shape
+    group = 16
+    place = lax.broadcasted_iota(jnp.int32, (group, pixels), 1)
+    squares = jnp.zeros((group, pixels), F32)
+    weight = jnp.zeros((group, pixels), F32)
+    for g in range(0, blocks, group):
+        rows = slice(g, g + group)
+        inside = place < column(count_ref, g, group, pixels)
+        valid = jnp.where(inside, mask_ref[rows, :].astype(F32), 0.0)
+        weight += valid
+        resid = []
+        for e in range(EPOCHS):
+            r = (predicted_ref[rows, e, :] - observed_ref[rows, e, :]) * valid
+            squares += r * r
+            resid.append(r)
+        for c in range(3):
+            total = look_ref[0, c] * resid[0]
+            for e in range(1, EPOCHS):
+                total += look_ref[e, c] * resid[e]
+            coeffs_ref[c * blocks + g : c * blocks + g + group, :] = total.astype(jnp.bfloat16)
+    spot = lax.broadcasted_iota(jnp.int32, tally_ref.shape, 1)
+    tally = jnp.where(spot == 6, jnp.sum(squares), 0.0)
+    tally_ref[...] = jnp.where(spot == 7, jnp.sum(weight), tally)
+
+
+def project(count, look, observed, predicted, mask):
+    blocks, _, pixels = observed.shape
+    return pl.pallas_call(
+        project_kernel,
+        out_shape=(
+            jax.ShapeDtypeStruct((3 * blocks, pixels), jnp.bfloat16),
+            jax.ShapeDtypeStruct((1, ROW), F32),
+        ),
+        in_specs=[SMEM, SMEM, VMEM, VMEM, VMEM],
+        out_specs=(VMEM, VMEM),
+        compiler_params=pltpu.CompilerParams(vmem_limit_bytes=8 << 20),
+        cost_estimate=pl.CostEstimate(flops=8_000_000, bytes_accessed=1 << 20, transcendentals=0),
+        name="project",
+    )(count, look, observed, predicted, mask)
+
+
+def block_sums_kernel(
+    owner_ref, patch_ref, choice_ref, coeffs_ref, weights_ref, below_ref, own_ref, above_ref,
+    out_ref, tall_ref, packed_ref, sums_ref, slots_ref, used_ref, ids_ref, rank_ref,
+):
     blocks = owner_ref.shape[0]
     tables = weights_ref.shape[0]
-    owners = out_ref.shape[1]
-    choice = choice_ref[...]
+    owners, lanes = slots_ref.shape[1:]
+
+    layers, local_x = own_ref.shape[:2]
+    lane = lax.broadcasted_iota(jnp.int32, (local_x + 2 * REACH, lanes), 1)
+    packed = jnp.zeros((local_x + 2 * REACH, lanes), F32)
+    for z in range(layers):
+        tall_ref[z, 0:REACH, :] = below_ref[z]
+        tall_ref[z, REACH : REACH + local_x, :] = own_ref[z]
+        tall_ref[z, REACH + local_x :, :] = above_ref[z]
+        moved = pltpu.roll(tall_ref[z], (2 * REACH * z + REACH) % lanes, 1)
+        packed = jnp.where(lane // (2 * REACH) == z, moved, packed)
+    packed_ref[...] = packed
+
+    for o in range(owners):
+        used_ref[o] = 0
+        for r in range(CAP):
+            ids_ref[o * CAP + r] = 0
+    for b in range(blocks):
+        o = owner_ref[b]
+        r = used_ref[o]
+        used_ref[o] = r + 1
+        rank_ref[b] = r
+        ids_ref[o * CAP + r] = patch_ref[b]
+
+    choice = jnp.concatenate([column(choice_ref, g, 8, lanes) for g in range(0, blocks, 8)] * 3, axis=0)
     coeffs = coeffs_ref[...]
-
-    @pl.when(step == 0)
-    def _():
-        sums_ref[...] = jnp.zeros_like(sums_ref)
-
-    total = sums_ref[...]
+    total = jnp.zeros(sums_ref.shape, F32)
     for t in range(tables):
         product = jnp.dot(coeffs, weights_ref[t], preferred_element_type=F32)
-        total = jnp.where(choice == step * tables + t, product, total)
+        total = jnp.where(choice == t, product, total)
     sums_ref[...] = total
 
-    @pl.when(step == pl.num_programs(0) - 1)
-    def _():
-        out_ref[...] = jnp.zeros_like(out_ref)
-        lane = lax.broadcasted_iota(jnp.int32, (1, LANES), 1)
-
-        def clear(o, carry):
-            used_ref[o] = 0
-            return carry
-
-        lax.fori_loop(0, owners, clear, 0)
-
-        def put(b, carry):
-            o = owner_ref[b]
-            r = used_ref[o]
-            used_ref[o] = r + 1
-            for c in range(3):
-                out_ref[r * 3 + c, pl.ds(o, 1), :] = sums_ref[pl.ds(c * blocks + b, 1), :]
-            ids = out_ref[3 * CAP, pl.ds(o, 1), :]
-            out_ref[3 * CAP, pl.ds(o, 1), :] = jnp.where(lane == r, patch_ref[b].astype(F32), ids)
-            return carry
-
-        lax.fori_loop(0, blocks, put, 0)
-
-
-def block_sums(owner, patch, coeffs, choice, weights, owners):
+    slots_ref[...] = jnp.zeros_like(slots_ref)
+    for b in range(blocks):
+        o, r = owner_ref[b], rank_ref[b]
+        for c in range(3):
+            slots_ref[r * 3 + c, pl.ds(o, 1), :] = sums_ref[c * blocks + b : c * blocks + b + 1, :]
+    for k in range(3 * CAP):
+        out_ref[:, k * lanes : (k + 1) * lanes] = slots_ref[k]
+    spot = lax.broadcasted_iota(jnp.int32, (8, lanes), 1)
+    spot = jnp.where(spot < CAP, lax.broadcasted_iota(jnp.int32, (8, lanes), 0) * CAP + spot, -1)
+    for g in range(0, owners, 8):
+        ids = jnp.zeros((8, lanes), jnp.int32)
+        for k in range(8 * CAP):
+            ids = jnp.where(spot == k, ids_ref[g * CAP + k], ids)
+        out_ref[g : g + 8, 3 * CAP * lanes :] = ids.astype(F32)
+
+
+def block_sums(owner, patch, choice, coeffs, weights, below, own, above, owners):
     tables, pixels, cells = weights.shape
     blocks = owner.shape[0]
-    steps = 8
-    per = tables // steps
+    layers, local_x, lanes = own.shape
+    rows = local_x + 2 * REACH
     return pl.pallas_call(
         block_sums_kernel,
-        grid=(steps,),
-        out_shape=jax.ShapeDtypeStruct((3 * CAP + 1, owners, cells), F32),
-        in_specs=[
-            SMEM,
-            SMEM,
-            pl.BlockSpec((3 * blocks, pixels), lambda i: (0, 0)),
-            pl.BlockSpec((3 * blocks, LANES), lambda i: (0, 0)),
-            pl.BlockSpec((per, pixels, cells), lambda i: (i, 0, 0)),
+        out_shape=(
+            jax.ShapeDtypeStruct((owners, (3 * CAP + 1) * cells), F32),
+            jax.ShapeDtypeStruct((layers, rows, lanes), F32),
+            jax.ShapeDtypeStruct((rows, lanes), F32),
+        ),
+        in_specs=[SMEM] * 3 + [VMEM] * 5,
+        out_specs=(VMEM,) * 3,
+        scratch_shapes=[
+            pltpu.VMEM((3 * blocks, cells), F32),
+            pltpu.VMEM((3 * CAP, owners, cells), F32),
+            pltpu.SMEM((owners,), jnp.int32),
+            pltpu.SMEM((owners * CAP,), jnp.int32),
+            pltpu.SMEM((blocks,), jnp.int32),
         ],
-        out_specs=pl.BlockSpec((3 * CAP + 1, owners, cells), lambda i: (0, 0, 0)),
-        scratch_shapes=[pltpu.VMEM((3 * blocks, cells), F32), pltpu.SMEM((owners,), jnp.int32)],
+        compiler_params=pltpu.CompilerParams(vmem_limit_bytes=8 << 20),
+        cost_estimate=pl.CostEstimate(flops=400_000_000, bytes_accessed=4 << 20, transcendentals=0),
         name="block_sums",
-    )(owner, patch, coeffs, choice, weights)
+    )(owner, patch, choice, coeffs, weights, below, own, above)
 
 
 def swap_granules(tile, size):
@@ -102,18 +172,19 @@
 
 
 def place_kernel(got_ref, out_ref):
-    sources, cells = got_ref.shape[1:]
+    sources = got_ref.shape[0]
+    cells = PATCH_X * PATCH_Y
     local_x, local_y = out_ref.shape[1:]
     places_x, places_y = local_x // PATCH_X, local_y // PATCH_Y
     places = places_x * places_y
     place = lax.broadcasted_iota(jnp.int32, (sources, places), 1).astype(F32)
-    ids = got_ref[3 * CAP]
+    ids = got_ref[:, 3 * CAP * cells :]
     total = jnp.zeros((places, 3 * cells), F32)
     for r in range(CAP):
         hot = (ids[:, r : r + 1] == place).astype(F32)
         total += lax.dot_general(
             hot,
-            jnp.concatenate([got_ref[3 * r + c] for c in range(3)], axis=1),
+            got_ref[:, r * 3 * cells : (r + 1) * 3 * cells],
             (((0,), (0,)), ((), ())),
             precision=lax.Precision.HIGHEST,
             preferred_element_type=F32,
@@ -130,6 +201,8 @@
         out_shape=jax.ShapeDtypeStruct((3, local_x, local_y), F32),
         in_specs=[VMEM],
         out_specs=VMEM,
+        compiler_params=pltpu.CompilerParams(vmem_limit_bytes=8 << 20),
+        cost_estimate=pl.CostEstimate(flops=40_000_000, bytes_accessed=1 << 19, transcendentals=0),
         name="place",
     )(got)
 
@@ -145,12 +218,17 @@
 
 
 def powers_kernel(
-    at_ref, depth_ref, beyond_ref, own_ref, left_ref, right_ref, stiff_ref, stiff_side_ref, stiff_beyond_ref,
+    sizes, at_ref, depth_ref, beyond_ref, own_ref, left_ref, right_ref, stiff_ref, side_ref, partner_ref,
     tally_ref, one_ref, two_ref, three_ref, row_ref, flat, keep, diag, w1, w2, div,
 ):
     layers, rows = stiff_ref.shape[0], stiff_ref.shape[1]
     local_x = one_ref.shape[2]
-    upper = at_ref[0] == 1
+    size_x, size_y, size_z = sizes
+    at = at_ref[0]
+    at_z = lax.rem(at, size_z)
+    at_y = lax.rem(lax.div(at, size_z), size_y)
+    at_x = lax.div(at, size_z * size_y)
+    upper = at_z == 1
     sign = jnp.where(upper, -1.0, 1.0).astype(F32)
     tall = own_ref.shape[1]
 
@@ -164,9 +242,9 @@
 
     lane = lax.broadcasted_iota(jnp.int32, (tall, LANES), 1)
     line = lax.broadcasted_iota(jnp.int32, (tall, LANES), 0)
-    outside_x = ((line < EDGE) & (at_ref[1] == 1)) | ((line >= tall - EDGE) & (at_ref[2] == 1))
+    outside_x = ((line < EDGE) & (at_x == 0)) | ((line >= tall - EDGE) & (at_x == size_x - 1))
     half = lane < LANES // 2
-    outside_y = (half & (at_ref[4] == 1)) | (jnp.logical_not(half) & (at_ref[3] == 1))
+    outside_y = (half & (at_y == size_y - 1)) | (jnp.logical_not(half) & (at_y == 0))
     in0 = jnp.where(outside_x, 0.0, 1.0)
     in1 = jnp.where(outside_x | outside_y, 0.0, 1.0)
     inside = (in0, in1)
@@ -213,9 +291,15 @@
         sides = before + after
         z_in = layer_of(jnp.minimum(z, layers - 1))
         z_out = jnp.clip(jnp.where(upper, REACH - 1 - (z - layers), z - layers), 0, REACH - 1)
+        here = z < layers
+        packed = jnp.where(here, side_ref[...], partner_ref[REACH])
+        which = jnp.where(here, z_in, jnp.where(upper, layers - REACH, 0) + z_out)
+        turn = LANES - REACH - 2 * REACH * which
         for t in range(2):
-            inner = (stiff_ref if t == 0 else stiff_side_ref)[z_in]
-            stiff = jnp.where(z < layers, inner, stiff_beyond_ref[t, z_out])
+            if t == 0:
+                stiff = jnp.where(here, stiff_ref[z_in], partner_ref[z_out])
+            else:
+                stiff = pltpu.roll(packed, turn, 1)
             centre = stiff + (6.0 - SHIFT)
             diag[z, t] = centre
             for c in range(3):
@@ -318,25 +402,23 @@
 
     zero = jnp.zeros((8, LANES), F32)
     sums = lax.fori_loop(0, layers, apply_third, (zero,) * 6)
-    spot = lax.broadcasted_iota(jnp.int32, (1, row_ref.shape[1]), 1)
-    row = jnp.zeros((1, row_ref.shape[1]), F32)
+    spot = lax.broadcasted_iota(jnp.int32, (1, ROW), 1)
+    row = tally_ref[...]
     for k in range(6):
         row = jnp.where(spot == k, jnp.sum(sums[k]), row)
-    for k in range(2):
-        row = jnp.where(spot == 6 + k, tally_ref[k], row)
     row_ref[...] = jnp.broadcast_to(row, row_ref.shape)
 
 
-def powers(at, depth, beyond, own, left, right, stiff, stiff_side, stiff_beyond, tally, copies):
+def powers(sizes, at, depth, beyond, own, left, right, stiff, side, partner, tally):
     layers, rows, lanes = stiff.shape
     tall = own.shape[1]
     local_x = tall - 2 * EDGE
     field = jax.ShapeDtypeStruct((3, layers, local_x, lanes), F32)
     deep = rows + 2 * EDGE
     return pl.pallas_call(
-        powers_kernel,
-        out_shape=(field, field, field, jax.ShapeDtypeStruct((copies, 16), F32)),
-        in_specs=[SMEM] * 3 + [VMEM] * 6 + [SMEM],
+        functools.partial(powers_kernel, sizes),
+        out_shape=(field, field, field, jax.ShapeDtypeStruct((math.prod(sizes), ROW), F32)),
+        in_specs=[SMEM] * 3 + [VMEM] * 7,
         out_specs=(VMEM,) * 4,
         scratch_shapes=[
             pltpu.VMEM((2, 9, tall, lanes), F32),
@@ -346,8 +428,10 @@
             pltpu.VMEM((3, layers + REACH - 1, 2, deep, lanes), F32),
             pltpu.VMEM((layers + REACH, 2, deep, lanes), F32),
         ],
+        compiler_params=pltpu.CompilerParams(vmem_limit_bytes=20 << 20),
+        cost_estimate=pl.CostEstimate(flops=100_000_000, bytes_accessed=4 << 20, transcendentals=0),
         name="powers",
-    )(at, depth, beyond, own, left, right, stiff, stiff_side, stiff_beyond, tally)
+    )(at, depth, beyond, own, left, right, stiff, side, partner, tally)
 
 
 def step_factors(nu):
@@ -393,42 +477,56 @@
     return found, resid
 
 
-def finish_kernel(depth_ref, got_ref, surface_ref, one_ref, two_ref, three_ref, field_ref, resid_ref):
-    block = one_ref.shape[1]
-    step = pl.program_id(0)
+def finish_kernel(
+    depth_ref, got_ref, surface_ref, one_ref, two_ref, three_ref, field_out, resid_out, field_ref, resid_ref, sems
+):
+    layers = one_ref.shape[1]
     totals = jnp.sum(got_ref[...], axis=0, keepdims=True)
     values = [totals[:, k : k + 1] for k in range(8)]
     found, resid = step_factors(values[:6])
     scale = lax.rsqrt(values[6] / (EPOCHS * values[7]) + EPS)
-    found = [scale * v for v in found]
-    resid = [scale * v for v in resid]
-    for z in range(block):
-        d = depth_ref[step * block + z]
-        for c in range(3):
-            begin = d * surface_ref[c]
-            once, twice = one_ref[c, z], two_ref[c, z]
-            field_ref[c, z] = found[0] * begin + found[1] * once + found[2] * twice
-            resid_ref[c, z] = resid[0] * begin + resid[1] * once + resid[2] * twice + resid[3] * three_ref[c, z]
+    shape = surface_ref.shape[1:]
+    found = [jnp.broadcast_to(scale * v, shape) for v in found]
+    resid = [jnp.broadcast_to(scale * v, shape) for v in resid]
+    chunk = layers // PIECES
+    copies = []
+    for piece in range(PIECES):
+        first = piece * chunk
+
+        def one_layer(k, carry, first=first):
+            z = first + k
+            d = depth_ref[z]
+            for c in range(3):
+                begin = d * surface_ref[c]
+                once, twice = one_ref[c, z], two_ref[c, z]
+                field_ref[c, z] = found[0] * begin + found[1] * once + found[2] * twice
+                resid_ref[c, z] = resid[0] * begin + resid[1] * once + resid[2] * twice + resid[3] * three_ref[c, z]
+            return carry
+
+        lax.fori_loop(0, chunk, one_layer, 0)
+        for k, (src, dst) in enumerate(((field_ref, field_out), (resid_ref, resid_out))):
+            part = pl.ds(first, chunk)
+            copy = pltpu.make_async_copy(src.at[:, part], dst.at[:, part], sems.at[k, piece])
+            copy.start()
+            copies.append(copy)
+    for copy in copies:
+        copy.wait()
 
 
 def finish(depth, got, surface, one, two, three):
-    layers = one.shape[1]
-    block = 4
-    spec = pl.BlockSpec((3, block) + one.shape[2:], lambda i: (0, i, 0, 0))
     field = jax.ShapeDtypeStruct(one.shape, F32)
     return pl.pallas_call(
         finish_kernel,
-        grid=(layers // block,),
         out_shape=(field, field),
-        in_specs=[
-            SMEM,
-            pl.BlockSpec(got.shape, lambda i: (0, 0)),
-            pl.BlockSpec(surface.shape, lambda i: (0, 0, 0)),
-            spec,
-            spec,
-            spec,
+        in_specs=[SMEM] + [VMEM] * 5,
+        out_specs=(pl.BlockSpec(memory_space=pl.ANY),) * 2,
+        scratch_shapes=[
+            pltpu.VMEM(one.shape, F32),
+            pltpu.VMEM(one.shape, F32),
+            pltpu.SemaphoreType.DMA((2, PIECES)),
         ],
-        out_specs=(spec, spec),
+        compiler_params=pltpu.CompilerParams(vmem_limit_bytes=12 << 20),
+        cost_estimate=pl.CostEstimate(flops=20_000_000, bytes_accessed=4 << 20, transcendentals=0),
         name="finish",
     )(depth, got, surface, one, two, three)
 
@@ -445,11 +543,6 @@
 
 def from_partner(value, axis):
     return lax.ppermute(value, axis, [(0, 1), (1, 0)])
-
-
-def beside(left, right):
-    lane = lax.broadcasted_iota(jnp.int32, left.shape, left.ndim - 1)
-    return jnp.where(lane < LANES // 2, right, left)
 
 
 def per_device(
@@ -465,44 +558,27 @@
     depth_kernel,
     stiffness,
 ):
-    blocks, _, pixels = observed.shape
     layers, local_x, local_y = stiffness.shape
-    owners = lax.axis_size("gx") * lax.axis_size("gy")
-    copies = owners * lax.axis_size("gz")
-    gx, gy, gz = (lax.axis_index(a) for a in ("gx", "gy", "gz"))
-
-    tall = jnp.concatenate(
-        [
-            from_below(stiffness[:, local_x - REACH :, :], "gx"),
-            stiffness,
-            from_above(stiffness[:, :REACH, :], "gx"),
-        ],
-        axis=1,
+    sizes = tuple(lax.axis_size(a) for a in ("gx", "gy", "gz"))
+    owners = sizes[0] * sizes[1]
+    at = lax.axis_index(("gx", "gy", "gz")).astype(jnp.int32).reshape(1)
+    upper = lax.axis_index("gz") == 1
+
+    below = from_below(stiffness[:, local_x - REACH :, :], "gx")
+    above = from_above(stiffness[:, :REACH, :], "gx")
+    coeffs, tally = project(block_count, look_vector, observed, predicted, coherence_mask)
+    sums, tall, packed = block_sums(
+        block_owner[:, 0], block_patch, block_matrix_choice, coeffs, interp_weights, below, stiffness, above, owners
     )
-    stiff_side = beside(from_below(tall, "gy"), from_above(tall, "gy"))
-    start = jnp.where(gz == 0, layers - REACH, 0)
-    stiff_beyond = from_partner(
-        jnp.stack([lax.dynamic_slice_in_dim(v, start, REACH, axis=0) for v in (tall, stiff_side)]), "gz"
-    )
+    packed_left, packed_right = from_below(packed, "gy"), from_above(packed, "gy")
+    got = lax.all_to_all(sums, ("gx", "gy"), split_axis=0, concat_axis=0, tiled=True)
+
+    lane = lax.broadcasted_iota(jnp.int32, packed.shape, 1)
+    side = jnp.where(lane % (2 * REACH) >= REACH, packed_right, packed_left)
+    near = jnp.where(upper, tall[:REACH], tall[layers - REACH :])
+    partner = from_partner(jnp.concatenate([near, side[None]]), "gz")
     depth_beyond = from_partner(depth_kernel, "gz")
 
-    column = lax.broadcasted_iota(jnp.int32, (blocks, pixels), 1)
-    valid = coherence_mask.astype(F32) * (column < block_count[:, None]).astype(F32)
-    resid = (predicted - observed) * valid[:, None, :]
-    tally = jnp.stack([jnp.sum(resid * resid), jnp.sum(valid)])
-    coeffs = jnp.stack(
-        [sum(look_vector[e, c] * resid[:, e, :] for e in range(EPOCHS)) for c in range(3)]
-    ).astype(jnp.bfloat16)
-    choice = jnp.broadcast_to(block_matrix_choice[None, :, None], (3, blocks, LANES))
-    sums = block_sums(
-        block_owner[:, 0],
-        block_patch,
-        coeffs.reshape(3 * blocks, pixels),
-        choice.reshape(3 * blocks, LANES),
-        interp_weights,
-        owners,
-    )
-    got = lax.all_to_all(sums, ("gx", "gy"), split_axis=1, concat_axis=1, tiled=True)
     part = place(got, local_x, local_y)
     surface = part + from_partner(part, "gz")
     own = jnp.concatenate(
@@ -514,17 +590,8 @@
         axis=1,
     )
     left, right = from_below(own, "gy"), from_above(own, "gy")
-    at = jnp.stack(
-        [
-            gz,
-            (gx == 0).astype(jnp.int32),
-            (gx == lax.axis_size("gx") - 1).astype(jnp.int32),
-            (gy == 0).astype(jnp.int32),
-            (gy == lax.axis_size("gy") - 1).astype(jnp.int32),
-        ]
-    )
     one, two, three, rows = powers(
-        at, depth_kernel, depth_beyond, own, left, right, tall, stiff_side, stiff_beyond, tally, copies
+        sizes, at, depth_kernel, depth_beyond, own, left, right, tall, side, partner, tally
     )
     rows = lax.all_to_all(rows, ("gx", "gy", "gz"), split_axis=0, concat_axis=0, tiled=True)
     return finish(depth_kernel, rows, surface, one, two, three)

time: 166 us -> 137 us (0.83)
  other arithmetic: 14.5 us -> 0.05 us
  Pallas kernels: 27.2 us -> 17.5 us
  blocking collectives: 35.8 us -> 27.4 us
  local copies, waits for them, and re-layouts: 8.12 us -> 10.7 us
    all_to_all x1, waiting for transfers between devices: 0.01 us -> 20.7 us  [per_device(): lax.all_to_all(sums, ('gx', 'gy'), split_axis=0, concat_axis=0, tiled=True)]
    ppermute x4, waiting for transfers between devices: 12.5 us -> 2.38 us  [from_above(): return lax.ppermute(value, axis, [(i + 1, i) for i in range(count - 1)])]
    ppermute x4, waiting for transfers between devices: 9.75 us -> 0.01 us  [from_below(): return lax.ppermute(value, axis, [(i, i + 1) for i in range(count - 1)])]
    all_to_all x1, blocking collectives: 35.8 us -> 27.4 us  [per_device(): lax.all_to_all(rows, ('gx', 'gy', 'gz'), split_axis=0, concat_axis=0, til...]
    pallas_call x3 -> x4, Pallas kernels: 24.9 us -> 16.8 us  [the longest x1 11.9 us: powers(): pl.pallas_call(functools.partial(powers_kernel, sizes), out_shape=(field,...]
    add x2 -> x0, other arithmetic: 7.72 us -> none  [per_device(): sum((look_vector[e, c] * resid[:, e, :] for e in range(EPOCHS)))]
    unnamed x20 -> x23, local copies, waits for them, and re-layouts: 1.27 us -> 8.6 us
    reduce_sum x2 -> x0, other arithmetic: 3.34 us -> none  [per_device(): tally = jnp.stack([jnp.sum(resid * resid), jnp.sum(valid)])]
  transfers between devices with their start and end apart: 12 -> 12, of which waited for: 5 -> 4; matrix products, arithmetic and copies ran while one was open for 3% -> 0% of each run, Pallas kernels for 1% -> 1%
where the time goes in v1:
time: 137 us; the launch traced here: 136 us
  starting transfers between devices  55.1 us (40%)
  blocking collectives  27.4 us (20%)
  waiting for transfers between devices  24.8 us (18%)
  Pallas kernels  17.5 us (13%)
  local copies, waits for them, and re-layouts  10.7 us (8%)
    all_to_all x1, starting transfers between devices, per_device(): lax.all_to_all(sums, ('gx', 'gy'), split_axis=0, concat_axis=0, tiled=True)  28.5 us
    all_to_all x1, blocking collectives, per_device(): lax.all_to_all(rows, ('gx', 'gy', 'gz'), split_axis=0, concat_axis=0, til...  27.4 us
    all_to_all x1, waiting for transfers between devices, per_device(): lax.all_to_all(sums, ('gx', 'gy'), split_axis=0, concat_axis=0, tiled=True)  20.7 us
    ppermute x4, starting transfers between devices, from_below(): return lax.ppermute(value, axis, [(i, i + 1) for i in range(count - 1)])  13.9 us
    pallas_call x1, Pallas kernels, powers(): pl.pallas_call(functools.partial(powers_kernel, sizes), out_shape=(field,...  11.9 us
    unnamed x23, local copies, waits for them, and re-layouts  8.6 us
    ppermute x3, starting transfers between devices, from_partner(): return lax.ppermute(value, axis, [(0, 1), (1, 0)])  7.4 us
    ppermute x4, starting transfers between devices, from_above(): return lax.ppermute(value, axis, [(i + 1, i) for i in range(count - 1)])  5.22 us
  transfers between devices with their start and end apart: 12, of which 4 were waited for; matrix products, arithmetic and copies ran while one was open for 0% of the time, Pallas kernels for 1%

profile of v1, /device:TPU:33, one launch (start us, length us, event | category | flops | bytes accessed | tf_op | source)
XLA Modules:
  0.0 136.4 jit_solution(17182763531810428466)
XLA Ops:
  0.6 0.9 fusion.1
  1.5 1.3 collective-permute-start.2
  2.8 5.9 %collective-permute-start.1 = (f32[16,4,128]{2,1,0:T(4,128)S(1)}, f32[16,4,128]{2,1,0:T(4,128)S(1)}, u32[]{:S(2)}, u32[]{:S(2)}) collective-permute-start(f32[16,4,128]{2,1,0:T(4,128)S(1)} %get-tuple-element.21), channel_id=1, source_target_pairs={{0,8},{8,16},{16,24},{24,32},{32,40},{40,48},{48,56},{56,64},{64,7... | collective-permute-start | bytes 98312 | tf_op jit(solution)/shard_map/ppermute | solution.py:536
  8.7 0.0 copy-start.2
  8.7 0.9 copy-done.2
  9.7 0.9 copy-done.3
  10.6 0.0 copy-start.4
  10.6 0.8 copy-done.4
  11.5 0.0 copy-start.5
  11.5 0.7 copy-done.5
  12.2 0.7 copy-done.10
  12.8 0.9 project.1
  13.7 0.0 collective-permute-done.2.above_ref
  13.7 0.0 collective-permute-done.1.below_ref
  13.7 0.0 copy-start
  13.7 1.6 %copy-done = bf16[32,256,128]{2,1,0:T(8,128)(2,1)S(1)} copy-done((bf16[32,256,128]{2,1,0:T(8,128)(2,1)S(1)}, bf16[32,256,128]{2,1,0:T(8,128)(2,1)}, u32[]{:S(2)}) %copy-start) | copy-done | bytes 2097176
  15.3 0.9 copy-done.1
  16.3 0.7 copy-done.7
  16.9 0.7 copy-done.8
  17.6 0.7 copy-done.9
  18.2 1.8 %block_sums.1 = (f32[64,1664]{1,0:T(8,128)S(1)}, f32[16,40,128]{2,1,0:T(8,128)S(1)}, f32[40,128]{1,0:T(8,128)S(1)}) custom-call(s32[64]{0:T(128)S(1)} %bitcast.16, s32[64]{0:T(128)S(1)} %copy-done.8, s32[64]{0:T(128)S(1)} %copy-done.9, bf16[192,256]{1,0:T(8,128)(2,1)S(1)} %get-tuple-element.11.coeffs_ref, bf16[32,256,128]{2,1,0:T(8,128)(2,1)S(1)} %copy-done, ...), custom_call_target="tpu_custom_call" | custom-call | flops 400000000 | bytes 4194304 | tf_op jit(solution)/shard_map/block_sums/pallas_call | solution.py:136
  20.1 0.0 copy-start.6
  20.1 1.2 copy.13
  21.3 28.5 %all-to-all-start = ((f32[64,1,1664]{2,1,0:T(1,128)}), f32[64,1,1664]{2,1,0:T(1,128)S(1)}, u32[]{:S(2)}, u32[]{:S(2)}) async-start(f32[64,1,1664]{2,1,0:T(1,128)} %copy.13), calls=%async_computation | async-start | bytes 851968 | tf_op jit(solution)/shard_map/all_to_all | solution.py:574
  49.8 2.1 %collective-permute-start.9 = (f32[40,128]{1,0:T(8,128)S(1)}, f32[40,128]{1,0:T(8,128)S(1)}, u32[]{:S(2)}, u32[]{:S(2)}) collective-permute-start(f32[40,128]{1,0:T(8,128)S(1)} %get-tuple-element.14), channel_id=1, source_target_pairs={{0,2},{2,4},{4,6},{1,3},{3,5},{5,7},{8,10},{10,12},{12,14},{9,11},... | collective-permute-start | bytes 61448 | tf_op jit(solution)/shard_map/ppermute | solution.py:536
  51.9 1.3 collective-permute-start.8
  53.2 20.7 %all-to-all-done = f32[64,1,1664]{2,1,0:T(1,128)S(1)} async-done(((f32[64,1,1664]{2,1,0:T(1,128)}), f32[64,1,1664]{2,1,0:T(1,128)S(1)}, u32[]{:S(2)}, u32[]{:S(2)}) %all-to-all-start) | async-done | bytes 426016 | tf_op jit(solution)/shard_map/all_to_all | solution.py:574
  74.0 0.7 place.1
  74.7 4.2 %collective-permute-start.3 = (f32[3,32,128]{2,1,0:T(8,128)S(1)}, f32[3,32,128]{2,1,0:T(8,128)S(1)}, u32[]{:S(2)}, u32[]{:S(2)}) collective-permute-start(f32[3,32,128]{2,1,0:T(8,128)S(1)} %place.1), channel_id=1, source_target_pairs={{0,1},{1,0},{2,3},{3,2},{4,5},{5,4},{6,7},{7,6},{8,9},{9,8},{10,11... | collective-permute-start | bytes 147464 | tf_op jit(solution)/shard_map/ppermute | solution.py:545
  78.9 0.0 collective-permute-done.9
  78.9 0.0 collective-permute-done.8
  78.9 0.9 collective-permute-done.3
  79.8 1.9 %collective-permute-start.4 = (f32[3,8,128]{2,1,0:T(8,128)S(1)}, f32[3,8,128]{2,1,0:T(8,128)S(1)}, u32[]{:S(2)}, u32[]{:S(2)}) collective-permute-start(f32[3,8,128]{2,1,0:T(8,128)S(1)} %get-tuple-element.22), channel_id=1, source_target_pairs={{0,8},{8,16},{16,24},{24,32},{32,40},{40,48},{48,56},{56,64},{64,7... | collective-permute-start | bytes 36872 | tf_op jit(solution)/shard_map/ppermute | solution.py:536
  81.7 1.3 collective-permute-start.5
  83.1 0.8 collective-permute-start.10
  83.8 0.0 collective-permute-done.4
  83.8 2.4 %collective-permute-done.5 = f32[3,8,128]{2,1,0:T(8,128)S(1)} collective-permute-done((f32[3,8,128]{2,1,0:T(8,128)S(1)}, f32[3,8,128]{2,1,0:T(8,128)S(1)}, u32[]{:S(2)}, u32[]{:S(2)}) %collective-permute-start.5) | collective-permute-done | bytes 12320 | tf_op jit(solution)/shard_map/ppermute | solution.py:541
  86.2 1.3 collective-permute-start.7
  87.5 4.0 %collective-permute-start.6 = (f32[3,48,128]{2,1,0:T(8,128)S(1)}, f32[3,48,128]{2,1,0:T(8,128)S(1)}, u32[]{:S(2)}, u32[]{:S(2)}) collective-permute-start(f32[3,48,128]{2,1,0:T(8,128)S(1)} %pad_maximum_fusion.1.own_ref), channel_id=1, source_target_pairs={{0,2},{2,4},{4,6},{1,3},{3,5},{5,7},{8,10},{10,12},{12,14},{9,11},... | collective-permute-start | bytes 221192 | tf_op jit(solution)/shard_map/ppermute | solution.py:536
  91.6 0.0 copy-done.6
  91.6 2.5 %collective-permute-start = (f32[16]{0:T(128)S(1)}, f32[16]{0:T(128)S(1)}, u32[]{:S(2)}, u32[]{:S(2)}) collective-permute-start(f32[16]{0:T(128)S(1)} %copy-done.6), channel_id=1, source_target_pairs={{0,1},{1,0},{2,3},{3,2},{4,5},{5,4},{6,7},{7,6},{8,9},{9,8},{10,11... | collective-permute-start | bytes 200 | tf_op jit(solution)/shard_map/ppermute | solution.py:545
  94.0 0.8 collective-permute-done.beyond_ref
  94.9 0.0 collective-permute-done.10.partner_ref
  94.9 0.0 collective-permute-done.7.right_ref
  94.9 0.0 collective-permute-done.6.left_ref
  94.9 11.9 %powers.1 = (f32[3,16,32,128]{3,2,1,0:T(8,128)S(1)}, f32[3,16,32,128]{3,2,1,0:T(8,128)S(1)}, f32[3,16,32,128]{3,2,1,0:T(8,128)S(1)}, f32[128,16]{1,0:T(8,128)S(1)}) custom-call(s32[1]{0:T(128)} %bitcast.at_ref, f32[16]{0:T(128)S(1)} %copy-done.6, f32[16]{0:T(128)S(1)} %collective-permute-done.beyond_ref, f32[3,48,128]{2,1,0:T(8,128)S(1)} %pad_maximum_fusion.1.own_ref, ...), custom_call_target="tpu_custom_call" | custom-call | flops 100000000 | bytes 4194304 | tf_op jit(solution)/shard_map/powers/pallas_call | solution.py:418
  106.8 27.4 %all_to_all.22 = f32[128,1,16]{2,1,0:T(1,128)S(1)} all-to-all(f32[128,1,16]{2,1,0:T(1,128)S(1)} %bitcast.15), channel_id=1, replica_groups=mesh['grp'=2,'gx'=16,'gy'=4,'gz'=2] {'gx','gy','gz'}, dimensions={0} | all-to-all | bytes 16384 | tf_op jit(solution)/shard_map/all_to_all | solution.py:596
  134.2 2.2 %finish.1 = (f32[3,16,32,128]{3,2,1,0:T(8,128)}, f32[3,16,32,128]{3,2,1,0:T(8,128)}) custom-call(f32[16]{0:T(128)S(1)} %copy-done.6, f32[128,16]{1,0:T(8,128)S(1)} %bitcast.13, f32[3,32,128]{2,1,0:T(8,128)S(1)} %add.18.surface_ref, f32[3,16,32,128]{3,2,1,0:T(8,128)S(1)} %get-tuple-element.17.one_ref, f32[3,16,32,128]{3,2,1,0:T(8,128)S(1)} %get-tuple-element.18.two_ref, ...), custom_call_target="tpu_custom_call" | custom-call | flops 20000000 | bytes 4194304 | tf_op jit(solution)/shard_map/finish/pallas_call | solution.py:518
  (15 shorter events, 0.1 us)
Async XLA Ops:
  1.5 12.2 %collective-permute-start.2 = (f32[16,4,128]{2,1,0:T(4,128)S(1)}, f32[16,4,128]{2,1,0:T(4,128)S(1)}, u32[]{:S(2)}, u32[]{:S(2)}) collective-permute-start(f32[16,4,128]{2,1,0:T(4,128)S(1)} %get-tuple-element.20), channel_id=1, source_target_pairs={{8,0},{16,8},{24,16},{32,24},{40,32},{48,40},{56,48},{64,56},{72,6... | collective-permute-start | bytes 98312 | tf_op jit(solution)/shard_map/ppermute | solution.py:541
  2.8 10.9 %collective-permute-start.1 = (f32[16,4,128]{2,1,0:T(4,128)S(1)}, f32[16,4,128]{2,1,0:T(4,128)S(1)}, u32[]{:S(2)}, u32[]{:S(2)}) collective-permute-start(f32[16,4,128]{2,1,0:T(4,128)S(1)} %get-tuple-element.21), channel_id=1, source_target_pairs={{0,8},{8,16},{16,24},{24,32},{32,40},{40,48},{48,56},{56,64},{64,7... | collective-permute-start | bytes 98312 | tf_op jit(solution)/shard_map/ppermute | solution.py:536
  8.7 1.0 copy-start.2
  9.7 0.9 copy-start.3
  10.6 0.8 copy-start.4
  11.5 0.7 copy-start.5
  12.2 0.7 copy-start.10
  13.7 1.6 %copy-start = (bf16[32,256,128]{2,1,0:T(8,128)(2,1)S(1)}, bf16[32,256,128]{2,1,0:T(8,128)(2,1)}, u32[]{:S(2)}) copy-start(bf16[32,256,128]{2,1,0:T(8,128)(2,1)} %weights_ref.1) | copy-start | bytes 6291460
  15.3 0.9 copy-start.1
  16.3 0.7 copy-start.7
  16.9 0.7 copy-start.8
  17.6 0.7 copy-start.9
  20.1 71.5 %copy-start.6 = (f32[16]{0:T(128)S(1)}, f32[16]{0:T(128)}, u32[]{:S(2)}) copy-start(f32[16]{0:T(128)} %depth_ref.3) | copy-start | bytes 196
  21.3 52.7 %all-to-all-start = ((f32[64,1,1664]{2,1,0:T(1,128)}), f32[64,1,1664]{2,1,0:T(1,128)S(1)}, u32[]{:S(2)}, u32[]{:S(2)}) async-start(f32[64,1,1664]{2,1,0:T(1,128)} %copy.13), calls=%async_computation | async-start | bytes 851968 | tf_op jit(solution)/shard_map/all_to_all | solution.py:574
  49.8 29.1 %collective-permute-start.9 = (f32[40,128]{1,0:T(8,128)S(1)}, f32[40,128]{1,0:T(8,128)S(1)}, u32[]{:S(2)}, u32[]{:S(2)}) collective-permute-start(f32[40,128]{1,0:T(8,128)S(1)} %get-tuple-element.14), channel_id=1, source_target_pairs={{0,2},{2,4},{4,6},{1,3},{3,5},{5,7},{8,10},{10,12},{12,14},{9,11},... | collective-permute-start | bytes 61448 | tf_op jit(solution)/shard_map/ppermute | solution.py:536
  51.9 27.0 %collective-permute-start.8 = (f32[40,128]{1,0:T(8,128)S(1)}, f32[40,128]{1,0:T(8,128)S(1)}, u32[]{:S(2)}, u32[]{:S(2)}) collective-permute-start(f32[40,128]{1,0:T(8,128)S(1)} %get-tuple-element.14), channel_id=1, source_target_pairs={{2,0},{4,2},{6,4},{3,1},{5,3},{7,5},{10,8},{12,10},{14,12},{11,9},... | collective-permute-start | bytes 61448 | tf_op jit(solution)/shard_map/ppermute | solution.py:541
  74.7 5.1 %collective-permute-start.3 = (f32[3,32,128]{2,1,0:T(8,128)S(1)}, f32[3,32,128]{2,1,0:T(8,128)S(1)}, u32[]{:S(2)}, u32[]{:S(2)}) collective-permute-start(f32[3,32,128]{2,1,0:T(8,128)S(1)} %place.1), channel_id=1, source_target_pairs={{0,1},{1,0},{2,3},{3,2},{4,5},{5,4},{6,7},{7,6},{8,9},{9,8},{10,11... | collective-permute-start | bytes 147464 | tf_op jit(solution)/shard_map/ppermute | solution.py:545
  79.8 4.0 %collective-permute-start.4 = (f32[3,8,128]{2,1,0:T(8,128)S(1)}, f32[3,8,128]{2,1,0:T(8,128)S(1)}, u32[]{:S(2)}, u32[]{:S(2)}) collective-permute-start(f32[3,8,128]{2,1,0:T(8,128)S(1)} %get-tuple-element.22), channel_id=1, source_target_pairs={{0,8},{8,16},{16,24},{24,32},{32,40},{40,48},{48,56},{56,64},{64,7... | collective-permute-start | bytes 36872 | tf_op jit(solution)/shard_map/ppermute | solution.py:536
  81.7 4.5 %collective-permute-start.5 = (f32[3,8,128]{2,1,0:T(8,128)S(1)}, f32[3,8,128]{2,1,0:T(8,128)S(1)}, u32[]{:S(2)}, u32[]{:S(2)}) collective-permute-start(f32[3,8,128]{2,1,0:T(8,128)S(1)} %get-tuple-element.23), channel_id=1, source_target_pairs={{8,0},{16,8},{24,16},{32,24},{40,32},{48,40},{56,48},{64,56},{72,6... | collective-permute-start | bytes 36872 | tf_op jit(solution)/shard_map/ppermute | solution.py:541
  83.1 11.8 %collective-permute-start.10 = (f32[5,40,128]{2,1,0:T(8,128)S(1)}, f32[5,40,128]{2,1,0:T(8,128)S(1)}, u32[]{:S(2)}, u32[]{:S(2)}) collective-permute-start(f32[5,40,128]{2,1,0:T(8,128)S(1)} %pad_maximum_fusion), channel_id=1, source_target_pairs={{0,1},{1,0},{2,3},{3,2},{4,5},{5,4},{6,7},{7,6},{8,9},{9,8},{10,11... | collective-permute-start | bytes 307208 | tf_op jit(solution)/shard_map/ppermute | solution.py:545
  86.2 8.7 %collective-permute-start.7 = (f32[3,48,128]{2,1,0:T(8,128)S(1)}, f32[3,48,128]{2,1,0:T(8,128)S(1)}, u32[]{:S(2)}, u32[]{:S(2)}) collective-permute-start(f32[3,48,128]{2,1,0:T(8,128)S(1)} %pad_maximum_fusion.1.own_ref), channel_id=1, source_target_pairs={{2,0},{4,2},{6,4},{3,1},{5,3},{7,5},{10,8},{12,10},{14,12},{11,9},... | collective-permute-start | bytes 221192 | tf_op jit(solution)/shard_map/ppermute | solution.py:541
  87.5 7.4 %collective-permute-start.6 = (f32[3,48,128]{2,1,0:T(8,128)S(1)}, f32[3,48,128]{2,1,0:T(8,128)S(1)}, u32[]{:S(2)}, u32[]{:S(2)}) collective-permute-start(f32[3,48,128]{2,1,0:T(8,128)S(1)} %pad_maximum_fusion.1.own_ref), channel_id=1, source_target_pairs={{0,2},{2,4},{4,6},{1,3},{3,5},{5,7},{8,10},{10,12},{12,14},{9,11},... | collective-permute-start | bytes 221192 | tf_op jit(solution)/shard_map/ppermute | solution.py:536
  91.6 3.3 %collective-permute-start = (f32[16]{0:T(128)S(1)}, f32[16]{0:T(128)S(1)}, u32[]{:S(2)}, u32[]{:S(2)}) collective-permute-start(f32[16]{0:T(128)S(1)} %copy-done.6), channel_id=1, source_target_pairs={{0,1},{1,0},{2,3},{3,2},{4,5},{5,4},{6,7},{7,6},{8,9},{9,8},{10,11... | collective-permute-start | bytes 200 | tf_op jit(solution)/shard_map/ppermute | solution.py:545

commit v2 on v1

--- a/solution.py
+++ b/solution.py
@@ -7,6 +7,7 @@
 from jax.experimental import pallas as pl
 from jax.experimental.pallas import tpu as pltpu
 from jax.sharding import PartitionSpec as P
+
 
 EPOCHS = 4
 PATCH_X = 8
@@ -22,6 +23,7 @@
 F32 = jnp.float32
 VMEM = pl.BlockSpec(memory_space=pltpu.VMEM)
 SMEM = pl.BlockSpec(memory_space=pltpu.SMEM)
+ANY = pl.BlockSpec(memory_space=pl.ANY)
 
 
 def column(ref, first, count, lanes):
@@ -32,8 +34,50 @@
     return out
 
 
-def project_kernel(count_ref, look_ref, observed_ref, predicted_ref, mask_ref, coeffs_ref, tally_ref):
+def front_kernel(
+    count_ref, look_ref, owner_ref, patch_ref, choice_ref, observed_hbm, predicted_hbm, mask_hbm, weights_hbm,
+    out_ref, tally_ref,
+    observed_ref, predicted_ref, mask_ref, weights_ref, coeffs_ref, sums_ref, used_ref, ids_ref, rank_ref, sems,
+):
     blocks, _, pixels = observed_ref.shape
+    tables, _, lanes = weights_ref.shape
+    owners = out_ref.shape[0]
+
+    first = [
+        pltpu.make_async_copy(src, dst, sems.at[k])
+        for k, (src, dst) in enumerate(
+            ((observed_hbm, observed_ref), (predicted_hbm, predicted_ref), (mask_hbm, mask_ref))
+        )
+    ]
+    chunk = tables // PIECES
+    second = []
+    for piece in range(PIECES):
+        part = pl.ds(piece * chunk, chunk)
+        second.append(pltpu.make_async_copy(weights_hbm.at[part], weights_ref.at[part], sems.at[len(first) + piece]))
+    for copy in first + second:
+        copy.start()
+
+    for o in range(owners):
+        used_ref[o] = 0
+        for r in range(CAP):
+            ids_ref[o * CAP + r] = 0
+    for b in range(blocks):
+        o = owner_ref[b]
+        r = used_ref[o]
+        used_ref[o] = r + 1
+        rank_ref[b] = r
+        ids_ref[o * CAP + r] = patch_ref[b]
+    out_ref[...] = jnp.zeros_like(out_ref)
+    spot = lax.broadcasted_iota(jnp.int32, (1, lanes), 1)
+    for o in range(owners):
+        ids = jnp.zeros((1, lanes), jnp.int32)
+        for r in range(CAP):
+            ids = jnp.where(spot == r, ids_ref[o * CAP + r], ids)
+        out_ref[o, :, 3 * CAP * lanes :] = ids.astype(F32)
+    choice = jnp.concatenate([column(choice_ref, g, 8, lanes) for g in range(0, blocks, 8)] * 3, axis=0)
+
+    for copy in first:
+        copy.wait()
     group = 16
     place = lax.broadcasted_iota(jnp.int32, (group, pixels), 1)
     squares = jnp.zeros((group, pixels), F32)
@@ -57,102 +101,69 @@
     tally = jnp.where(spot == 6, jnp.sum(squares), 0.0)
     tally_ref[...] = jnp.where(spot == 7, jnp.sum(weight), tally)
 
-
-def project(count, look, observed, predicted, mask):
-    blocks, _, pixels = observed.shape
-    return pl.pallas_call(
-        project_kernel,
-        out_shape=(
-            jax.ShapeDtypeStruct((3 * blocks, pixels), jnp.bfloat16),
-            jax.ShapeDtypeStruct((1, ROW), F32),
-        ),
-        in_specs=[SMEM, SMEM, VMEM, VMEM, VMEM],
-        out_specs=(VMEM, VMEM),
-        compiler_params=pltpu.CompilerParams(vmem_limit_bytes=8 << 20),
-        cost_estimate=pl.CostEstimate(flops=8_000_000, bytes_accessed=1 << 20, transcendentals=0),
-        name="project",
-    )(count, look, observed, predicted, mask)
-
-
-def block_sums_kernel(
-    owner_ref, patch_ref, choice_ref, coeffs_ref, weights_ref, below_ref, own_ref, above_ref,
-    out_ref, tall_ref, packed_ref, sums_ref, slots_ref, used_ref, ids_ref, rank_ref,
-):
-    blocks = owner_ref.shape[0]
-    tables = weights_ref.shape[0]
-    owners, lanes = slots_ref.shape[1:]
-
-    layers, local_x = own_ref.shape[:2]
-    lane = lax.broadcasted_iota(jnp.int32, (local_x + 2 * REACH, lanes), 1)
-    packed = jnp.zeros((local_x + 2 * REACH, lanes), F32)
-    for z in range(layers):
-        tall_ref[z, 0:REACH, :] = below_ref[z]
-        tall_ref[z, REACH : REACH + local_x, :] = own_ref[z]
-        tall_ref[z, REACH + local_x :, :] = above_ref[z]
-        moved = pltpu.roll(tall_ref[z], (2 * REACH * z + REACH) % lanes, 1)
-        packed = jnp.where(lane // (2 * REACH) == z, moved, packed)
-    packed_ref[...] = packed
-
-    for o in range(owners):
-        used_ref[o] = 0
-        for r in range(CAP):
-            ids_ref[o * CAP + r] = 0
-    for b in range(blocks):
-        o = owner_ref[b]
-        r = used_ref[o]
-        used_ref[o] = r + 1
-        rank_ref[b] = r
-        ids_ref[o * CAP + r] = patch_ref[b]
-
-    choice = jnp.concatenate([column(choice_ref, g, 8, lanes) for g in range(0, blocks, 8)] * 3, axis=0)
     coeffs = coeffs_ref[...]
     total = jnp.zeros(sums_ref.shape, F32)
-    for t in range(tables):
-        product = jnp.dot(coeffs, weights_ref[t], preferred_element_type=F32)
-        total = jnp.where(choice == t, product, total)
+    for piece in range(PIECES):
+        second[piece].wait()
+        for t in range(piece * chunk, (piece + 1) * chunk):
+            product = jnp.dot(coeffs, weights_ref[t], preferred_element_type=F32)
+            total = jnp.where(choice == t, product, total)
     sums_ref[...] = total
-
-    slots_ref[...] = jnp.zeros_like(slots_ref)
     for b in range(blocks):
         o, r = owner_ref[b], rank_ref[b]
         for c in range(3):
-            slots_ref[r * 3 + c, pl.ds(o, 1), :] = sums_ref[c * blocks + b : c * blocks + b + 1, :]
-    for k in range(3 * CAP):
-        out_ref[:, k * lanes : (k + 1) * lanes] = slots_ref[k]
-    spot = lax.broadcasted_iota(jnp.int32, (8, lanes), 1)
-    spot = jnp.where(spot < CAP, lax.broadcasted_iota(jnp.int32, (8, lanes), 0) * CAP + spot, -1)
-    for g in range(0, owners, 8):
-        ids = jnp.zeros((8, lanes), jnp.int32)
-        for k in range(8 * CAP):
-            ids = jnp.where(spot == k, ids_ref[g * CAP + k], ids)
-        out_ref[g : g + 8, 3 * CAP * lanes :] = ids.astype(F32)
-
-
-def block_sums(owner, patch, choice, coeffs, weights, below, own, above, owners):
-    tables, pixels, cells = weights.shape
+            at = pl.multiple_of((r * 3 + c) * lanes, lanes)
+            out_ref[o, :, pl.ds(at, lanes)] = sums_ref[c * blocks + b : c * blocks + b + 1, :]
+
+
+def front(count, look, owner, patch, choice, observed, predicted, mask, weights, owners):
+    _, pixels, cells = weights.shape
     blocks = owner.shape[0]
-    layers, local_x, lanes = own.shape
-    rows = local_x + 2 * REACH
     return pl.pallas_call(
-        block_sums_kernel,
+        front_kernel,
         out_shape=(
-            jax.ShapeDtypeStruct((owners, (3 * CAP + 1) * cells), F32),
-            jax.ShapeDtypeStruct((layers, rows, lanes), F32),
-            jax.ShapeDtypeStruct((rows, lanes), F32),
+            jax.ShapeDtypeStruct((owners, 1, (3 * CAP + 1) * cells), F32),
+            jax.ShapeDtypeStruct((1, ROW), F32),
         ),
-        in_specs=[SMEM] * 3 + [VMEM] * 5,
-        out_specs=(VMEM,) * 3,
+        in_specs=[SMEM] * 5 + [ANY] * 4,
+        out_specs=(VMEM,) * 2,
         scratch_shapes=[
+            pltpu.VMEM(observed.shape, F32),
+            pltpu.VMEM(observed.shape, F32),
+            pltpu.VMEM(mask.shape, jnp.int32),
+            pltpu.VMEM(weights.shape, weights.dtype),
+            pltpu.VMEM((3 * blocks, pixels), jnp.bfloat16),
             pltpu.VMEM((3 * blocks, cells), F32),
-            pltpu.VMEM((3 * CAP, owners, cells), F32),
             pltpu.SMEM((owners,), jnp.int32),
             pltpu.SMEM((owners * CAP,), jnp.int32),
             pltpu.SMEM((blocks,), jnp.int32),
+            pltpu.SemaphoreType.DMA((3 + PIECES,)),
         ],
-        compiler_params=pltpu.CompilerParams(vmem_limit_bytes=8 << 20),
         cost_estimate=pl.CostEstimate(flops=400_000_000, bytes_accessed=4 << 20, transcendentals=0),
-        name="block_sums",
-    )(owner, patch, choice, coeffs, weights, below, own, above)
+        name="front",
+    )(count, look, owner, patch, choice, observed, predicted, mask, weights)
+
+
+def pack_kernel(own_ref, far_ref, out_ref):
+    lane = lax.broadcasted_iota(jnp.int32, out_ref.shape[1:], 1)
+    for k, ref in enumerate((own_ref, far_ref)):
+        packed = jnp.zeros(out_ref.shape[1:], F32)
+        for z in range(ref.shape[0]):
+            moved = pltpu.roll(ref[z], (2 * REACH * z + REACH) % LANES, 1)
+            packed = jnp.where(lane // (2 * REACH) == z, moved, packed)
+        out_ref[k] = packed
+
+
+def pack(own, far):
+    return pl.pallas_call(
+        pack_kernel,
+        out_shape=jax.ShapeDtypeStruct((2,) + own.shape[1:], F32),
+        in_specs=[VMEM] * 2,
+        out_specs=VMEM,
+        compiler_params=pltpu.CompilerParams(vmem_limit_bytes=4 << 20),
+        cost_estimate=pl.CostEstimate(flops=1_000_000, bytes_accessed=1 << 18, transcendentals=0),
+        name="pack",
+    )(own, far)
 
 
 def swap_granules(tile, size):
@@ -218,11 +229,10 @@
 
 
 def powers_kernel(
-    sizes, at_ref, depth_ref, beyond_ref, own_ref, left_ref, right_ref, stiff_ref, side_ref, partner_ref,
-    tally_ref, one_ref, two_ref, three_ref, row_ref, flat, keep, diag, w1, w2, div,
+    sizes, layers, at_ref, depth_ref, beyond_ref, own_ref, left_ref, right_ref, stiff_ref,
+    tally_ref, one_ref, two_ref, three_ref, row_ref, flat, keep, diag, w1, w2, div1, div2,
 ):
-    layers, rows = stiff_ref.shape[0], stiff_ref.shape[1]
-    local_x = one_ref.shape[2]
+    rows, local_x = stiff_ref.shape[1], one_ref.shape[2]
     size_x, size_y, size_z = sizes
     at = at_ref[0]
     at_z = lax.rem(at, size_z)
@@ -235,10 +245,11 @@
     def layer_of(z):
         return jnp.where(upper, layers - 1 - z, z)
 
+    depths = [depth_ref[layer_of(z)] for z in range(layers)]
+    depths += [beyond_ref[layer_of(z)] for z in range(REACH + 2)]
+
     def depth(z):
-        inner = depth_ref[layer_of(jnp.clip(z, 0, layers - 1))]
-        outer = beyond_ref[layer_of(jnp.clip(z - layers, 0, layers - 1))]
-        return jnp.where(z < 0, 0.0, jnp.where(z < layers, inner, outer))
+        return depths[z] if z >= 0 else jnp.zeros((), F32)
 
     lane = lax.broadcasted_iota(jnp.int32, (tall, LANES), 1)
     line = lax.broadcasted_iota(jnp.int32, (tall, LANES), 0)
@@ -281,26 +292,23 @@
     ahead_x, behind_x = pl.ds(EDGE + 1, rows), pl.ds(EDGE - 1, rows)
     flat_rows = pl.ds(first, rows)
 
-    def apply_first(z, carry):
+    def apply_first(z):
         d = depth(z)
         before, after = depth(z - 1), depth(z + 1)
         slope = 0.5 * (after - before)
         slope_after = 0.5 * (depth(z + 2) - d)
-        slope_before = jnp.where(z > 0, 0.5 * (d - depth(z - 2)), 0.0)
+        slope_before = 0.5 * (d - depth(z - 2)) if z > 0 else 0.0
         bend = 0.5 * (slope_after - slope_before)
         sides = before + after
-        z_in = layer_of(jnp.minimum(z, layers - 1))
-        z_out = jnp.clip(jnp.where(upper, REACH - 1 - (z - layers), z - layers), 0, REACH - 1)
-        here = z < layers
-        packed = jnp.where(here, side_ref[...], partner_ref[REACH])
-        which = jnp.where(here, z_in, jnp.where(upper, layers - REACH, 0) + z_out)
-        turn = LANES - REACH - 2 * REACH * which
+        if z < layers:
+            place = layer_of(z)
+            stiff, packed, group = stiff_ref[place], stiff_ref[layers + REACH], place
+        else:
+            group = jnp.where(upper, REACH - 1 - (z - layers), z - layers)
+            stiff, packed = stiff_ref[layers + group], stiff_ref[layers + REACH + 1]
+        turned = pltpu.roll(packed, LANES - REACH - 2 * REACH * group, 1)
         for t in range(2):
-            if t == 0:
-                stiff = jnp.where(here, stiff_ref[z_in], partner_ref[z_out])
-            else:
-                stiff = pltpu.roll(packed, turn, 1)
-            centre = stiff + (6.0 - SHIFT)
+            centre = (stiff if t == 0 else turned) + (6.0 - SHIFT)
             diag[z, t] = centre
             for c in range(3):
                 v = flat[t, c, flat_rows, :]
@@ -308,53 +316,37 @@
                 cross = flat[t, 6 + c, flat_rows, :]
                 own_part = sides if c < 2 else sides + 0.5 * bend
                 w1[c, z + 1, t, body, :] = d * (centre * v + rest) - own_part * v + slope * cross
-        return carry
 
     for c in range(3):
         for t in range(2):
             w1[c, 0, t] = jnp.zeros_like(w1[c, 0, t])
             w2[c, 0, t] = jnp.zeros_like(w2[c, 0, t])
     for t in range(2):
-        div[0, t] = jnp.zeros_like(div[0, t])
-    lax.fori_loop(0, layers + REACH, apply_first, 0)
-
-    def spread(w, z):
+        div1[0, t] = jnp.zeros_like(div1[0, t])
+        div2[0, t] = jnp.zeros_like(div2[0, t])
+
+    def spread(w, div, z):
         ahead, behind = lane_steps(w[1, z, 0, body, :], w[1, z, 1, body, :])
         for t in range(2):
             total = w[0, z, t, ahead_x, :] - w[0, z, t, behind_x, :] + ahead[t] - behind[t]
             total += w[2, z + 1, t, body, :] - w[2, z - 1, t, body, :]
             div[z, t, body, :] = keep[t, flat_rows, :] * total
 
-    def spread_first(z, carry):
-        spread(w1, z + 1)
-        return carry
-
-    lax.fori_loop(0, layers + REACH - 1, spread_first, 0)
-
-    def apply_second(z, carry):
-        ahead, behind = lane_steps(div[z + 1, 0, body, :], div[z + 1, 1, body, :])
+    def apply_second(z):
+        ahead, behind = lane_steps(div1[z + 1, 0, body, :], div1[z + 1, 1, body, :])
         for c in range(3):
             yp, ym = lane_steps(w1[c, z + 1, 0, body, :], w1[c, z + 1, 1, body, :])
             for t in range(2):
                 around = w1[c, z + 1, t, ahead_x, :] + w1[c, z + 1, t, behind_x, :] + yp[t] + ym[t]
                 around += w1[c, z, t, body, :] + w1[c, z + 2, t, body, :]
                 if c == 0:
-                    slope = div[z + 1, t, ahead_x, :] - div[z + 1, t, behind_x, :]
+                    slope = div1[z + 1, t, ahead_x, :] - div1[z + 1, t, behind_x, :]
                 elif c == 1:
                     slope = ahead[t] - behind[t]
                 else:
-                    slope = div[z + 2, t, body, :] - div[z, t, body, :]
+                    slope = div1[z + 2, t, body, :] - div1[z, t, body, :]
                 value = diag[z, t] * w1[c, z + 1, t, body, :] - around - 0.125 * slope
                 w2[c, z + 1, t, body, :] = keep[t, flat_rows, :] * value
-        return carry
-
-    lax.fori_loop(0, layers + REACH - 2, apply_second, 0)
-
-    def spread_second(z, carry):
-        spread(w2, z + 1)
-        return carry
-
-    lax.fori_loop(0, layers + REACH // 4, spread_second, 0)
 
     lo = EDGE + REACH
     mid = pl.ds(lo, local_x)
@@ -374,21 +366,20 @@
         return out
 
     def apply_third(z, sums):
-        sums = list(sums)
         d = depth(z)
         z_out = layer_of(z)
-        ahead, behind = sides_of(div[z + 1, 0, mid, :], div[z + 1, 1, mid, :])
+        ahead, behind = sides_of(div2[z + 1, 0, mid, :], div2[z + 1, 1, mid, :])
         for c in range(3):
             centre = w2[c, z + 1, 0, mid, :]
             yp, ym = sides_of(centre, w2[c, z + 1, 1, mid, :])
             around = w2[c, z + 1, 0, mid_ahead, :] + w2[c, z + 1, 0, mid_behind, :] + yp + ym
             around += w2[c, z, 0, mid, :] + w2[c, z + 2, 0, mid, :]
             if c == 0:
-                slope = div[z + 1, 0, mid_ahead, :] - div[z + 1, 0, mid_behind, :]
+                slope = div2[z + 1, 0, mid_ahead, :] - div2[z + 1, 0, mid_behind, :]
             elif c == 1:
                 slope = ahead - behind
             else:
-                slope = div[z + 2, 0, mid, :] - div[z, 0, mid, :]
+                slope = div2[z + 2, 0, mid, :] - div2[z, 0, mid, :]
             third = diag[z, 0, pl.ds(REACH, local_x), :] * centre - around - 0.125 * slope
             begin = d * flat[0, c, pl.ds(EDGE, local_x), :]
             once = w1[c, z + 1, 0, mid, :]
@@ -398,10 +389,24 @@
             pairs = ((begin, begin), (begin, once), (once, once), (once, centre), (centre, centre), (centre, third))
             for k, (a, b) in enumerate(pairs):
                 sums[k] = sums[k] + fold(a * b)
-        return tuple(sums)
 
     zero = jnp.zeros((8, LANES), F32)
-    sums = lax.fori_loop(0, layers, apply_third, (zero,) * 6)
+    sums = [zero] * 6
+    for step in range(layers + REACH + 4):
+        for stage, (count, lag) in enumerate(((REACH, 0), (REACH - 1, 1), (REACH - 2, 2), (1, 3), (0, 4))):
+            z = step - lag
+            if not 0 <= z < layers + count:
+                continue
+            if stage == 0:
+                apply_first(z)
+            elif stage == 1:
+                spread(w1, div1, z + 1)
+            elif stage == 2:
+                apply_second(z)
+            elif stage == 3:
+                spread(w2, div2, z + 1)
+            else:
+                apply_third(z, sums)
     spot = lax.broadcasted_iota(jnp.int32, (1, ROW), 1)
     row = tally_ref[...]
     for k in range(6):
@@ -409,16 +414,17 @@
     row_ref[...] = jnp.broadcast_to(row, row_ref.shape)
 
 
-def powers(sizes, at, depth, beyond, own, left, right, stiff, side, partner, tally):
-    layers, rows, lanes = stiff.shape
+def powers(sizes, at, depth, beyond, own, left, right, stiff, tally):
+    layers = depth.shape[0]
+    _, rows, lanes = stiff.shape
     tall = own.shape[1]
     local_x = tall - 2 * EDGE
     field = jax.ShapeDtypeStruct((3, layers, local_x, lanes), F32)
     deep = rows + 2 * EDGE
     return pl.pallas_call(
-        functools.partial(powers_kernel, sizes),
+        functools.partial(powers_kernel, sizes, layers),
         out_shape=(field, field, field, jax.ShapeDtypeStruct((math.prod(sizes), ROW), F32)),
-        in_specs=[SMEM] * 3 + [VMEM] * 7,
+        in_specs=[SMEM] * 3 + [VMEM] * 5,
         out_specs=(VMEM,) * 4,
         scratch_shapes=[
             pltpu.VMEM((2, 9, tall, lanes), F32),
@@ -427,11 +433,12 @@
             pltpu.VMEM((3, layers + REACH + 1, 2, deep, lanes), F32),
             pltpu.VMEM((3, layers + REACH - 1, 2, deep, lanes), F32),
             pltpu.VMEM((layers + REACH, 2, deep, lanes), F32),
+            pltpu.VMEM((layers + REACH // 2, 2, deep, lanes), F32),
         ],
         compiler_params=pltpu.CompilerParams(vmem_limit_bytes=20 << 20),
         cost_estimate=pl.CostEstimate(flops=100_000_000, bytes_accessed=4 << 20, transcendentals=0),
         name="powers",
-    )(at, depth, beyond, own, left, right, stiff, side, partner, tally)
+    )(at, depth, beyond, own, left, right, stiff, tally)
 
 
 def step_factors(nu):
@@ -519,7 +526,7 @@
         finish_kernel,
         out_shape=(field, field),
         in_specs=[SMEM] + [VMEM] * 5,
-        out_specs=(pl.BlockSpec(memory_space=pl.ANY),) * 2,
+        out_specs=(ANY,) * 2,
         scratch_shapes=[
             pltpu.VMEM(one.shape, F32),
             pltpu.VMEM(one.shape, F32),
@@ -564,22 +571,24 @@
     at = lax.axis_index(("gx", "gy", "gz")).astype(jnp.int32).reshape(1)
     upper = lax.axis_index("gz") == 1
 
-    below = from_below(stiffness[:, local_x - REACH :, :], "gx")
-    above = from_above(stiffness[:, :REACH, :], "gx")
-    coeffs, tally = project(block_count, look_vector, observed, predicted, coherence_mask)
-    sums, tall, packed = block_sums(
-        block_owner[:, 0], block_patch, block_matrix_choice, coeffs, interp_weights, below, stiffness, above, owners
+    sums, tally = front(
+        block_count, look_vector, block_owner[:, 0], block_patch, block_matrix_choice,
+        observed, predicted, coherence_mask, interp_weights, owners,
     )
-    packed_left, packed_right = from_below(packed, "gy"), from_above(packed, "gy")
+    sums, stiffness, depth_kernel = lax.optimization_barrier((sums, stiffness, depth_kernel))
     got = lax.all_to_all(sums, ("gx", "gy"), split_axis=0, concat_axis=0, tiled=True)
-
-    lane = lax.broadcasted_iota(jnp.int32, packed.shape, 1)
-    side = jnp.where(lane % (2 * REACH) >= REACH, packed_right, packed_left)
-    near = jnp.where(upper, tall[:REACH], tall[layers - REACH :])
-    partner = from_partner(jnp.concatenate([near, side[None]]), "gz")
     depth_beyond = from_partner(depth_kernel, "gz")
-
-    part = place(got, local_x, local_y)
+    far = from_partner(jnp.where(upper, stiffness[:REACH], stiffness[layers - REACH :]), "gz")
+    packed = pack(stiffness, far)
+    lane = lax.broadcasted_iota(jnp.int32, packed.shape, 2)
+    side = jnp.where(lane % (2 * REACH) >= REACH, from_above(packed, "gy"), from_below(packed, "gy"))
+    stiff = jnp.concatenate([stiffness, far, side])
+    low, high = stiff[:, :REACH, :], stiff[:, local_x - REACH :, :]
+    below = from_below(high, "gx")
+    above = from_above(low, "gx")
+    stiff = jnp.concatenate([below, stiff, above], axis=1)
+
+    part = place(got[:, 0], local_x, local_y)
     surface = part + from_partner(part, "gz")
     own = jnp.concatenate(
         [
@@ -591,7 +600,7 @@
     )
     left, right = from_below(own, "gy"), from_above(own, "gy")
     one, two, three, rows = powers(
-        sizes, at, depth_kernel, depth_beyond, own, left, right, tall, side, partner, tally
+        sizes, at, depth_kernel, depth_beyond, own, left, right, stiff, tally
     )
     rows = lax.all_to_all(rows, ("gx", "gy", "gz"), split_axis=0, concat_axis=0, tiled=True)
     return finish(depth_kernel, rows, surface, one, two, three)
@@ -612,6 +621,4 @@
         P(("grp", "gz"), "gx", "gy"),
     )
     out_specs = (P(None, ("grp", "gz"), "gx", "gy"), P(None, ("grp", "gz"), "gx", "gy"))
-    return jax.shard_map(
-        per_device, mesh=mesh, in_specs=in_specs, out_specs=out_specs, check_vma=False
-    )
+    return jax.shard_map(per_device, mesh=mesh, in_specs=in_specs, out_specs=out_specs, check_vma=False)

time: 137 us -> 119 us (0.87)
  local copies, waits for them, and re-layouts: 10.7 us -> 0.05 us
  Pallas kernels: 17.5 us -> 12.6 us
  starting transfers between devices: 55.1 us -> 51.8 us
  blocking collectives: 27.4 us -> 30.6 us
  waiting for transfers between devices: 24.8 us -> 21.9 us
    unnamed x23 -> x7, local copies, waits for them, and re-layouts: 8.6 us -> 0.04 us
    pallas_call x3, Pallas kernels: 14.6 us -> 9.66 us  [the longest x1 4.88 us: powers(): pl.pallas_call(functools.partial(powers_kernel, sizes, layers), out_shape...]
    all_to_all x1, blocking collectives: 27.4 us -> 30.6 us  [per_device(): lax.all_to_all(rows, ('gx', 'gy', 'gz'), split_axis=0, concat_axis=0, til...]
    ppermute x3, starting transfers between devices: 7.4 us -> 4.6 us  [from_partner(): return lax.ppermute(value, axis, [(0, 1), (1, 0)])]
    ppermute x4, waiting for transfers between devices: 2.38 us -> 0.01 us  [from_above(): return lax.ppermute(value, axis, [(i + 1, i) for i in range(count - 1)])]
    all_to_all x1, waiting for transfers between devices: 20.7 us -> 18.6 us  [per_device(): lax.all_to_all(sums, ('gx', 'gy'), split_axis=0, concat_axis=0, tiled=True)]
    ppermute x4, starting transfers between devices: 13.9 us -> 12.4 us  [from_below(): return lax.ppermute(value, axis, [(i, i + 1) for i in range(count - 1)])]
where the time goes in v2:
time: 119 us; the launch traced here: 118 us
  starting transfers between devices  51.8 us (44%)
  blocking collectives  30.6 us (26%)
  waiting for transfers between devices  21.9 us (18%)
  Pallas kernels  12.6 us (11%)
    all_to_all x1, blocking collectives, per_device(): lax.all_to_all(rows, ('gx', 'gy', 'gz'), split_axis=0, concat_axis=0, til...  30.6 us
    all_to_all x1, starting transfers between devices, per_device(): lax.all_to_all(sums, ('gx', 'gy'), split_axis=0, concat_axis=0, tiled=True)  29.6 us
    all_to_all x1, waiting for transfers between devices, per_device(): lax.all_to_all(sums, ('gx', 'gy'), split_axis=0, concat_axis=0, tiled=True)  18.6 us
    ppermute x4, starting transfers between devices, from_below(): return lax.ppermute(value, axis, [(i, i + 1) for i in range(count - 1)])  12.4 us
    ppermute x4, starting transfers between devices, from_above(): return lax.ppermute(value, axis, [(i + 1, i) for i in range(count - 1)])  5.23 us
    pallas_call x1, Pallas kernels, powers(): pl.pallas_call(functools.partial(powers_kernel, sizes, layers), out_shape...  4.88 us
    pallas_call x1, Pallas kernels, front(): pl.pallas_call(front_kernel, out_shape=(jax.ShapeDtypeStruct((owners, 1,...  4.64 us
    ppermute x3, starting transfers between devices, from_partner(): return lax.ppermute(value, axis, [(0, 1), (1, 0)])  4.6 us
  transfers between devices with their start and end apart: 12, of which 4 were waited for; matrix products, arithmetic and copies ran while one was open for 0% of the time, Pallas kernels for 1%

profile of v2, /device:TPU:33, one launch (start us, length us, event | category | flops | bytes accessed | tf_op | source)
XLA Modules:
  0.0 118.1 jit_solution(17041838526840012489)
XLA Ops:
  0.6 0.0 copy-start
  0.6 0.0 copy-start.1
  0.7 4.6 %front.1 = (f32[64,1,1664]{2,1,0:T(1,128)}, f32[1,16]{1,0:T(1,128)}) custom-call(s32[64]{0:T(128)} %count_ref.1, f32[4,3]{1,0:T(4,128)} %look_ref.1, s32[64]{0:T(128)} %bitcast.12, s32[64]{0:T(128)} %patch_ref.1, s32[64]{0:T(128)} %choice_ref.1, f32[64,4,256]{2,1,0:T(4,128)} %observed_hbm.1, f32[64,4,256]{2,1,0:T(4,128)} %predicted_hbm.1, ...), custom_call_target="tpu_custom_call" | custom-call | flops 400000000 | bytes 4194304 | tf_op jit(solution)/shard_map/front/pallas_call | solution.py:122
  5.3 0.0 copy-start.2
  5.3 29.6 %all-to-all-start = ((f32[64,1,1664]{2,1,0:T(1,128)}), f32[64,1,1664]{2,1,0:T(1,128)S(1)}, u32[]{:S(2)}, u32[]{:S(2)}) async-start(f32[64,1,1664]{2,1,0:T(1,128)} %get-tuple-element.13), calls=%async_computation | async-start | bytes 851968 | tf_op jit(solution)/shard_map/all_to_all | solution.py:579
  34.9 0.0 copy-done.1
  34.9 1.0 collective-permute-start
  35.9 0.0 copy-done
  35.9 0.2 collective-permute-start.6
  36.1 1.2 %collective-permute-done.6.far_ref = f32[4,32,128]{2,1,0:T(8,128)S(1)} collective-permute-done((f32[4,32,128]{2,1,0:T(8,128)S(1)}, f32[4,32,128]{2,1,0:T(8,128)S(1)}, u32[]{:S(2)}, u32[]{:S(2)}) %collective-permute-start.6) | collective-permute-done | bytes 65568 | tf_op jit(solution)/shard_map/ppermute | solution.py:552
  37.3 0.1 pack.1
  37.5 2.4 %collective-permute-start.8 = (f32[2,32,128]{2,1,0:T(8,128)S(1)}, f32[2,32,128]{2,1,0:T(8,128)S(1)}, u32[]{:S(2)}, u32[]{:S(2)}) collective-permute-start(f32[2,32,128]{2,1,0:T(8,128)S(1)} %pack.1), channel_id=1, source_target_pairs={{0,2},{2,4},{4,6},{1,3},{3,5},{5,7},{8,10},{10,12},{12,14},{9,11},... | collective-permute-start | bytes 98312 | tf_op jit(solution)/shard_map/ppermute | solution.py:543
  39.8 1.3 %collective-permute-start.7 = (f32[2,32,128]{2,1,0:T(8,128)S(1)}, f32[2,32,128]{2,1,0:T(8,128)S(1)}, u32[]{:S(2)}, u32[]{:S(2)}) collective-permute-start(f32[2,32,128]{2,1,0:T(8,128)S(1)} %pack.1), channel_id=1, source_target_pairs={{2,0},{4,2},{6,4},{3,1},{5,3},{7,5},{10,8},{12,10},{14,12},{11,9},... | collective-permute-start | bytes 98312 | tf_op jit(solution)/shard_map/ppermute | solution.py:548
  41.2 18.6 %all-to-all-done = f32[64,1,1664]{2,1,0:T(1,128)S(1)} async-done(((f32[64,1,1664]{2,1,0:T(1,128)}), f32[64,1,1664]{2,1,0:T(1,128)S(1)}, u32[]{:S(2)}, u32[]{:S(2)}) %all-to-all-start) | async-done | bytes 426016 | tf_op jit(solution)/shard_map/all_to_all | solution.py:579
  59.8 0.7 place.1
  60.5 3.4 %collective-permute-start.1 = (f32[3,32,128]{2,1,0:T(8,128)S(1)}, f32[3,32,128]{2,1,0:T(8,128)S(1)}, u32[]{:S(2)}, u32[]{:S(2)}) collective-permute-start(f32[3,32,128]{2,1,0:T(8,128)S(1)} %place.1), channel_id=1, source_target_pairs={{0,1},{1,0},{2,3},{3,2},{4,5},{5,4},{6,7},{7,6},{8,9},{9,8},{10,11... | collective-permute-start | bytes 147464 | tf_op jit(solution)/shard_map/ppermute | solution.py:552
  63.9 0.0 collective-permute-done.8
  63.9 0.0 collective-permute-done.7
  63.9 0.9 collective-permute-done.1
  64.8 2.0 %collective-permute-start.2 = (f32[3,8,128]{2,1,0:T(8,128)S(1)}, f32[3,8,128]{2,1,0:T(8,128)S(1)}, u32[]{:S(2)}, u32[]{:S(2)}) collective-permute-start(f32[3,8,128]{2,1,0:T(8,128)S(1)} %get-tuple-element.22), channel_id=1, source_target_pairs={{0,8},{8,16},{16,24},{24,32},{32,40},{40,48},{48,56},{56,64},{64,7... | collective-permute-start | bytes 36872 | tf_op jit(solution)/shard_map/ppermute | solution.py:543
  66.8 1.3 %collective-permute-start.3 = (f32[3,8,128]{2,1,0:T(8,128)S(1)}, f32[3,8,128]{2,1,0:T(8,128)S(1)}, u32[]{:S(2)}, u32[]{:S(2)}) collective-permute-start(f32[3,8,128]{2,1,0:T(8,128)S(1)} %get-tuple-element.23), channel_id=1, source_target_pairs={{8,0},{16,8},{24,16},{32,24},{40,32},{48,40},{56,48},{64,56},{72,6... | collective-permute-start | bytes 36872 | tf_op jit(solution)/shard_map/ppermute | solution.py:548
  68.1 4.0 %collective-permute-start.9 = (f32[22,4,128]{2,1,0:T(4,128)S(1)}, f32[22,4,128]{2,1,0:T(4,128)S(1)}, u32[]{:S(2)}, u32[]{:S(2)}) collective-permute-start(f32[22,4,128]{2,1,0:T(4,128)S(1)} %get-tuple-element.20), channel_id=1, source_target_pairs={{0,8},{8,16},{16,24},{24,32},{32,40},{40,48},{48,56},{56,64},{64,7... | collective-permute-start | bytes 135176 | tf_op jit(solution)/shard_map/ppermute | solution.py:543
  72.2 1.3 %collective-permute-start.10 = (f32[22,4,128]{2,1,0:T(4,128)S(1)}, f32[22,4,128]{2,1,0:T(4,128)S(1)}, u32[]{:S(2)}, u32[]{:S(2)}) collective-permute-start(f32[22,4,128]{2,1,0:T(4,128)S(1)} %get-tuple-element.21), channel_id=1, source_target_pairs={{8,0},{16,8},{24,16},{32,24},{40,32},{48,40},{56,48},{64,56},{72,6... | collective-permute-start | bytes 135176 | tf_op jit(solution)/shard_map/ppermute | solution.py:548
  73.5 0.0 collective-permute-done.2
  73.5 0.0 collective-permute-done.3
  73.5 1.3 %collective-permute-start.5 = (f32[3,48,128]{2,1,0:T(8,128)S(1)}, f32[3,48,128]{2,1,0:T(8,128)S(1)}, u32[]{:S(2)}, u32[]{:S(2)}) collective-permute-start(f32[3,48,128]{2,1,0:T(8,128)S(1)} %pad_maximum_fusion.1.own_ref), channel_id=1, source_target_pairs={{2,0},{4,2},{6,4},{3,1},{5,3},{7,5},{10,8},{12,10},{14,12},{11,9},... | collective-permute-start | bytes 221192 | tf_op jit(solution)/shard_map/ppermute | solution.py:548
  74.8 4.0 %collective-permute-start.4 = (f32[3,48,128]{2,1,0:T(8,128)S(1)}, f32[3,48,128]{2,1,0:T(8,128)S(1)}, u32[]{:S(2)}, u32[]{:S(2)}) collective-permute-start(f32[3,48,128]{2,1,0:T(8,128)S(1)} %pad_maximum_fusion.1.own_ref), channel_id=1, source_target_pairs={{0,2},{2,4},{4,6},{1,3},{3,5},{5,7},{8,10},{10,12},{12,14},{9,11},... | collective-permute-start | bytes 221192 | tf_op jit(solution)/shard_map/ppermute | solution.py:543
  78.9 0.0 collective-permute-done.9
  78.9 0.0 collective-permute-done.10
  78.9 0.1 pad_maximum_fusion.stiff_ref
  79.0 0.0 collective-permute-done.beyond_ref
  79.0 0.0 collective-permute-done.5.right_ref
  79.0 1.3 %collective-permute-done.4.left_ref = f32[3,48,128]{2,1,0:T(8,128)S(1)} collective-permute-done((f32[3,48,128]{2,1,0:T(8,128)S(1)}, f32[3,48,128]{2,1,0:T(8,128)S(1)}, u32[]{:S(2)}, u32[]{:S(2)}) %collective-permute-start.4) | collective-permute-done | bytes 73760 | tf_op jit(solution)/shard_map/ppermute | solution.py:543
  80.3 0.0 copy-done.2
  80.3 4.9 %powers.1 = (f32[3,16,32,128]{3,2,1,0:T(8,128)S(1)}, f32[3,16,32,128]{3,2,1,0:T(8,128)S(1)}, f32[3,16,32,128]{3,2,1,0:T(8,128)S(1)}, f32[128,16]{1,0:T(8,128)S(1)}) custom-call(s32[1]{0:T(128)} %bitcast.1.at_ref, f32[16]{0:T(128)S(1)} %copy-done.1, f32[16]{0:T(128)S(1)} %collective-permute-done.beyond_ref, f32[3,48,128]{2,1,0:T(8,128)S(1)} %pad_maximum_fusion.1.own_ref, ...), custom_call_target="tpu_custom_call" | custom-call | flops 100000000 | bytes 4194304 | tf_op jit(solution)/shard_map/powers/pallas_call | solution.py:424
  85.1 30.6 %all_to_all.16 = f32[128,1,16]{2,1,0:T(1,128)S(1)} all-to-all(f32[128,1,16]{2,1,0:T(1,128)S(1)} %bitcast.11), channel_id=1, replica_groups=mesh['grp'=2,'gx'=16,'gy'=4,'gz'=2] {'gx','gy','gz'}, dimensions={0} | all-to-all | bytes 16384 | tf_op jit(solution)/shard_map/all_to_all | solution.py:605
  115.8 2.2 %finish.1 = (f32[3,16,32,128]{3,2,1,0:T(8,128)}, f32[3,16,32,128]{3,2,1,0:T(8,128)}) custom-call(f32[16]{0:T(128)S(1)} %copy-done.1, f32[128,16]{1,0:T(8,128)S(1)} %bitcast.10, f32[3,32,128]{2,1,0:T(8,128)S(1)} %add.18.surface_ref, f32[3,16,32,128]{3,2,1,0:T(8,128)S(1)} %get-tuple-element.17.one_ref, f32[3,16,32,128]{3,2,1,0:T(8,128)S(1)} %get-tuple-element.18.two_ref, ...), custom_call_target="tpu_custom_call" | custom-call | flops 20000000 | bytes 4194304 | tf_op jit(solution)/shard_map/finish/pallas_call | solution.py:525
  (9 shorter events, 0.1 us)
Async XLA Ops:
  0.6 35.3 %copy-start = (f32[16,32,128]{2,1,0:T(8,128)S(1)}, f32[16,32,128]{2,1,0:T(8,128)}, u32[]{:S(2)}) copy-start(f32[16,32,128]{2,1,0:T(8,128)} %own_ref) | copy-start | bytes 786436
  0.6 34.3 %copy-start.1 = (f32[16]{0:T(128)S(1)}, f32[16]{0:T(128)}, u32[]{:S(2)}) copy-start(f32[16]{0:T(128)} %depth_ref.1) | copy-start | bytes 196
  5.3 75.0 %copy-start.2 = (f32[1,16]{1,0:T(1,128)S(1)}, f32[1,16]{1,0:T(1,128)}, u32[]{:S(2)}) copy-start(f32[1,16]{1,0:T(1,128)} %get-tuple-element.15.tally_ref) | copy-start | bytes 196
  5.3 54.4 %all-to-all-start = ((f32[64,1,1664]{2,1,0:T(1,128)}), f32[64,1,1664]{2,1,0:T(1,128)S(1)}, u32[]{:S(2)}, u32[]{:S(2)}) async-start(f32[64,1,1664]{2,1,0:T(1,128)} %get-tuple-element.13), calls=%async_computation | async-start | bytes 851968 | tf_op jit(solution)/shard_map/all_to_all | solution.py:579
  34.9 44.0 %collective-permute-start = (f32[16]{0:T(128)S(1)}, f32[16]{0:T(128)S(1)}, u32[]{:S(2)}, u32[]{:S(2)}) collective-permute-start(f32[16]{0:T(128)S(1)} %copy-done.1), channel_id=1, source_target_pairs={{0,1},{1,0},{2,3},{3,2},{4,5},{5,4},{6,7},{7,6},{8,9},{9,8},{10,11... | collective-permute-start | bytes 200 | tf_op jit(solution)/shard_map/ppermute | solution.py:552
  35.9 1.4 %collective-permute-start.6 = (f32[4,32,128]{2,1,0:T(8,128)S(1)}, f32[4,32,128]{2,1,0:T(8,128)S(1)}, u32[]{:S(2)}, u32[]{:S(2)}) collective-permute-start(f32[4,32,128]{2,1,0:T(8,128)S(1)} %slice_select_fusion), channel_id=1, source_target_pairs={{0,1},{1,0},{2,3},{3,2},{4,5},{5,4},{6,7},{7,6},{8,9},{9,8},{10,11... | collective-permute-start | bytes 196616 | tf_op jit(solution)/shard_map/ppermute | solution.py:552
  37.5 26.4 %collective-permute-start.8 = (f32[2,32,128]{2,1,0:T(8,128)S(1)}, f32[2,32,128]{2,1,0:T(8,128)S(1)}, u32[]{:S(2)}, u32[]{:S(2)}) collective-permute-start(f32[2,32,128]{2,1,0:T(8,128)S(1)} %pack.1), channel_id=1, source_target_pairs={{0,2},{2,4},{4,6},{1,3},{3,5},{5,7},{8,10},{10,12},{12,14},{9,11},... | collective-permute-start | bytes 98312 | tf_op jit(solution)/shard_map/ppermute | solution.py:543
  39.8 24.1 %collective-permute-start.7 = (f32[2,32,128]{2,1,0:T(8,128)S(1)}, f32[2,32,128]{2,1,0:T(8,128)S(1)}, u32[]{:S(2)}, u32[]{:S(2)}) collective-permute-start(f32[2,32,128]{2,1,0:T(8,128)S(1)} %pack.1), channel_id=1, source_target_pairs={{2,0},{4,2},{6,4},{3,1},{5,3},{7,5},{10,8},{12,10},{14,12},{11,9},... | collective-permute-start | bytes 98312 | tf_op jit(solution)/shard_map/ppermute | solution.py:548
  60.5 4.3 %collective-permute-start.1 = (f32[3,32,128]{2,1,0:T(8,128)S(1)}, f32[3,32,128]{2,1,0:T(8,128)S(1)}, u32[]{:S(2)}, u32[]{:S(2)}) collective-permute-start(f32[3,32,128]{2,1,0:T(8,128)S(1)} %place.1), channel_id=1, source_target_pairs={{0,1},{1,0},{2,3},{3,2},{4,5},{5,4},{6,7},{7,6},{8,9},{9,8},{10,11... | collective-permute-start | bytes 147464 | tf_op jit(solution)/shard_map/ppermute | solution.py:552
  64.8 8.7 %collective-permute-start.2 = (f32[3,8,128]{2,1,0:T(8,128)S(1)}, f32[3,8,128]{2,1,0:T(8,128)S(1)}, u32[]{:S(2)}, u32[]{:S(2)}) collective-permute-start(f32[3,8,128]{2,1,0:T(8,128)S(1)} %get-tuple-element.22), channel_id=1, source_target_pairs={{0,8},{8,16},{16,24},{24,32},{32,40},{40,48},{48,56},{56,64},{64,7... | collective-permute-start | bytes 36872 | tf_op jit(solution)/shard_map/ppermute | solution.py:543
  66.8 6.7 %collective-permute-start.3 = (f32[3,8,128]{2,1,0:T(8,128)S(1)}, f32[3,8,128]{2,1,0:T(8,128)S(1)}, u32[]{:S(2)}, u32[]{:S(2)}) collective-permute-start(f32[3,8,128]{2,1,0:T(8,128)S(1)} %get-tuple-element.23), channel_id=1, source_target_pairs={{8,0},{16,8},{24,16},{32,24},{40,32},{48,40},{56,48},{64,56},{72,6... | collective-permute-start | bytes 36872 | tf_op jit(solution)/shard_map/ppermute | solution.py:548
  68.1 10.8 %collective-permute-start.9 = (f32[22,4,128]{2,1,0:T(4,128)S(1)}, f32[22,4,128]{2,1,0:T(4,128)S(1)}, u32[]{:S(2)}, u32[]{:S(2)}) collective-permute-start(f32[22,4,128]{2,1,0:T(4,128)S(1)} %get-tuple-element.20), channel_id=1, source_target_pairs={{0,8},{8,16},{16,24},{24,32},{32,40},{40,48},{48,56},{56,64},{64,7... | collective-permute-start | bytes 135176 | tf_op jit(solution)/shard_map/ppermute | solution.py:543
  72.2 6.7 %collective-permute-start.10 = (f32[22,4,128]{2,1,0:T(4,128)S(1)}, f32[22,4,128]{2,1,0:T(4,128)S(1)}, u32[]{:S(2)}, u32[]{:S(2)}) collective-permute-start(f32[22,4,128]{2,1,0:T(4,128)S(1)} %get-tuple-element.21), channel_id=1, source_target_pairs={{8,0},{16,8},{24,16},{32,24},{40,32},{48,40},{56,48},{64,56},{72,6... | collective-permute-start | bytes 135176 | tf_op jit(solution)/shard_map/ppermute | solution.py:548
  73.5 5.5 %collective-permute-start.5 = (f32[3,48,128]{2,1,0:T(8,128)S(1)}, f32[3,48,128]{2,1,0:T(8,128)S(1)}, u32[]{:S(2)}, u32[]{:S(2)}) collective-permute-start(f32[3,48,128]{2,1,0:T(8,128)S(1)} %pad_maximum_fusion.1.own_ref), channel_id=1, source_target_pairs={{2,0},{4,2},{6,4},{3,1},{5,3},{7,5},{10,8},{12,10},{14,12},{11,9},... | collective-permute-start | bytes 221192 | tf_op jit(solution)/shard_map/ppermute | solution.py:548
  74.8 5.4 %collective-permute-start.4 = (f32[3,48,128]{2,1,0:T(8,128)S(1)}, f32[3,48,128]{2,1,0:T(8,128)S(1)}, u32[]{:S(2)}, u32[]{:S(2)}) collective-permute-start(f32[3,48,128]{2,1,0:T(8,128)S(1)} %pad_maximum_fusion.1.own_ref), channel_id=1, source_target_pairs={{0,2},{2,4},{4,6},{1,3},{3,5},{5,7},{8,10},{10,12},{12,14},{9,11},... | collective-permute-start | bytes 221192 | tf_op jit(solution)/shard_map/ppermute | solution.py:543

commit v3 on v2

--- a/solution.py
+++ b/solution.py
@@ -1,5 +1,4 @@
 import functools
-import math
 
 import jax
 import jax.numpy as jnp
@@ -182,7 +181,7 @@
     return tile
 
 
-def place_kernel(got_ref, out_ref):
+def place_kernel(got_ref, out_ref, edge_ref):
     sources = got_ref.shape[0]
     cells = PATCH_X * PATCH_Y
     local_x, local_y = out_ref.shape[1:]
@@ -204,14 +203,23 @@
         for i in range(places_x):
             tile = total[i * places_y : (i + 1) * places_y, c * cells : (c + 1) * cells]
             out_ref[c, i * PATCH_X : (i + 1) * PATCH_X, :] = swap_granules(tile, PATCH_Y)
+    lane = lax.broadcasted_iota(jnp.int32, edge_ref.shape, 1)
+    packed = jnp.zeros(edge_ref.shape, F32)
+    for c in range(3):
+        moved = pltpu.roll(out_ref[c], 2 * EDGE * c + EDGE, 1)
+        packed = jnp.where(lane // (2 * EDGE) == c, moved, packed)
+    edge_ref[...] = packed
 
 
 def place(got, local_x, local_y):
     return pl.pallas_call(
         place_kernel,
-        out_shape=jax.ShapeDtypeStruct((3, local_x, local_y), F32),
+        out_shape=(
+            jax.ShapeDtypeStruct((3, local_x, local_y), F32),
+            jax.ShapeDtypeStruct((local_x, local_y), F32),
+        ),
         in_specs=[VMEM],
-        out_specs=VMEM,
+        out_specs=(VMEM,) * 2,
         compiler_params=pltpu.CompilerParams(vmem_limit_bytes=8 << 20),
         cost_estimate=pl.CostEstimate(flops=40_000_000, bytes_accessed=1 << 19, transcendentals=0),
         name="place",
@@ -229,8 +237,8 @@
 
 
 def powers_kernel(
-    sizes, layers, at_ref, depth_ref, beyond_ref, own_ref, left_ref, right_ref, stiff_ref,
-    tally_ref, one_ref, two_ref, three_ref, row_ref, flat, keep, diag, w1, w2, div1, div2,
+    sizes, layers, at_ref, depth_ref, beyond_ref, mine_ref, theirs_ref, stiff_ref,
+    tally_ref, surface_ref, one_ref, two_ref, three_ref, row_ref, flat, keep, diag, w1, w2, div1, div2,
 ):
     rows, local_x = stiff_ref.shape[1], one_ref.shape[2]
     size_x, size_y, size_z = sizes
@@ -240,7 +248,7 @@
     at_x = lax.div(at, size_z * size_y)
     upper = at_z == 1
     sign = jnp.where(upper, -1.0, 1.0).astype(F32)
-    tall = own_ref.shape[1]
+    tall = mine_ref.shape[1]
 
     def layer_of(z):
         return jnp.where(upper, layers - 1 - z, z)
@@ -260,8 +268,13 @@
     in1 = jnp.where(outside_x | outside_y, 0.0, 1.0)
     inside = (in0, in1)
 
+    edges = mine_ref[3] + theirs_ref[3]
+
     def tiles(c):
-        return own_ref[c], jnp.where(half, right_ref[c], left_ref[c])
+        own = mine_ref[c] + theirs_ref[c]
+        surface_ref[c] = own[EDGE : tall - EDGE]
+        side = pltpu.roll(edges, LANES - EDGE - 2 * EDGE * c, 1)
+        return jnp.where(outside_x, 0.0, own), jnp.where(outside_x | outside_y, 0.0, side)
 
     def down(v):
         return pltpu.roll(v, tall - 1, 0)
@@ -411,21 +424,27 @@
     row = tally_ref[...]
     for k in range(6):
         row = jnp.where(spot == k, jnp.sum(sums[k]), row)
-    row_ref[...] = jnp.broadcast_to(row, row_ref.shape)
-
-
-def powers(sizes, at, depth, beyond, own, left, right, stiff, tally):
+    row_ref[...] = row
+
+
+def powers(sizes, at, depth, beyond, mine, theirs, stiff, tally):
     layers = depth.shape[0]
     _, rows, lanes = stiff.shape
-    tall = own.shape[1]
+    tall = mine.shape[1]
     local_x = tall - 2 * EDGE
     field = jax.ShapeDtypeStruct((3, layers, local_x, lanes), F32)
     deep = rows + 2 * EDGE
     return pl.pallas_call(
         functools.partial(powers_kernel, sizes, layers),
-        out_shape=(field, field, field, jax.ShapeDtypeStruct((math.prod(sizes), ROW), F32)),
-        in_specs=[SMEM] * 3 + [VMEM] * 5,
-        out_specs=(VMEM,) * 4,
+        out_shape=(
+            jax.ShapeDtypeStruct((3, local_x, lanes), F32),
+            field,
+            field,
+            field,
+            jax.ShapeDtypeStruct((1, ROW), F32),
+        ),
+        in_specs=[SMEM] * 3 + [VMEM] * 4,
+        out_specs=(VMEM,) * 5,
         scratch_shapes=[
             pltpu.VMEM((2, 9, tall, lanes), F32),
             pltpu.VMEM((2, tall, lanes), F32),
@@ -438,7 +457,7 @@
         compiler_params=pltpu.CompilerParams(vmem_limit_bytes=20 << 20),
         cost_estimate=pl.CostEstimate(flops=100_000_000, bytes_accessed=4 << 20, transcendentals=0),
         name="powers",
-    )(at, depth, beyond, own, left, right, stiff, tally)
+    )(at, depth, beyond, mine, theirs, stiff, tally)
 
 
 def step_factors(nu):
@@ -540,16 +559,21 @@
 
 def from_below(value, axis):
     count = lax.axis_size(axis)
-    return lax.ppermute(value, axis, [(i, i + 1) for i in range(count - 1)])
+    return lax.ppermute(value, axis, [(i, (i + 1) % count) for i in range(count)])
 
 
 def from_above(value, axis):
     count = lax.axis_size(axis)
-    return lax.ppermute(value, axis, [(i + 1, i) for i in range(count - 1)])
+    return lax.ppermute(value, axis, [((i + 1) % count, i) for i in range(count)])
 
 
 def from_partner(value, axis):
     return lax.ppermute(value, axis, [(0, 1), (1, 0)])
+
+
+def beside(left, right, width):
+    lane = lax.broadcasted_iota(jnp.int32, left.shape, left.ndim - 1)
+    return jnp.where(lane % (2 * width) >= width, right, left)
 
 
 def per_device(
@@ -580,29 +604,24 @@
     depth_beyond = from_partner(depth_kernel, "gz")
     far = from_partner(jnp.where(upper, stiffness[:REACH], stiffness[layers - REACH :]), "gz")
     packed = pack(stiffness, far)
-    lane = lax.broadcasted_iota(jnp.int32, packed.shape, 2)
-    side = jnp.where(lane % (2 * REACH) >= REACH, from_above(packed, "gy"), from_below(packed, "gy"))
+    side = beside(from_below(packed, "gy"), from_above(packed, "gy"), REACH)
     stiff = jnp.concatenate([stiffness, far, side])
     low, high = stiff[:, :REACH, :], stiff[:, local_x - REACH :, :]
     below = from_below(high, "gx")
     above = from_above(low, "gx")
     stiff = jnp.concatenate([below, stiff, above], axis=1)
 
-    part = place(got[:, 0], local_x, local_y)
-    surface = part + from_partner(part, "gz")
-    own = jnp.concatenate(
-        [
-            from_below(surface[:, local_x - EDGE :, :], "gx"),
-            surface,
-            from_above(surface[:, :EDGE, :], "gx"),
-        ],
-        axis=1,
+    part, edges = place(got[:, 0], local_x, local_y)
+    side = beside(from_below(edges, "gy"), from_above(edges, "gy"), EDGE)
+    mine = jnp.concatenate([part, side[None]])
+    mine = jnp.concatenate(
+        [from_below(mine[:, local_x - EDGE :, :], "gx"), mine, from_above(mine[:, :EDGE, :], "gx")], axis=1
     )
-    left, right = from_below(own, "gy"), from_above(own, "gy")
-    one, two, three, rows = powers(
-        sizes, at, depth_kernel, depth_beyond, own, left, right, stiff, tally
+    surface, one, two, three, row = powers(
+        sizes, at, depth_kernel, depth_beyond, mine, from_partner(mine, "gz"), stiff, tally
     )
-    rows = lax.all_to_all(rows, ("gx", "gy", "gz"), split_axis=0, concat_axis=0, tiled=True)
+    rows = jnp.broadcast_to(row + from_partner(row, "gz"), (owners, ROW))
+    rows = lax.all_to_all(rows, ("gx", "gy"), split_axis=0, concat_axis=0, tiled=True)
     return finish(depth_kernel, rows, surface, one, two, three)
 
 

time: 119 us -> 110 us (0.924)
  blocking collectives: 30.6 us -> 23.3 us
  starting transfers between devices: 51.8 us -> 49 us
  waiting for transfers between devices: 21.9 us -> 23.3 us
    all_to_all x1, blocking collectives: 30.6 us -> 23.3 us  [per_device(): lax.all_to_all(rows, ('gx', 'gy'), split_axis=0, concat_axis=0, tiled=True)]
    ppermute x8, starting transfers between devices: 17.6 us -> 12.9 us  [the longest x4 10.5 us: from_above(): lax.ppermute(value, axis, [((i + 1) % count, i) for i in range(count)])]
    ppermute x3 -> x4, starting transfers between devices: 4.6 us -> 6.49 us  [from_partner(): return lax.ppermute(value, axis, [(0, 1), (1, 0)])]
    ppermute x3 -> x4, waiting for transfers between devices: 2.07 us -> 2.88 us  [from_partner(): return lax.ppermute(value, axis, [(0, 1), (1, 0)])]
  transfers between devices with their start and end apart: 12 -> 13, of which waited for: 4 -> 5; matrix products, arithmetic and copies ran while one was open for 0% -> 0% of each run, Pallas kernels for 1% -> 1%
where the time goes in v3:
time: 110 us; the launch traced here: 109 us
  starting transfers between devices  49 us (45%)
  waiting for transfers between devices  23.3 us (21%)
  blocking collectives  23.3 us (21%)
  Pallas kernels  12.5 us (11%)
    all_to_all x1, starting transfers between devices, per_device(): lax.all_to_all(sums, ('gx', 'gy'), split_axis=0, concat_axis=0, tiled=True)  29.6 us
    all_to_all x1, blocking collectives, per_device(): lax.all_to_all(rows, ('gx', 'gy'), split_axis=0, concat_axis=0, tiled=True)  23.3 us
    all_to_all x1, waiting for transfers between devices, per_device(): lax.all_to_all(sums, ('gx', 'gy'), split_axis=0, concat_axis=0, tiled=True)  19.5 us
    ppermute x4, starting transfers between devices, from_above(): lax.ppermute(value, axis, [((i + 1) % count, i) for i in range(count)])  10.5 us
    ppermute x4, starting transfers between devices, from_partner(): return lax.ppermute(value, axis, [(0, 1), (1, 0)])  6.49 us
    pallas_call x1, Pallas kernels, powers(): pl.pallas_call(functools.partial(powers_kernel, sizes, layers), out_shape...  4.79 us
    pallas_call x1, Pallas kernels, front(): pl.pallas_call(front_kernel, out_shape=(jax.ShapeDtypeStruct((owners, 1,...  4.64 us
    ppermute x4, waiting for transfers between devices, from_partner(): return lax.ppermute(value, axis, [(0, 1), (1, 0)])  2.88 us
  transfers between devices with their start and end apart: 13, of which 5 were waited for; matrix products, arithmetic and copies ran while one was open for 0% of the time, Pallas kernels for 1%

profile of v3, /device:TPU:33, one launch (start us, length us, event | category | flops | bytes accessed | tf_op | source)
XLA Modules:
  0.0 109.2 jit_solution(18120777207071114407)
XLA Ops:
  0.6 0.0 copy-start
  0.6 0.0 copy-start.1
  0.7 4.6 %front.1 = (f32[64,1,1664]{2,1,0:T(1,128)}, f32[1,16]{1,0:T(1,128)}) custom-call(s32[64]{0:T(128)} %count_ref.1, f32[4,3]{1,0:T(4,128)} %look_ref.1, s32[64]{0:T(128)} %bitcast.12, s32[64]{0:T(128)} %patch_ref.1, s32[64]{0:T(128)} %choice_ref.1, f32[64,4,256]{2,1,0:T(4,128)} %observed_hbm.1, f32[64,4,256]{2,1,0:T(4,128)} %predicted_hbm.1, ...), custom_call_target="tpu_custom_call" | custom-call | flops 400000000 | bytes 4194304 | tf_op jit(solution)/shard_map/front/pallas_call | solution.py:121
  5.3 0.0 copy-start.2
  5.3 29.6 %all-to-all-start = ((f32[64,1,1664]{2,1,0:T(1,128)}), f32[64,1,1664]{2,1,0:T(1,128)S(1)}, u32[]{:S(2)}, u32[]{:S(2)}) async-start(f32[64,1,1664]{2,1,0:T(1,128)} %get-tuple-element.16), calls=%async_computation | async-start | bytes 851968 | tf_op jit(solution)/shard_map/all_to_all | solution.py:603
  34.9 0.0 copy-done.1
  34.9 1.0 collective-permute-start
  35.9 0.0 copy-done
  35.9 0.2 collective-permute-start.6
  36.1 1.2 %collective-permute-done.6.far_ref = f32[4,32,128]{2,1,0:T(8,128)S(1)} collective-permute-done((f32[4,32,128]{2,1,0:T(8,128)S(1)}, f32[4,32,128]{2,1,0:T(8,128)S(1)}, u32[]{:S(2)}, u32[]{:S(2)}) %collective-permute-start.6) | collective-permute-done | bytes 65568 | tf_op jit(solution)/shard_map/ppermute | solution.py:571
  37.3 0.1 pack.1
  37.5 0.5 collective-permute-start.8
  38.0 2.3 %collective-permute-start.7 = (f32[2,32,128]{2,1,0:T(8,128)S(1)}, f32[2,32,128]{2,1,0:T(8,128)S(1)}, u32[]{:S(2)}, u32[]{:S(2)}) collective-permute-start(f32[2,32,128]{2,1,0:T(8,128)S(1)} %pack.1), channel_id=1, source_target_pairs={{2,0},{4,2},{6,4},{0,6},{3,1},{5,3},{7,5},{1,7},{10,8},{12,10},{14... | collective-permute-start | bytes 98312 | tf_op jit(solution)/shard_map/ppermute | solution.py:567
  40.3 19.5 %all-to-all-done = f32[64,1,1664]{2,1,0:T(1,128)S(1)} async-done(((f32[64,1,1664]{2,1,0:T(1,128)}), f32[64,1,1664]{2,1,0:T(1,128)S(1)}, u32[]{:S(2)}, u32[]{:S(2)}) %all-to-all-start) | async-done | bytes 426016 | tf_op jit(solution)/shard_map/all_to_all | solution.py:603
  59.8 0.8 place.1
  60.5 1.6 %collective-permute-start.2 = (f32[32,128]{1,0:T(8,128)S(1)}, f32[32,128]{1,0:T(8,128)S(1)}, u32[]{:S(2)}, u32[]{:S(2)}) collective-permute-start(f32[32,128]{1,0:T(8,128)S(1)} %get-tuple-element.18), channel_id=1, source_target_pairs={{0,2},{2,4},{4,6},{6,0},{1,3},{3,5},{5,7},{7,1},{8,10},{10,12},{12... | collective-permute-start | bytes 49160 | tf_op jit(solution)/shard_map/ppermute | solution.py:562
  62.2 2.9 %collective-permute-start.1 = (f32[32,128]{1,0:T(8,128)S(1)}, f32[32,128]{1,0:T(8,128)S(1)}, u32[]{:S(2)}, u32[]{:S(2)}) collective-permute-start(f32[32,128]{1,0:T(8,128)S(1)} %get-tuple-element.18), channel_id=1, source_target_pairs={{2,0},{4,2},{6,4},{0,6},{3,1},{5,3},{7,5},{1,7},{10,8},{12,10},{14... | collective-permute-start | bytes 49160 | tf_op jit(solution)/shard_map/ppermute | solution.py:567
  65.1 0.0 collective-permute-done.8
  65.1 0.0 collective-permute-done.7
  65.1 1.0 collective-permute-done.2
  66.1 0.0 collective-permute-done.1
  66.1 0.1 collective-permute-start.3
  66.3 2.6 %collective-permute-start.4 = (f32[4,8,128]{2,1,0:T(8,128)S(1)}, f32[4,8,128]{2,1,0:T(8,128)S(1)}, u32[]{:S(2)}, u32[]{:S(2)}) collective-permute-start(f32[4,8,128]{2,1,0:T(8,128)S(1)} %get-tuple-element.29), channel_id=1, source_target_pairs={{8,0},{16,8},{24,16},{32,24},{40,32},{48,40},{56,48},{64,56},{72,6... | collective-permute-start | bytes 49160 | tf_op jit(solution)/shard_map/ppermute | solution.py:567
  68.9 0.1 collective-permute-start.9
  69.1 2.7 %collective-permute-start.10 = (f32[22,4,128]{2,1,0:T(4,128)S(1)}, f32[22,4,128]{2,1,0:T(4,128)S(1)}, u32[]{:S(2)}, u32[]{:S(2)}) collective-permute-start(f32[22,4,128]{2,1,0:T(4,128)S(1)} %get-tuple-element.27), channel_id=1, source_target_pairs={{8,0},{16,8},{24,16},{32,24},{40,32},{48,40},{56,48},{64,56},{72,6... | collective-permute-start | bytes 135176 | tf_op jit(solution)/shard_map/ppermute | solution.py:567
  71.7 0.0 collective-permute-done.3
  71.7 0.0 collective-permute-done.4
  71.7 4.2 %collective-permute-start.5 = (f32[4,48,128]{2,1,0:T(8,128)S(1)}, f32[4,48,128]{2,1,0:T(8,128)S(1)}, u32[]{:S(2)}, u32[]{:S(2)}) collective-permute-start(f32[4,48,128]{2,1,0:T(8,128)S(1)} %pad_maximum_fusion.1.mine_ref), channel_id=1, source_target_pairs={{0,1},{1,0},{2,3},{3,2},{4,5},{5,4},{6,7},{7,6},{8,9},{9,8},{10,11... | collective-permute-start | bytes 294920 | tf_op jit(solution)/shard_map/ppermute | solution.py:571
  75.9 0.0 collective-permute-done.9
  75.9 0.0 collective-permute-done.10
  75.9 0.1 pad_maximum_fusion.stiff_ref
  76.0 0.0 collective-permute-done.beyond_ref
  76.0 0.9 collective-permute-done.5.theirs_ref
  76.8 0.0 copy-done.2
  76.8 4.8 %powers.1 = (f32[3,32,128]{2,1,0:T(8,128)S(1)}, f32[3,16,32,128]{3,2,1,0:T(8,128)S(1)}, f32[3,16,32,128]{3,2,1,0:T(8,128)S(1)}, f32[3,16,32,128]{3,2,1,0:T(8,128)S(1)}, f32[1,16]{1,0:T(1,128)S(1)}) custom-call(s32[1]{0:T(128)} %bitcast.1.at_ref, f32[16]{0:T(128)S(1)} %copy-done.1, f32[16]{0:T(128)S(1)} %collective-permute-done.beyond_ref, ...), custom_call_target="tpu_custom_call" | custom-call | flops 100000000 | bytes 4194304 | tf_op jit(solution)/shard_map/powers/pallas_call | solution.py:437
  81.6 1.2 %collective-permute-start.11 = (f32[1,16]{1,0:T(1,128)S(1)}, f32[1,16]{1,0:T(1,128)S(1)}, u32[]{:S(2)}, u32[]{:S(2)}) collective-permute-start(f32[1,16]{1,0:T(1,128)S(1)} %get-tuple-element.21), channel_id=1, source_target_pairs={{0,1},{1,0},{2,3},{3,2},{4,5},{5,4},{6,7},{7,6},{8,9},{9,8},{10,11... | collective-permute-start | bytes 200 | tf_op jit(solution)/shard_map/ppermute | solution.py:571
  82.8 0.8 collective-permute-done.11
  83.7 23.3 %all_to_all.13 = f32[64,1,16]{2,1,0:T(1,128)S(1)} all-to-all(f32[64,1,16]{2,1,0:T(1,128)S(1)} %broadcast_in_dim.9), channel_id=1, replica_groups=mesh['grp'=2,'gx'=16,'gy'=4,'gz'=2] {'gx','gy'}, dimensions={0} | all-to-all | bytes 8192 | tf_op jit(solution)/shard_map/all_to_all | solution.py:624
  106.9 2.2 %finish.1 = (f32[3,16,32,128]{3,2,1,0:T(8,128)}, f32[3,16,32,128]{3,2,1,0:T(8,128)}) custom-call(f32[16]{0:T(128)S(1)} %copy-done.1, f32[64,16]{1,0:T(8,128)S(1)} %bitcast.11, f32[3,32,128]{2,1,0:T(8,128)S(1)} %get-tuple-element.22.surface_ref, f32[3,16,32,128]{3,2,1,0:T(8,128)S(1)} %get-tuple-element.23.one_ref, ...), custom_call_target="tpu_custom_call" | custom-call | flops 20000000 | bytes 4194304 | tf_op jit(solution)/shard_map/finish/pallas_call | solution.py:544
  (13 shorter events, 0.1 us)
Async XLA Ops:
  0.6 35.3 %copy-start = (f32[16,32,128]{2,1,0:T(8,128)S(1)}, f32[16,32,128]{2,1,0:T(8,128)}, u32[]{:S(2)}) copy-start(f32[16,32,128]{2,1,0:T(8,128)} %own_ref) | copy-start | bytes 786436
  0.6 34.3 %copy-start.1 = (f32[16]{0:T(128)S(1)}, f32[16]{0:T(128)}, u32[]{:S(2)}) copy-start(f32[16]{0:T(128)} %depth_ref.1) | copy-start | bytes 196
  5.3 71.5 %copy-start.2 = (f32[1,16]{1,0:T(1,128)S(1)}, f32[1,16]{1,0:T(1,128)}, u32[]{:S(2)}) copy-start(f32[1,16]{1,0:T(1,128)} %get-tuple-element.20.tally_ref) | copy-start | bytes 196
  5.3 54.4 %all-to-all-start = ((f32[64,1,1664]{2,1,0:T(1,128)}), f32[64,1,1664]{2,1,0:T(1,128)S(1)}, u32[]{:S(2)}, u32[]{:S(2)}) async-start(f32[64,1,1664]{2,1,0:T(1,128)} %get-tuple-element.16), calls=%async_computation | async-start | bytes 851968 | tf_op jit(solution)/shard_map/all_to_all | solution.py:603
  34.9 41.1 %collective-permute-start = (f32[16]{0:T(128)S(1)}, f32[16]{0:T(128)S(1)}, u32[]{:S(2)}, u32[]{:S(2)}) collective-permute-start(f32[16]{0:T(128)S(1)} %copy-done.1), channel_id=1, source_target_pairs={{0,1},{1,0},{2,3},{3,2},{4,5},{5,4},{6,7},{7,6},{8,9},{9,8},{10,11... | collective-permute-start | bytes 200 | tf_op jit(solution)/shard_map/ppermute | solution.py:571
  35.9 1.4 %collective-permute-start.6 = (f32[4,32,128]{2,1,0:T(8,128)S(1)}, f32[4,32,128]{2,1,0:T(8,128)S(1)}, u32[]{:S(2)}, u32[]{:S(2)}) collective-permute-start(f32[4,32,128]{2,1,0:T(8,128)S(1)} %slice_select_fusion), channel_id=1, source_target_pairs={{0,1},{1,0},{2,3},{3,2},{4,5},{5,4},{6,7},{7,6},{8,9},{9,8},{10,11... | collective-permute-start | bytes 196616 | tf_op jit(solution)/shard_map/ppermute | solution.py:571
  37.5 27.6 %collective-permute-start.8 = (f32[2,32,128]{2,1,0:T(8,128)S(1)}, f32[2,32,128]{2,1,0:T(8,128)S(1)}, u32[]{:S(2)}, u32[]{:S(2)}) collective-permute-start(f32[2,32,128]{2,1,0:T(8,128)S(1)} %pack.1), channel_id=1, source_target_pairs={{0,2},{2,4},{4,6},{6,0},{1,3},{3,5},{5,7},{7,1},{8,10},{10,12},{12... | collective-permute-start | bytes 98312 | tf_op jit(solution)/shard_map/ppermute | solution.py:562
  38.0 27.1 %collective-permute-start.7 = (f32[2,32,128]{2,1,0:T(8,128)S(1)}, f32[2,32,128]{2,1,0:T(8,128)S(1)}, u32[]{:S(2)}, u32[]{:S(2)}) collective-permute-start(f32[2,32,128]{2,1,0:T(8,128)S(1)} %pack.1), channel_id=1, source_target_pairs={{2,0},{4,2},{6,4},{0,6},{3,1},{5,3},{7,5},{1,7},{10,8},{12,10},{14... | collective-permute-start | bytes 98312 | tf_op jit(solution)/shard_map/ppermute | solution.py:567
  60.5 5.6 %collective-permute-start.2 = (f32[32,128]{1,0:T(8,128)S(1)}, f32[32,128]{1,0:T(8,128)S(1)}, u32[]{:S(2)}, u32[]{:S(2)}) collective-permute-start(f32[32,128]{1,0:T(8,128)S(1)} %get-tuple-element.18), channel_id=1, source_target_pairs={{0,2},{2,4},{4,6},{6,0},{1,3},{3,5},{5,7},{7,1},{8,10},{10,12},{12... | collective-permute-start | bytes 49160 | tf_op jit(solution)/shard_map/ppermute | solution.py:562
  62.2 3.9 %collective-permute-start.1 = (f32[32,128]{1,0:T(8,128)S(1)}, f32[32,128]{1,0:T(8,128)S(1)}, u32[]{:S(2)}, u32[]{:S(2)}) collective-permute-start(f32[32,128]{1,0:T(8,128)S(1)} %get-tuple-element.18), channel_id=1, source_target_pairs={{2,0},{4,2},{6,4},{0,6},{3,1},{5,3},{7,5},{1,7},{10,8},{12,10},{14... | collective-permute-start | bytes 49160 | tf_op jit(solution)/shard_map/ppermute | solution.py:567
  66.1 5.6 %collective-permute-start.3 = (f32[4,8,128]{2,1,0:T(8,128)S(1)}, f32[4,8,128]{2,1,0:T(8,128)S(1)}, u32[]{:S(2)}, u32[]{:S(2)}) collective-permute-start(f32[4,8,128]{2,1,0:T(8,128)S(1)} %get-tuple-element.28), channel_id=1, source_target_pairs={{0,8},{8,16},{16,24},{24,32},{32,40},{40,48},{48,56},{56,64},{64,7... | collective-permute-start | bytes 49160 | tf_op jit(solution)/shard_map/ppermute | solution.py:562
  66.3 5.5 %collective-permute-start.4 = (f32[4,8,128]{2,1,0:T(8,128)S(1)}, f32[4,8,128]{2,1,0:T(8,128)S(1)}, u32[]{:S(2)}, u32[]{:S(2)}) collective-permute-start(f32[4,8,128]{2,1,0:T(8,128)S(1)} %get-tuple-element.29), channel_id=1, source_target_pairs={{8,0},{16,8},{24,16},{32,24},{40,32},{48,40},{56,48},{64,56},{72,6... | collective-permute-start | bytes 49160 | tf_op jit(solution)/shard_map/ppermute | solution.py:567
  68.9 7.0 %collective-permute-start.9 = (f32[22,4,128]{2,1,0:T(4,128)S(1)}, f32[22,4,128]{2,1,0:T(4,128)S(1)}, u32[]{:S(2)}, u32[]{:S(2)}) collective-permute-start(f32[22,4,128]{2,1,0:T(4,128)S(1)} %get-tuple-element.26), channel_id=1, source_target_pairs={{0,8},{8,16},{16,24},{24,32},{32,40},{40,48},{48,56},{56,64},{64,7... | collective-permute-start | bytes 135176 | tf_op jit(solution)/shard_map/ppermute | solution.py:562
  69.1 6.8 %collective-permute-start.10 = (f32[22,4,128]{2,1,0:T(4,128)S(1)}, f32[22,4,128]{2,1,0:T(4,128)S(1)}, u32[]{:S(2)}, u32[]{:S(2)}) collective-permute-start(f32[22,4,128]{2,1,0:T(4,128)S(1)} %get-tuple-element.27), channel_id=1, source_target_pairs={{8,0},{16,8},{24,16},{32,24},{40,32},{48,40},{56,48},{64,56},{72,6... | collective-permute-start | bytes 135176 | tf_op jit(solution)/shard_map/ppermute | solution.py:567
  71.7 5.1 %collective-permute-start.5 = (f32[4,48,128]{2,1,0:T(8,128)S(1)}, f32[4,48,128]{2,1,0:T(8,128)S(1)}, u32[]{:S(2)}, u32[]{:S(2)}) collective-permute-start(f32[4,48,128]{2,1,0:T(8,128)S(1)} %pad_maximum_fusion.1.mine_ref), channel_id=1, source_target_pairs={{0,1},{1,0},{2,3},{3,2},{4,5},{5,4},{6,7},{7,6},{8,9},{9,8},{10,11... | collective-permute-start | bytes 294920 | tf_op jit(solution)/shard_map/ppermute | solution.py:571
  81.6 2.0 %collective-permute-start.11 = (f32[1,16]{1,0:T(1,128)S(1)}, f32[1,16]{1,0:T(1,128)S(1)}, u32[]{:S(2)}, u32[]{:S(2)}) collective-permute-start(f32[1,16]{1,0:T(1,128)S(1)} %get-tuple-element.21), channel_id=1, source_target_pairs={{0,1},{1,0},{2,3},{3,2},{4,5},{5,4},{6,7},{7,6},{8,9},{9,8},{10,11... | collective-permute-start | bytes 200 | tf_op jit(solution)/shard_map/ppermute | solution.py:571

commit v4 on v3

--- a/solution.py
+++ b/solution.py
@@ -34,8 +34,9 @@
 
 
 def front_kernel(
-    count_ref, look_ref, owner_ref, patch_ref, choice_ref, observed_hbm, predicted_hbm, mask_hbm, weights_hbm,
+    count_hbm, look_hbm, owner_hbm, patch_hbm, choice_hbm, observed_hbm, predicted_hbm, mask_hbm, weights_hbm,
     out_ref, tally_ref,
+    count_ref, look_ref, owner_ref, patch_ref, choice_ref,
     observed_ref, predicted_ref, mask_ref, weights_ref, coeffs_ref, sums_ref, used_ref, ids_ref, rank_ref, sems,
 ):
     blocks, _, pixels = observed_ref.shape
@@ -45,7 +46,16 @@
     first = [
         pltpu.make_async_copy(src, dst, sems.at[k])
         for k, (src, dst) in enumerate(
-            ((observed_hbm, observed_ref), (predicted_hbm, predicted_ref), (mask_hbm, mask_ref))
+            (
+                (owner_hbm, owner_ref),
+                (patch_hbm, patch_ref),
+                (choice_hbm, choice_ref),
+                (count_hbm, count_ref),
+                (look_hbm, look_ref),
+                (observed_hbm, observed_ref),
+                (predicted_hbm, predicted_ref),
+                (mask_hbm, mask_ref),
+            )
         )
     ]
     chunk = tables // PIECES
@@ -55,18 +65,20 @@
         second.append(pltpu.make_async_copy(weights_hbm.at[part], weights_ref.at[part], sems.at[len(first) + piece]))
     for copy in first + second:
         copy.start()
-
+    out_ref[...] = jnp.zeros_like(out_ref)
     for o in range(owners):
         used_ref[o] = 0
         for r in range(CAP):
             ids_ref[o * CAP + r] = 0
+    for copy in first[:3]:
+        copy.wait()
+
     for b in range(blocks):
         o = owner_ref[b]
         r = used_ref[o]
         used_ref[o] = r + 1
         rank_ref[b] = r
         ids_ref[o * CAP + r] = patch_ref[b]
-    out_ref[...] = jnp.zeros_like(out_ref)
     spot = lax.broadcasted_iota(jnp.int32, (1, lanes), 1)
     for o in range(owners):
         ids = jnp.zeros((1, lanes), jnp.int32)
@@ -75,7 +87,7 @@
         out_ref[o, :, 3 * CAP * lanes :] = ids.astype(F32)
     choice = jnp.concatenate([column(choice_ref, g, 8, lanes) for g in range(0, blocks, 8)] * 3, axis=0)
 
-    for copy in first:
+    for copy in first[3:]:
         copy.wait()
     group = 16
     place = lax.broadcasted_iota(jnp.int32, (group, pixels), 1)
@@ -104,9 +116,11 @@
     total = jnp.zeros(sums_ref.shape, F32)
     for piece in range(PIECES):
         second[piece].wait()
-        for t in range(piece * chunk, (piece + 1) * chunk):
-            product = jnp.dot(coeffs, weights_ref[t], preferred_element_type=F32)
-            total = jnp.where(choice == t, product, total)
+        for t in range(piece * chunk, (piece + 1) * chunk, 2):
+            pair = jnp.concatenate([weights_ref[t], weights_ref[t + 1]], axis=1)
+            product = jnp.dot(coeffs, pair, preferred_element_type=F32)
+            total = jnp.where(choice == t, product[:, :lanes], total)
+            total = jnp.where(choice == t + 1, product[:, lanes:], total)
     sums_ref[...] = total
     for b in range(blocks):
         o, r = owner_ref[b], rank_ref[b]
@@ -124,9 +138,14 @@
             jax.ShapeDtypeStruct((owners, 1, (3 * CAP + 1) * cells), F32),
             jax.ShapeDtypeStruct((1, ROW), F32),
         ),
-        in_specs=[SMEM] * 5 + [ANY] * 4,
+        in_specs=[ANY] * 9,
         out_specs=(VMEM,) * 2,
         scratch_shapes=[
+            pltpu.SMEM((blocks,), jnp.int32),
+            pltpu.SMEM(look.shape, F32),
+            pltpu.SMEM((blocks,), jnp.int32),
+            pltpu.SMEM((blocks,), jnp.int32),
+            pltpu.SMEM((blocks,), jnp.int32),
             pltpu.VMEM(observed.shape, F32),
             pltpu.VMEM(observed.shape, F32),
             pltpu.VMEM(mask.shape, jnp.int32),
@@ -136,7 +155,7 @@
             pltpu.SMEM((owners,), jnp.int32),
             pltpu.SMEM((owners * CAP,), jnp.int32),
             pltpu.SMEM((blocks,), jnp.int32),
-            pltpu.SemaphoreType.DMA((3 + PIECES,)),
+            pltpu.SemaphoreType.DMA((8 + PIECES,)),
         ],
         cost_estimate=pl.CostEstimate(flops=400_000_000, bytes_accessed=4 << 20, transcendentals=0),
         name="front",
@@ -238,7 +257,7 @@
 
 def powers_kernel(
     sizes, layers, at_ref, depth_ref, beyond_ref, mine_ref, theirs_ref, stiff_ref,
-    tally_ref, surface_ref, one_ref, two_ref, three_ref, row_ref, flat, keep, diag, w1, w2, div1, div2,
+    tally_ref, surface_ref, one_ref, two_ref, three_ref, row_ref, flat, keep, diag, w1, w2, div1, div2, across1, across2,
 ):
     rows, local_x = stiff_ref.shape[1], one_ref.shape[2]
     size_x, size_y, size_z = sizes
@@ -338,9 +357,10 @@
         div1[0, t] = jnp.zeros_like(div1[0, t])
         div2[0, t] = jnp.zeros_like(div2[0, t])
 
-    def spread(w, div, z):
+    def spread(w, div, across, z):
         ahead, behind = lane_steps(w[1, z, 0, body, :], w[1, z, 1, body, :])
         for t in range(2):
+            across[z, t] = ahead[t] + behind[t]
             total = w[0, z, t, ahead_x, :] - w[0, z, t, behind_x, :] + ahead[t] - behind[t]
             total += w[2, z + 1, t, body, :] - w[2, z - 1, t, body, :]
             div[z, t, body, :] = keep[t, flat_rows, :] * total
@@ -348,9 +368,11 @@
     def apply_second(z):
         ahead, behind = lane_steps(div1[z + 1, 0, body, :], div1[z + 1, 1, body, :])
         for c in range(3):
-            yp, ym = lane_steps(w1[c, z + 1, 0, body, :], w1[c, z + 1, 1, body, :])
+            if c != 1:
+                yp, ym = lane_steps(w1[c, z + 1, 0, body, :], w1[c, z + 1, 1, body, :])
             for t in range(2):
-                around = w1[c, z + 1, t, ahead_x, :] + w1[c, z + 1, t, behind_x, :] + yp[t] + ym[t]
+                around = w1[c, z + 1, t, ahead_x, :] + w1[c, z + 1, t, behind_x, :]
+                around += across1[z + 1, t] if c == 1 else yp[t] + ym[t]
                 around += w1[c, z, t, body, :] + w1[c, z + 2, t, body, :]
                 if c == 0:
                     slope = div1[z + 1, t, ahead_x, :] - div1[z + 1, t, behind_x, :]
@@ -368,8 +390,8 @@
     at_last, at_first = narrow == LANES - 1, narrow == 0
 
     def sides_of(own, side):
-        ahead = jnp.where(at_last, pltpu.roll(side, LANES - 1, 1), pltpu.roll(own, LANES - 1, 1))
-        behind = jnp.where(at_first, pltpu.roll(side, 1, 1), pltpu.roll(own, 1, 1))
+        ahead = pltpu.roll(jnp.where(at_first, side, own), LANES - 1, 1)
+        behind = pltpu.roll(jnp.where(at_last, side, own), 1, 1)
         return ahead, behind
 
     def fold(v):
@@ -384,8 +406,12 @@
         ahead, behind = sides_of(div2[z + 1, 0, mid, :], div2[z + 1, 1, mid, :])
         for c in range(3):
             centre = w2[c, z + 1, 0, mid, :]
-            yp, ym = sides_of(centre, w2[c, z + 1, 1, mid, :])
-            around = w2[c, z + 1, 0, mid_ahead, :] + w2[c, z + 1, 0, mid_behind, :] + yp + ym
+            around = w2[c, z + 1, 0, mid_ahead, :] + w2[c, z + 1, 0, mid_behind, :]
+            if c == 1:
+                around += across2[z + 1, 0, pl.ds(REACH, local_x), :]
+            else:
+                yp, ym = sides_of(centre, w2[c, z + 1, 1, mid, :])
+                around += yp + ym
             around += w2[c, z, 0, mid, :] + w2[c, z + 2, 0, mid, :]
             if c == 0:
                 slope = div2[z + 1, 0, mid_ahead, :] - div2[z + 1, 0, mid_behind, :]
@@ -405,19 +431,19 @@
 
     zero = jnp.zeros((8, LANES), F32)
     sums = [zero] * 6
-    for step in range(layers + REACH + 4):
-        for stage, (count, lag) in enumerate(((REACH, 0), (REACH - 1, 1), (REACH - 2, 2), (1, 3), (0, 4))):
+    for step in range(layers + REACH + 8):
+        for stage, (count, lag) in reversed(tuple(enumerate(((REACH, 0), (REACH - 1, 2), (REACH - 2, 4), (1, 6), (0, 8))))):
             z = step - lag
             if not 0 <= z < layers + count:
                 continue
             if stage == 0:
                 apply_first(z)
             elif stage == 1:
-                spread(w1, div1, z + 1)
+                spread(w1, div1, across1, z + 1)
             elif stage == 2:
                 apply_second(z)
             elif stage == 3:
-                spread(w2, div2, z + 1)
+                spread(w2, div2, across2, z + 1)
             else:
                 apply_third(z, sums)
     spot = lax.broadcasted_iota(jnp.int32, (1, ROW), 1)
@@ -453,6 +479,8 @@
             pltpu.VMEM((3, layers + REACH - 1, 2, deep, lanes), F32),
             pltpu.VMEM((layers + REACH, 2, deep, lanes), F32),
             pltpu.VMEM((layers + REACH // 2, 2, deep, lanes), F32),
+            pltpu.VMEM((layers + REACH, 2, rows, lanes), F32),
+            pltpu.VMEM((layers + REACH // 2, 2, rows, lanes), F32),
         ],
         compiler_params=pltpu.CompilerParams(vmem_limit_bytes=20 << 20),
         cost_estimate=pl.CostEstimate(flops=100_000_000, bytes_accessed=4 << 20, transcendentals=0),
@@ -514,9 +542,9 @@
     shape = surface_ref.shape[1:]
     found = [jnp.broadcast_to(scale * v, shape) for v in found]
     resid = [jnp.broadcast_to(scale * v, shape) for v in resid]
-    chunk = layers // PIECES
+    chunk = layers // 8
     copies = []
-    for piece in range(PIECES):
+    for piece in range(8):
         first = piece * chunk
 
         def one_layer(k, carry, first=first):
@@ -549,7 +577,7 @@
         scratch_shapes=[
             pltpu.VMEM(one.shape, F32),
             pltpu.VMEM(one.shape, F32),
-            pltpu.SemaphoreType.DMA((2, PIECES)),
+            pltpu.SemaphoreType.DMA((2, 8)),
         ],
         compiler_params=pltpu.CompilerParams(vmem_limit_bytes=12 << 20),
         cost_estimate=pl.CostEstimate(flops=20_000_000, bytes_accessed=4 << 20, transcendentals=0),

time: 110 us -> 108 us (0.982)
  Pallas kernels: 12.5 us -> 11 us
where the time goes in v4:
time: 108 us
  starting transfers between devices  49 us (45%)
  waiting for transfers between devices  23.3 us (22%)
  blocking collectives  23.3 us (22%)
  Pallas kernels  11 us (10%)
    all_to_all x1, starting transfers between devices, per_device(): lax.all_to_all(sums, ('gx', 'gy'), split_axis=0, concat_axis=0, tiled=True)  29.6 us
    all_to_all x1, blocking collectives, per_device(): lax.all_to_all(rows, ('gx', 'gy'), split_axis=0, concat_axis=0, tiled=True)  23.3 us
    all_to_all x1, waiting for transfers between devices, per_device(): lax.all_to_all(sums, ('gx', 'gy'), split_axis=0, concat_axis=0, tiled=True)  19.5 us
    ppermute x4, starting transfers between devices, from_above(): lax.ppermute(value, axis, [((i + 1) % count, i) for i in range(count)])  10.5 us
    ppermute x4, starting transfers between devices, from_partner(): return lax.ppermute(value, axis, [(0, 1), (1, 0)])  6.5 us
    pallas_call x1, Pallas kernels, powers(): pl.pallas_call(functools.partial(powers_kernel, sizes, layers), out_shape...  4.25 us
    pallas_call x1, Pallas kernels, front(): pl.pallas_call(front_kernel, out_shape=(jax.ShapeDtypeStruct((owners, 1,...  3.67 us
    ppermute x4, waiting for transfers between devices, from_partner(): return lax.ppermute(value, axis, [(0, 1), (1, 0)])  2.88 us
  transfers between devices with their start and end apart: 13, of which 5 were waited for; matrix products, arithmetic and copies ran while one was open for 0% of the time, Pallas kernels for 1%

profile of v4, /device:TPU:33, one launch (start us, length us, event | category | flops | bytes accessed | tf_op | source)
XLA Modules:
  0.0 107.7 jit_solution(8277432416603622127)
XLA Ops:
  0.6 0.0 copy-start
  0.6 0.0 copy-start.1
  0.7 3.7 %front.1 = (f32[64,1,1664]{2,1,0:T(1,128)}, f32[1,16]{1,0:T(1,128)}) custom-call(s32[64]{0:T(128)} %count_hbm.1, f32[4,3]{1,0:T(4,128)} %look_hbm.1, s32[64]{0:T(128)} %bitcast.12, s32[64]{0:T(128)} %patch_hbm.1, s32[64]{0:T(128)} %choice_hbm.1, f32[64,4,256]{2,1,0:T(4,128)} %observed_hbm.1, f32[64,4,256]{2,1,0:T(4,128)} %predicted_hbm.1, ...), custom_call_target="tpu_custom_call" | custom-call | flops 400000000 | bytes 4194304 | tf_op jit(solution)/shard_map/front/pallas_call | solution.py:135
  4.3 0.0 copy-start.2
  4.3 29.6 %all-to-all-start = ((f32[64,1,1664]{2,1,0:T(1,128)}), f32[64,1,1664]{2,1,0:T(1,128)S(1)}, u32[]{:S(2)}, u32[]{:S(2)}) async-start(f32[64,1,1664]{2,1,0:T(1,128)} %get-tuple-element.16), calls=%async_computation | async-start | bytes 851968 | tf_op jit(solution)/shard_map/all_to_all | solution.py:631
  33.9 0.0 copy-done.1
  34.0 1.0 collective-permute-start
  35.0 0.0 copy-done
  35.0 0.2 collective-permute-start.6
  35.2 1.2 %collective-permute-done.6.far_ref = f32[4,32,128]{2,1,0:T(8,128)S(1)} collective-permute-done((f32[4,32,128]{2,1,0:T(8,128)S(1)}, f32[4,32,128]{2,1,0:T(8,128)S(1)}, u32[]{:S(2)}, u32[]{:S(2)}) %collective-permute-start.6) | collective-permute-done | bytes 65568 | tf_op jit(solution)/shard_map/ppermute | solution.py:599
  36.4 0.1 pack.1
  36.5 0.5 collective-permute-start.8
  37.0 2.3 %collective-permute-start.7 = (f32[2,32,128]{2,1,0:T(8,128)S(1)}, f32[2,32,128]{2,1,0:T(8,128)S(1)}, u32[]{:S(2)}, u32[]{:S(2)}) collective-permute-start(f32[2,32,128]{2,1,0:T(8,128)S(1)} %pack.1), channel_id=1, source_target_pairs={{2,0},{4,2},{6,4},{0,6},{3,1},{5,3},{7,5},{1,7},{10,8},{12,10},{14... | collective-permute-start | bytes 98312 | tf_op jit(solution)/shard_map/ppermute | solution.py:595
  39.3 19.5 %all-to-all-done = f32[64,1,1664]{2,1,0:T(1,128)S(1)} async-done(((f32[64,1,1664]{2,1,0:T(1,128)}), f32[64,1,1664]{2,1,0:T(1,128)S(1)}, u32[]{:S(2)}, u32[]{:S(2)}) %all-to-all-start) | async-done | bytes 426016 | tf_op jit(solution)/shard_map/all_to_all | solution.py:631
  58.8 0.8 place.1
  59.6 1.6 %collective-permute-start.2 = (f32[32,128]{1,0:T(8,128)S(1)}, f32[32,128]{1,0:T(8,128)S(1)}, u32[]{:S(2)}, u32[]{:S(2)}) collective-permute-start(f32[32,128]{1,0:T(8,128)S(1)} %get-tuple-element.18), channel_id=1, source_target_pairs={{0,2},{2,4},{4,6},{6,0},{1,3},{3,5},{5,7},{7,1},{8,10},{10,12},{12... | collective-permute-start | bytes 49160 | tf_op jit(solution)/shard_map/ppermute | solution.py:590
  61.2 2.9 %collective-permute-start.1 = (f32[32,128]{1,0:T(8,128)S(1)}, f32[32,128]{1,0:T(8,128)S(1)}, u32[]{:S(2)}, u32[]{:S(2)}) collective-permute-start(f32[32,128]{1,0:T(8,128)S(1)} %get-tuple-element.18), channel_id=1, source_target_pairs={{2,0},{4,2},{6,4},{0,6},{3,1},{5,3},{7,5},{1,7},{10,8},{12,10},{14... | collective-permute-start | bytes 49160 | tf_op jit(solution)/shard_map/ppermute | solution.py:595
  64.1 0.0 collective-permute-done.8
  64.1 0.0 collective-permute-done.7
  64.1 1.0 collective-permute-done.2
  65.1 0.0 collective-permute-done.1
  65.2 0.1 collective-permute-start.3
  65.3 2.6 %collective-permute-start.4 = (f32[4,8,128]{2,1,0:T(8,128)S(1)}, f32[4,8,128]{2,1,0:T(8,128)S(1)}, u32[]{:S(2)}, u32[]{:S(2)}) collective-permute-start(f32[4,8,128]{2,1,0:T(8,128)S(1)} %get-tuple-element.29), channel_id=1, source_target_pairs={{8,0},{16,8},{24,16},{32,24},{40,32},{48,40},{56,48},{64,56},{72,6... | collective-permute-start | bytes 49160 | tf_op jit(solution)/shard_map/ppermute | solution.py:595
  68.0 0.1 collective-permute-start.9
  68.1 2.6 %collective-permute-start.10 = (f32[22,4,128]{2,1,0:T(4,128)S(1)}, f32[22,4,128]{2,1,0:T(4,128)S(1)}, u32[]{:S(2)}, u32[]{:S(2)}) collective-permute-start(f32[22,4,128]{2,1,0:T(4,128)S(1)} %get-tuple-element.27), channel_id=1, source_target_pairs={{8,0},{16,8},{24,16},{32,24},{40,32},{48,40},{56,48},{64,56},{72,6... | collective-permute-start | bytes 135176 | tf_op jit(solution)/shard_map/ppermute | solution.py:595
  70.8 0.0 collective-permute-done.3
  70.8 0.0 collective-permute-done.4
  70.8 4.3 %collective-permute-start.5 = (f32[4,48,128]{2,1,0:T(8,128)S(1)}, f32[4,48,128]{2,1,0:T(8,128)S(1)}, u32[]{:S(2)}, u32[]{:S(2)}) collective-permute-start(f32[4,48,128]{2,1,0:T(8,128)S(1)} %pad_maximum_fusion.1.mine_ref), channel_id=1, source_target_pairs={{0,1},{1,0},{2,3},{3,2},{4,5},{5,4},{6,7},{7,6},{8,9},{9,8},{10,11... | collective-permute-start | bytes 294920 | tf_op jit(solution)/shard_map/ppermute | solution.py:599
  75.1 0.0 collective-permute-done.9
  75.1 0.0 collective-permute-done.10
  75.1 0.1 pad_maximum_fusion.stiff_ref
  75.2 0.0 collective-permute-done.beyond_ref
  75.2 0.9 collective-permute-done.5.theirs_ref
  76.1 0.0 copy-done.2
  76.1 4.2 %powers.1 = (f32[3,32,128]{2,1,0:T(8,128)S(1)}, f32[3,16,32,128]{3,2,1,0:T(8,128)S(1)}, f32[3,16,32,128]{3,2,1,0:T(8,128)S(1)}, f32[3,16,32,128]{3,2,1,0:T(8,128)S(1)}, f32[1,16]{1,0:T(1,128)S(1)}) custom-call(s32[1]{0:T(128)} %bitcast.1.at_ref, f32[16]{0:T(128)S(1)} %copy-done.1, f32[16]{0:T(128)S(1)} %collective-permute-done.beyond_ref, ...), custom_call_target="tpu_custom_call" | custom-call | flops 100000000 | bytes 4194304 | tf_op jit(solution)/shard_map/powers/pallas_call | solution.py:463
  80.3 1.0 collective-permute-start.11
  81.3 0.8 collective-permute-done.11
  82.1 23.3 %all_to_all.13 = f32[64,1,16]{2,1,0:T(1,128)S(1)} all-to-all(f32[64,1,16]{2,1,0:T(1,128)S(1)} %broadcast_in_dim.9), channel_id=1, replica_groups=mesh['grp'=2,'gx'=16,'gy'=4,'gz'=2] {'gx','gy'}, dimensions={0} | all-to-all | bytes 8192 | tf_op jit(solution)/shard_map/all_to_all | solution.py:652
  105.4 2.2 %finish.1 = (f32[3,16,32,128]{3,2,1,0:T(8,128)}, f32[3,16,32,128]{3,2,1,0:T(8,128)}) custom-call(f32[16]{0:T(128)S(1)} %copy-done.1, f32[64,16]{1,0:T(8,128)S(1)} %bitcast.11, f32[3,32,128]{2,1,0:T(8,128)S(1)} %get-tuple-element.22.surface_ref, f32[3,16,32,128]{3,2,1,0:T(8,128)S(1)} %get-tuple-element.23.one_ref, ...), custom_call_target="tpu_custom_call" | custom-call | flops 20000000 | bytes 4194304 | tf_op jit(solution)/shard_map/finish/pallas_call | solution.py:572
  (13 shorter events, 0.1 us)
Async XLA Ops:
  0.6 34.3 %copy-start = (f32[16,32,128]{2,1,0:T(8,128)S(1)}, f32[16,32,128]{2,1,0:T(8,128)}, u32[]{:S(2)}) copy-start(f32[16,32,128]{2,1,0:T(8,128)} %own_ref) | copy-start | bytes 786436
  0.6 33.3 %copy-start.1 = (f32[16]{0:T(128)S(1)}, f32[16]{0:T(128)}, u32[]{:S(2)}) copy-start(f32[16]{0:T(128)} %depth_ref.1) | copy-start | bytes 196
  4.3 71.7 %copy-start.2 = (f32[1,16]{1,0:T(1,128)S(1)}, f32[1,16]{1,0:T(1,128)}, u32[]{:S(2)}) copy-start(f32[1,16]{1,0:T(1,128)} %get-tuple-element.20.tally_ref) | copy-start | bytes 196
  4.3 54.4 %all-to-all-start = ((f32[64,1,1664]{2,1,0:T(1,128)}), f32[64,1,1664]{2,1,0:T(1,128)S(1)}, u32[]{:S(2)}, u32[]{:S(2)}) async-start(f32[64,1,1664]{2,1,0:T(1,128)} %get-tuple-element.16), calls=%async_computation | async-start | bytes 851968 | tf_op jit(solution)/shard_map/all_to_all | solution.py:631
  34.0 41.2 %collective-permute-start = (f32[16]{0:T(128)S(1)}, f32[16]{0:T(128)S(1)}, u32[]{:S(2)}, u32[]{:S(2)}) collective-permute-start(f32[16]{0:T(128)S(1)} %copy-done.1), channel_id=1, source_target_pairs={{0,1},{1,0},{2,3},{3,2},{4,5},{5,4},{6,7},{7,6},{8,9},{9,8},{10,11... | collective-permute-start | bytes 200 | tf_op jit(solution)/shard_map/ppermute | solution.py:599
  35.0 1.4 %collective-permute-start.6 = (f32[4,32,128]{2,1,0:T(8,128)S(1)}, f32[4,32,128]{2,1,0:T(8,128)S(1)}, u32[]{:S(2)}, u32[]{:S(2)}) collective-permute-start(f32[4,32,128]{2,1,0:T(8,128)S(1)} %slice_select_fusion), channel_id=1, source_target_pairs={{0,1},{1,0},{2,3},{3,2},{4,5},{5,4},{6,7},{7,6},{8,9},{9,8},{10,11... | collective-permute-start | bytes 196616 | tf_op jit(solution)/shard_map/ppermute | solution.py:599
  36.5 27.6 %collective-permute-start.8 = (f32[2,32,128]{2,1,0:T(8,128)S(1)}, f32[2,32,128]{2,1,0:T(8,128)S(1)}, u32[]{:S(2)}, u32[]{:S(2)}) collective-permute-start(f32[2,32,128]{2,1,0:T(8,128)S(1)} %pack.1), channel_id=1, source_target_pairs={{0,2},{2,4},{4,6},{6,0},{1,3},{3,5},{5,7},{7,1},{8,10},{10,12},{12... | collective-permute-start | bytes 98312 | tf_op jit(solution)/shard_map/ppermute | solution.py:590
  37.0 27.1 %collective-permute-start.7 = (f32[2,32,128]{2,1,0:T(8,128)S(1)}, f32[2,32,128]{2,1,0:T(8,128)S(1)}, u32[]{:S(2)}, u32[]{:S(2)}) collective-permute-start(f32[2,32,128]{2,1,0:T(8,128)S(1)} %pack.1), channel_id=1, source_target_pairs={{2,0},{4,2},{6,4},{0,6},{3,1},{5,3},{7,5},{1,7},{10,8},{12,10},{14... | collective-permute-start | bytes 98312 | tf_op jit(solution)/shard_map/ppermute | solution.py:595
  59.6 5.6 %collective-permute-start.2 = (f32[32,128]{1,0:T(8,128)S(1)}, f32[32,128]{1,0:T(8,128)S(1)}, u32[]{:S(2)}, u32[]{:S(2)}) collective-permute-start(f32[32,128]{1,0:T(8,128)S(1)} %get-tuple-element.18), channel_id=1, source_target_pairs={{0,2},{2,4},{4,6},{6,0},{1,3},{3,5},{5,7},{7,1},{8,10},{10,12},{12... | collective-permute-start | bytes 49160 | tf_op jit(solution)/shard_map/ppermute | solution.py:590
  61.2 3.9 %collective-permute-start.1 = (f32[32,128]{1,0:T(8,128)S(1)}, f32[32,128]{1,0:T(8,128)S(1)}, u32[]{:S(2)}, u32[]{:S(2)}) collective-permute-start(f32[32,128]{1,0:T(8,128)S(1)} %get-tuple-element.18), channel_id=1, source_target_pairs={{2,0},{4,2},{6,4},{0,6},{3,1},{5,3},{7,5},{1,7},{10,8},{12,10},{14... | collective-permute-start | bytes 49160 | tf_op jit(solution)/shard_map/ppermute | solution.py:595
  65.2 5.6 %collective-permute-start.3 = (f32[4,8,128]{2,1,0:T(8,128)S(1)}, f32[4,8,128]{2,1,0:T(8,128)S(1)}, u32[]{:S(2)}, u32[]{:S(2)}) collective-permute-start(f32[4,8,128]{2,1,0:T(8,128)S(1)} %get-tuple-element.28), channel_id=1, source_target_pairs={{0,8},{8,16},{16,24},{24,32},{32,40},{40,48},{48,56},{56,64},{64,7... | collective-permute-start | bytes 49160 | tf_op jit(solution)/shard_map/ppermute | solution.py:590
  65.3 5.5 %collective-permute-start.4 = (f32[4,8,128]{2,1,0:T(8,128)S(1)}, f32[4,8,128]{2,1,0:T(8,128)S(1)}, u32[]{:S(2)}, u32[]{:S(2)}) collective-permute-start(f32[4,8,128]{2,1,0:T(8,128)S(1)} %get-tuple-element.29), channel_id=1, source_target_pairs={{8,0},{16,8},{24,16},{32,24},{40,32},{48,40},{56,48},{64,56},{72,6... | collective-permute-start | bytes 49160 | tf_op jit(solution)/shard_map/ppermute | solution.py:595
  68.0 7.2 %collective-permute-start.9 = (f32[22,4,128]{2,1,0:T(4,128)S(1)}, f32[22,4,128]{2,1,0:T(4,128)S(1)}, u32[]{:S(2)}, u32[]{:S(2)}) collective-permute-start(f32[22,4,128]{2,1,0:T(4,128)S(1)} %get-tuple-element.26), channel_id=1, source_target_pairs={{0,8},{8,16},{16,24},{24,32},{32,40},{40,48},{48,56},{56,64},{64,7... | collective-permute-start | bytes 135176 | tf_op jit(solution)/shard_map/ppermute | solution.py:590
  68.1 7.0 %collective-permute-start.10 = (f32[22,4,128]{2,1,0:T(4,128)S(1)}, f32[22,4,128]{2,1,0:T(4,128)S(1)}, u32[]{:S(2)}, u32[]{:S(2)}) collective-permute-start(f32[22,4,128]{2,1,0:T(4,128)S(1)} %get-tuple-element.27), channel_id=1, source_target_pairs={{8,0},{16,8},{24,16},{32,24},{40,32},{48,40},{56,48},{64,56},{72,6... | collective-permute-start | bytes 135176 | tf_op jit(solution)/shard_map/ppermute | solution.py:595
  70.8 5.3 %collective-permute-start.5 = (f32[4,48,128]{2,1,0:T(8,128)S(1)}, f32[4,48,128]{2,1,0:T(8,128)S(1)}, u32[]{:S(2)}, u32[]{:S(2)}) collective-permute-start(f32[4,48,128]{2,1,0:T(8,128)S(1)} %pad_maximum_fusion.1.mine_ref), channel_id=1, source_target_pairs={{0,1},{1,0},{2,3},{3,2},{4,5},{5,4},{6,7},{7,6},{8,9},{9,8},{10,11... | collective-permute-start | bytes 294920 | tf_op jit(solution)/shard_map/ppermute | solution.py:599
  80.3 1.8 %collective-permute-start.11 = (f32[1,16]{1,0:T(1,128)S(1)}, f32[1,16]{1,0:T(1,128)S(1)}, u32[]{:S(2)}, u32[]{:S(2)}) collective-permute-start(f32[1,16]{1,0:T(1,128)S(1)} %get-tuple-element.21), channel_id=1, source_target_pairs={{0,1},{1,0},{2,3},{3,2},{4,5},{5,4},{6,7},{7,6},{8,9},{9,8},{10,11... | collective-permute-start | bytes 200 | tf_op jit(solution)/shard_map/ppermute | solution.py:599

commit v5 on v4

--- a/solution.py
+++ b/solution.py
@@ -34,7 +34,7 @@
 
 
 def front_kernel(
-    count_hbm, look_hbm, owner_hbm, patch_hbm, choice_hbm, observed_hbm, predicted_hbm, mask_hbm, weights_hbm,
+    size_y, count_hbm, look_hbm, owner_hbm, patch_hbm, choice_hbm, observed_hbm, predicted_hbm, mask_hbm, weights_hbm,
     out_ref, tally_ref,
     count_ref, look_ref, owner_ref, patch_ref, choice_ref,
     observed_ref, predicted_ref, mask_ref, weights_ref, coeffs_ref, sums_ref, used_ref, ids_ref, rank_ref, sems,
@@ -73,8 +73,12 @@
     for copy in first[:3]:
         copy.wait()
 
+    def target(b):
+        o = owner_ref[b]
+        return lax.rem(o, size_y) * (owners // size_y) + lax.div(o, size_y)
+
     for b in range(blocks):
-        o = owner_ref[b]
+        o = target(b)
         r = used_ref[o]
         used_ref[o] = r + 1
         rank_ref[b] = r
@@ -123,17 +127,17 @@
             total = jnp.where(choice == t + 1, product[:, lanes:], total)
     sums_ref[...] = total
     for b in range(blocks):
-        o, r = owner_ref[b], rank_ref[b]
+        o, r = target(b), rank_ref[b]
         for c in range(3):
             at = pl.multiple_of((r * 3 + c) * lanes, lanes)
             out_ref[o, :, pl.ds(at, lanes)] = sums_ref[c * blocks + b : c * blocks + b + 1, :]
 
 
-def front(count, look, owner, patch, choice, observed, predicted, mask, weights, owners):
+def front(count, look, owner, patch, choice, observed, predicted, mask, weights, owners, size_y):
     _, pixels, cells = weights.shape
     blocks = owner.shape[0]
     return pl.pallas_call(
-        front_kernel,
+        functools.partial(front_kernel, size_y),
         out_shape=(
             jax.ShapeDtypeStruct((owners, 1, (3 * CAP + 1) * cells), F32),
             jax.ShapeDtypeStruct((1, ROW), F32),
@@ -257,7 +261,7 @@
 
 def powers_kernel(
     sizes, layers, at_ref, depth_ref, beyond_ref, mine_ref, theirs_ref, stiff_ref,
-    tally_ref, surface_ref, one_ref, two_ref, three_ref, row_ref, flat, keep, diag, w1, w2, div1, div2, across1, across2,
+    tally_ref, zero_ref, one_ref, two_ref, three_ref, row_ref, flat, keep, diag, w1, w2, div1, div2, across1, across2,
 ):
     rows, local_x = stiff_ref.shape[1], one_ref.shape[2]
     size_x, size_y, size_z = sizes
@@ -291,7 +295,6 @@
 
     def tiles(c):
         own = mine_ref[c] + theirs_ref[c]
-        surface_ref[c] = own[EDGE : tall - EDGE]
         side = pltpu.roll(edges, LANES - EDGE - 2 * EDGE * c, 1)
         return jnp.where(outside_x, 0.0, own), jnp.where(outside_x | outside_y, 0.0, side)
 
@@ -423,7 +426,7 @@
             begin = d * flat[0, c, pl.ds(EDGE, local_x), :]
             once = w1[c, z + 1, 0, mid, :]
             factor = sign if c == 2 else None
-            for ref, value in ((one_ref, once), (two_ref, centre), (three_ref, third)):
+            for ref, value in ((zero_ref, begin), (one_ref, once), (two_ref, centre), (three_ref, third)):
                 ref[c, z_out] = value if factor is None else factor * value
             pairs = ((begin, begin), (begin, once), (once, once), (once, centre), (centre, centre), (centre, third))
             for k, (a, b) in enumerate(pairs):
@@ -463,7 +466,7 @@
     return pl.pallas_call(
         functools.partial(powers_kernel, sizes, layers),
         out_shape=(
-            jax.ShapeDtypeStruct((3, local_x, lanes), F32),
+            field,
             field,
             field,
             field,
@@ -532,14 +535,14 @@
 
 
 def finish_kernel(
-    depth_ref, got_ref, surface_ref, one_ref, two_ref, three_ref, field_out, resid_out, field_ref, resid_ref, sems
+    got_ref, zero_ref, one_ref, two_ref, three_ref, field_out, resid_out, field_ref, resid_ref, sems
 ):
     layers = one_ref.shape[1]
     totals = jnp.sum(got_ref[...], axis=0, keepdims=True)
     values = [totals[:, k : k + 1] for k in range(8)]
     found, resid = step_factors(values[:6])
     scale = lax.rsqrt(values[6] / (EPOCHS * values[7]) + EPS)
-    shape = surface_ref.shape[1:]
+    shape = one_ref.shape[2:]
     found = [jnp.broadcast_to(scale * v, shape) for v in found]
     resid = [jnp.broadcast_to(scale * v, shape) for v in resid]
     chunk = layers // 8
@@ -549,10 +552,8 @@
 
         def one_layer(k, carry, first=first):
             z = first + k
-            d = depth_ref[z]
             for c in range(3):
-                begin = d * surface_ref[c]
-                once, twice = one_ref[c, z], two_ref[c, z]
+                begin, once, twice = zero_ref[c, z], one_ref[c, z], two_ref[c, z]
                 field_ref[c, z] = found[0] * begin + found[1] * once + found[2] * twice
                 resid_ref[c, z] = resid[0] * begin + resid[1] * once + resid[2] * twice + resid[3] * three_ref[c, z]
             return carry
@@ -567,12 +568,12 @@
         copy.wait()
 
 
-def finish(depth, got, surface, one, two, three):
+def finish(got, zero, one, two, three):
     field = jax.ShapeDtypeStruct(one.shape, F32)
     return pl.pallas_call(
         finish_kernel,
         out_shape=(field, field),
-        in_specs=[SMEM] + [VMEM] * 5,
+        in_specs=[VMEM] * 5,
         out_specs=(ANY,) * 2,
         scratch_shapes=[
             pltpu.VMEM(one.shape, F32),
@@ -582,7 +583,7 @@
         compiler_params=pltpu.CompilerParams(vmem_limit_bytes=12 << 20),
         cost_estimate=pl.CostEstimate(flops=20_000_000, bytes_accessed=4 << 20, transcendentals=0),
         name="finish",
-    )(depth, got, surface, one, two, three)
+    )(got, zero, one, two, three)
 
 
 def from_below(value, axis):
@@ -625,10 +626,10 @@
 
     sums, tally = front(
         block_count, look_vector, block_owner[:, 0], block_patch, block_matrix_choice,
-        observed, predicted, coherence_mask, interp_weights, owners,
+        observed, predicted, coherence_mask, interp_weights, owners, sizes[1],
     )
     sums, stiffness, depth_kernel = lax.optimization_barrier((sums, stiffness, depth_kernel))
-    got = lax.all_to_all(sums, ("gx", "gy"), split_axis=0, concat_axis=0, tiled=True)
+    got = lax.all_to_all(sums, ("gy", "gx"), split_axis=0, concat_axis=0, tiled=True)
     depth_beyond = from_partner(depth_kernel, "gz")
     far = from_partner(jnp.where(upper, stiffness[:REACH], stiffness[layers - REACH :]), "gz")
     packed = pack(stiffness, far)
@@ -645,12 +646,12 @@
     mine = jnp.concatenate(
         [from_below(mine[:, local_x - EDGE :, :], "gx"), mine, from_above(mine[:, :EDGE, :], "gx")], axis=1
     )
-    surface, one, two, three, row = powers(
+    zero, one, two, three, row = powers(
         sizes, at, depth_kernel, depth_beyond, mine, from_partner(mine, "gz"), stiff, tally
     )
     rows = jnp.broadcast_to(row + from_partner(row, "gz"), (owners, ROW))
-    rows = lax.all_to_all(rows, ("gx", "gy"), split_axis=0, concat_axis=0, tiled=True)
-    return finish(depth_kernel, rows, surface, one, two, three)
+    rows = lax.all_to_all(rows, ("gy", "gx"), split_axis=0, concat_axis=0, tiled=True)
+    return finish(rows, zero, one, two, three)
 
 
 def solution(mesh):

time: 108 us -> 106 us (0.981)
    ppermute x4, starting transfers between devices: 10.5 us -> 5.92 us  [from_above(): lax.ppermute(value, axis, [((i + 1) % count, i) for i in range(count)])]
    ppermute x4, starting transfers between devices: 2.41 us -> 5.63 us  [from_below(): lax.ppermute(value, axis, [(i, (i + 1) % count) for i in range(count)])]
where the time goes in v5:
time: 106 us
  starting transfers between devices  48.5 us (46%)
  waiting for transfers between devices  22.9 us (22%)
  blocking collectives  22.4 us (21%)
  Pallas kernels  10.7 us (10%)
    all_to_all x1, starting transfers between devices, per_device(): lax.all_to_all(sums, ('gy', 'gx'), split_axis=0, concat_axis=0, tiled=True)  29.6 us
    all_to_all x1, blocking collectives, per_device(): lax.all_to_all(rows, ('gy', 'gx'), split_axis=0, concat_axis=0, tiled=True)  22.4 us
    all_to_all x1, waiting for transfers between devices, per_device(): lax.all_to_all(sums, ('gy', 'gx'), split_axis=0, concat_axis=0, tiled=True)  19 us
    ppermute x4, starting transfers between devices, from_partner(): return lax.ppermute(value, axis, [(0, 1), (1, 0)])  7.37 us
    ppermute x4, starting transfers between devices, from_above(): lax.ppermute(value, axis, [((i + 1) % count, i) for i in range(count)])  5.92 us
    ppermute x4, starting transfers between devices, from_below(): lax.ppermute(value, axis, [(i, (i + 1) % count) for i in range(count)])  5.63 us
    pallas_call x1, Pallas kernels, powers(): pl.pallas_call(functools.partial(powers_kernel, sizes, layers), out_shape...  4.26 us
    pallas_call x1, Pallas kernels, front(): pl.pallas_call(functools.partial(front_kernel, size_y), out_shape=(jax.Sh...  3.94 us
  transfers between devices with their start and end apart: 13, of which 5 were waited for; matrix products, arithmetic and copies ran while one was open for 0% of the time, Pallas kernels for 1%

profile of v5, /device:TPU:33, one launch (start us, length us, event | category | flops | bytes accessed | tf_op | source)
XLA Modules:
  0.0 105.6 jit_solution(5290990974377311930)
XLA Ops:
  0.6 0.0 copy-start
  0.6 0.0 copy-start.1
  0.7 3.9 %front.1 = (f32[64,1,1664]{2,1,0:T(1,128)}, f32[1,16]{1,0:T(1,128)}) custom-call(s32[64]{0:T(128)} %count_hbm.1, f32[4,3]{1,0:T(4,128)} %look_hbm.1, s32[64]{0:T(128)} %bitcast.12, s32[64]{0:T(128)} %patch_hbm.1, s32[64]{0:T(128)} %choice_hbm.1, f32[64,4,256]{2,1,0:T(4,128)} %observed_hbm.1, f32[64,4,256]{2,1,0:T(4,128)} %predicted_hbm.1, ...), custom_call_target="tpu_custom_call" | custom-call | flops 400000000 | bytes 4194304 | tf_op jit(solution)/shard_map/front/pallas_call | solution.py:139
  4.6 0.0 copy-start.2
  4.6 29.6 %all-to-all-start = ((f32[64,1,1664]{2,1,0:T(1,128)}), f32[64,1,1664]{2,1,0:T(1,128)S(1)}, u32[]{:S(2)}, u32[]{:S(2)}) async-start(f32[64,1,1664]{2,1,0:T(1,128)} %get-tuple-element.16), calls=%async_computation | async-start | bytes 851968 | tf_op jit(solution)/shard_map/all_to_all | solution.py:632
  34.2 0.0 copy-done.1
  34.2 1.0 collective-permute-start
  35.2 0.0 copy-done
  35.2 0.2 collective-permute-start.6
  35.4 1.2 %collective-permute-done.6.far_ref = f32[4,32,128]{2,1,0:T(8,128)S(1)} collective-permute-done((f32[4,32,128]{2,1,0:T(8,128)S(1)}, f32[4,32,128]{2,1,0:T(8,128)S(1)}, u32[]{:S(2)}, u32[]{:S(2)}) %collective-permute-start.6) | collective-permute-done | bytes 65568 | tf_op jit(solution)/shard_map/ppermute | solution.py:600
  36.6 0.1 pack.1
  36.8 0.5 collective-permute-start.8
  37.3 2.2 %collective-permute-start.7 = (f32[2,32,128]{2,1,0:T(8,128)S(1)}, f32[2,32,128]{2,1,0:T(8,128)S(1)}, u32[]{:S(2)}, u32[]{:S(2)}) collective-permute-start(f32[2,32,128]{2,1,0:T(8,128)S(1)} %pack.1), channel_id=1, source_target_pairs={{2,0},{4,2},{6,4},{0,6},{3,1},{5,3},{7,5},{1,7},{10,8},{12,10},{14... | collective-permute-start | bytes 98312 | tf_op jit(solution)/shard_map/ppermute | solution.py:596
  39.6 19.0 %all-to-all-done = f32[64,1,1664]{2,1,0:T(1,128)S(1)} async-done(((f32[64,1,1664]{2,1,0:T(1,128)}), f32[64,1,1664]{2,1,0:T(1,128)S(1)}, u32[]{:S(2)}, u32[]{:S(2)}) %all-to-all-start) | async-done | bytes 426016 | tf_op jit(solution)/shard_map/all_to_all | solution.py:632
  58.6 0.8 place.1
  59.3 1.2 %collective-permute-start.2 = (f32[32,128]{1,0:T(8,128)S(1)}, f32[32,128]{1,0:T(8,128)S(1)}, u32[]{:S(2)}, u32[]{:S(2)}) collective-permute-start(f32[32,128]{1,0:T(8,128)S(1)} %get-tuple-element.18), channel_id=1, source_target_pairs={{0,2},{2,4},{4,6},{6,0},{1,3},{3,5},{5,7},{7,1},{8,10},{10,12},{12... | collective-permute-start | bytes 49160 | tf_op jit(solution)/shard_map/ppermute | solution.py:591
  60.6 2.0 %collective-permute-start.1 = (f32[32,128]{1,0:T(8,128)S(1)}, f32[32,128]{1,0:T(8,128)S(1)}, u32[]{:S(2)}, u32[]{:S(2)}) collective-permute-start(f32[32,128]{1,0:T(8,128)S(1)} %get-tuple-element.18), channel_id=1, source_target_pairs={{2,0},{4,2},{6,4},{0,6},{3,1},{5,3},{7,5},{1,7},{10,8},{12,10},{14... | collective-permute-start | bytes 49160 | tf_op jit(solution)/shard_map/ppermute | solution.py:596
  62.5 0.0 collective-permute-done.8
  62.5 0.0 collective-permute-done.7
  62.5 1.0 collective-permute-done.2
  63.5 0.0 collective-permute-done.1
  63.6 2.5 %collective-permute-start.3 = (f32[4,8,128]{2,1,0:T(8,128)S(1)}, f32[4,8,128]{2,1,0:T(8,128)S(1)}, u32[]{:S(2)}, u32[]{:S(2)}) collective-permute-start(f32[4,8,128]{2,1,0:T(8,128)S(1)} %get-tuple-element.28), channel_id=1, source_target_pairs={{0,8},{8,16},{16,24},{24,32},{32,40},{40,48},{48,56},{56,64},{64,7... | collective-permute-start | bytes 49160 | tf_op jit(solution)/shard_map/ppermute | solution.py:591
  66.1 0.3 collective-permute-start.4
  66.4 1.3 %collective-permute-start.9 = (f32[22,4,128]{2,1,0:T(4,128)S(1)}, f32[22,4,128]{2,1,0:T(4,128)S(1)}, u32[]{:S(2)}, u32[]{:S(2)}) collective-permute-start(f32[22,4,128]{2,1,0:T(4,128)S(1)} %get-tuple-element.26), channel_id=1, source_target_pairs={{0,8},{8,16},{16,24},{24,32},{32,40},{40,48},{48,56},{56,64},{64,7... | collective-permute-start | bytes 135176 | tf_op jit(solution)/shard_map/ppermute | solution.py:591
  67.7 1.5 %collective-permute-start.10 = (f32[22,4,128]{2,1,0:T(4,128)S(1)}, f32[22,4,128]{2,1,0:T(4,128)S(1)}, u32[]{:S(2)}, u32[]{:S(2)}) collective-permute-start(f32[22,4,128]{2,1,0:T(4,128)S(1)} %get-tuple-element.27), channel_id=1, source_target_pairs={{8,0},{16,8},{24,16},{32,24},{40,32},{48,40},{56,48},{64,56},{72,6... | collective-permute-start | bytes 135176 | tf_op jit(solution)/shard_map/ppermute | solution.py:596
  69.2 0.0 collective-permute-done.3
  69.2 0.0 collective-permute-done.4
  69.2 5.0 %collective-permute-start.5 = (f32[4,48,128]{2,1,0:T(8,128)S(1)}, f32[4,48,128]{2,1,0:T(8,128)S(1)}, u32[]{:S(2)}, u32[]{:S(2)}) collective-permute-start(f32[4,48,128]{2,1,0:T(8,128)S(1)} %pad_maximum_fusion.1.mine_ref), channel_id=1, source_target_pairs={{0,1},{1,0},{2,3},{3,2},{4,5},{5,4},{6,7},{7,6},{8,9},{9,8},{10,11... | collective-permute-start | bytes 294920 | tf_op jit(solution)/shard_map/ppermute | solution.py:600
  74.2 0.0 collective-permute-done.9
  74.2 0.0 collective-permute-done.10
  74.2 0.1 pad_maximum_fusion.stiff_ref
  74.3 0.0 collective-permute-done.beyond_ref
  74.3 0.9 collective-permute-done.5.theirs_ref
  75.1 0.0 copy-done.2
  75.1 4.3 %powers.1 = (f32[3,16,32,128]{3,2,1,0:T(8,128)S(1)}, f32[3,16,32,128]{3,2,1,0:T(8,128)S(1)}, f32[3,16,32,128]{3,2,1,0:T(8,128)S(1)}, f32[3,16,32,128]{3,2,1,0:T(8,128)S(1)}, f32[1,16]{1,0:T(1,128)S(1)}) custom-call(s32[1]{0:T(128)} %bitcast.at_ref, f32[16]{0:T(128)S(1)} %copy-done.1, f32[16]{0:T(128)S(1)} %collective-permute-done.beyond_ref, ...), custom_call_target="tpu_custom_call" | custom-call | flops 100000000 | bytes 4194304 | tf_op jit(solution)/shard_map/powers/pallas_call | solution.py:466
  79.4 1.2 %collective-permute-start.11 = (f32[1,16]{1,0:T(1,128)S(1)}, f32[1,16]{1,0:T(1,128)S(1)}, u32[]{:S(2)}, u32[]{:S(2)}) collective-permute-start(f32[1,16]{1,0:T(1,128)S(1)} %get-tuple-element.21), channel_id=1, source_target_pairs={{0,1},{1,0},{2,3},{3,2},{4,5},{5,4},{6,7},{7,6},{8,9},{9,8},{10,11... | collective-permute-start | bytes 200 | tf_op jit(solution)/shard_map/ppermute | solution.py:600
  80.6 0.8 collective-permute-done.11
  81.4 22.4 %all_to_all.13 = f32[64,1,16]{2,1,0:T(1,128)S(1)} all-to-all(f32[64,1,16]{2,1,0:T(1,128)S(1)} %broadcast_in_dim.9), channel_id=1, replica_groups=mesh['grp'=2,'gx'=16,'gy'=4,'gz'=2] {'gy','gx'}, dimensions={0} | all-to-all | bytes 8192 | tf_op jit(solution)/shard_map/all_to_all | solution.py:653
  103.8 1.6 %finish.1 = (f32[3,16,32,128]{3,2,1,0:T(8,128)}, f32[3,16,32,128]{3,2,1,0:T(8,128)}) custom-call(f32[64,16]{1,0:T(8,128)S(1)} %bitcast.11, f32[3,16,32,128]{3,2,1,0:T(8,128)S(1)} %get-tuple-element.22.zero_ref, f32[3,16,32,128]{3,2,1,0:T(8,128)S(1)} %get-tuple-element.23.one_ref, f32[3,16,32,128]{3,2,1,0:T(8,128)S(1)} %get-tuple-element.24.two_ref, ...), custom_call_target="tpu_custom_call" | custom-call | flops 20000000 | bytes 4194304 | tf_op jit(solution)/shard_map/finish/pallas_call | solution.py:573
  (13 shorter events, 0.1 us)
Async XLA Ops:
  0.6 34.6 %copy-start = (f32[16,32,128]{2,1,0:T(8,128)S(1)}, f32[16,32,128]{2,1,0:T(8,128)}, u32[]{:S(2)}) copy-start(f32[16,32,128]{2,1,0:T(8,128)} %own_ref) | copy-start | bytes 786436
  0.6 33.6 %copy-start.1 = (f32[16]{0:T(128)S(1)}, f32[16]{0:T(128)}, u32[]{:S(2)}) copy-start(f32[16]{0:T(128)} %depth_ref) | copy-start | bytes 196
  4.6 70.6 %copy-start.2 = (f32[1,16]{1,0:T(1,128)S(1)}, f32[1,16]{1,0:T(1,128)}, u32[]{:S(2)}) copy-start(f32[1,16]{1,0:T(1,128)} %get-tuple-element.20.tally_ref) | copy-start | bytes 196
  4.6 53.9 %all-to-all-start = ((f32[64,1,1664]{2,1,0:T(1,128)}), f32[64,1,1664]{2,1,0:T(1,128)S(1)}, u32[]{:S(2)}, u32[]{:S(2)}) async-start(f32[64,1,1664]{2,1,0:T(1,128)} %get-tuple-element.16), calls=%async_computation | async-start | bytes 851968 | tf_op jit(solution)/shard_map/all_to_all | solution.py:632
  34.2 40.1 %collective-permute-start = (f32[16]{0:T(128)S(1)}, f32[16]{0:T(128)S(1)}, u32[]{:S(2)}, u32[]{:S(2)}) collective-permute-start(f32[16]{0:T(128)S(1)} %copy-done.1), channel_id=1, source_target_pairs={{0,1},{1,0},{2,3},{3,2},{4,5},{5,4},{6,7},{7,6},{8,9},{9,8},{10,11... | collective-permute-start | bytes 200 | tf_op jit(solution)/shard_map/ppermute | solution.py:600
  35.2 1.4 %collective-permute-start.6 = (f32[4,32,128]{2,1,0:T(8,128)S(1)}, f32[4,32,128]{2,1,0:T(8,128)S(1)}, u32[]{:S(2)}, u32[]{:S(2)}) collective-permute-start(f32[4,32,128]{2,1,0:T(8,128)S(1)} %slice_select_fusion), channel_id=1, source_target_pairs={{0,1},{1,0},{2,3},{3,2},{4,5},{5,4},{6,7},{7,6},{8,9},{9,8},{10,11... | collective-permute-start | bytes 196616 | tf_op jit(solution)/shard_map/ppermute | solution.py:600
  36.8 25.8 %collective-permute-start.8 = (f32[2,32,128]{2,1,0:T(8,128)S(1)}, f32[2,32,128]{2,1,0:T(8,128)S(1)}, u32[]{:S(2)}, u32[]{:S(2)}) collective-permute-start(f32[2,32,128]{2,1,0:T(8,128)S(1)} %pack.1), channel_id=1, source_target_pairs={{0,2},{2,4},{4,6},{6,0},{1,3},{3,5},{5,7},{7,1},{8,10},{10,12},{12... | collective-permute-start | bytes 98312 | tf_op jit(solution)/shard_map/ppermute | solution.py:591
  37.3 25.2 %collective-permute-start.7 = (f32[2,32,128]{2,1,0:T(8,128)S(1)}, f32[2,32,128]{2,1,0:T(8,128)S(1)}, u32[]{:S(2)}, u32[]{:S(2)}) collective-permute-start(f32[2,32,128]{2,1,0:T(8,128)S(1)} %pack.1), channel_id=1, source_target_pairs={{2,0},{4,2},{6,4},{0,6},{3,1},{5,3},{7,5},{1,7},{10,8},{12,10},{14... | collective-permute-start | bytes 98312 | tf_op jit(solution)/shard_map/ppermute | solution.py:596
  59.3 4.2 %collective-permute-start.2 = (f32[32,128]{1,0:T(8,128)S(1)}, f32[32,128]{1,0:T(8,128)S(1)}, u32[]{:S(2)}, u32[]{:S(2)}) collective-permute-start(f32[32,128]{1,0:T(8,128)S(1)} %get-tuple-element.18), channel_id=1, source_target_pairs={{0,2},{2,4},{4,6},{6,0},{1,3},{3,5},{5,7},{7,1},{8,10},{10,12},{12... | collective-permute-start | bytes 49160 | tf_op jit(solution)/shard_map/ppermute | solution.py:591
  60.6 3.0 %collective-permute-start.1 = (f32[32,128]{1,0:T(8,128)S(1)}, f32[32,128]{1,0:T(8,128)S(1)}, u32[]{:S(2)}, u32[]{:S(2)}) collective-permute-start(f32[32,128]{1,0:T(8,128)S(1)} %get-tuple-element.18), channel_id=1, source_target_pairs={{2,0},{4,2},{6,4},{0,6},{3,1},{5,3},{7,5},{1,7},{10,8},{12,10},{14... | collective-permute-start | bytes 49160 | tf_op jit(solution)/shard_map/ppermute | solution.py:596
  63.6 5.6 %collective-permute-start.3 = (f32[4,8,128]{2,1,0:T(8,128)S(1)}, f32[4,8,128]{2,1,0:T(8,128)S(1)}, u32[]{:S(2)}, u32[]{:S(2)}) collective-permute-start(f32[4,8,128]{2,1,0:T(8,128)S(1)} %get-tuple-element.28), channel_id=1, source_target_pairs={{0,8},{8,16},{16,24},{24,32},{32,40},{40,48},{48,56},{56,64},{64,7... | collective-permute-start | bytes 49160 | tf_op jit(solution)/shard_map/ppermute | solution.py:591
  66.1 3.1 %collective-permute-start.4 = (f32[4,8,128]{2,1,0:T(8,128)S(1)}, f32[4,8,128]{2,1,0:T(8,128)S(1)}, u32[]{:S(2)}, u32[]{:S(2)}) collective-permute-start(f32[4,8,128]{2,1,0:T(8,128)S(1)} %get-tuple-element.29), channel_id=1, source_target_pairs={{8,0},{16,8},{24,16},{32,24},{40,32},{48,40},{56,48},{64,56},{72,6... | collective-permute-start | bytes 49160 | tf_op jit(solution)/shard_map/ppermute | solution.py:596
  66.4 7.8 %collective-permute-start.9 = (f32[22,4,128]{2,1,0:T(4,128)S(1)}, f32[22,4,128]{2,1,0:T(4,128)S(1)}, u32[]{:S(2)}, u32[]{:S(2)}) collective-permute-start(f32[22,4,128]{2,1,0:T(4,128)S(1)} %get-tuple-element.26), channel_id=1, source_target_pairs={{0,8},{8,16},{16,24},{24,32},{32,40},{40,48},{48,56},{56,64},{64,7... | collective-permute-start | bytes 135176 | tf_op jit(solution)/shard_map/ppermute | solution.py:591
  67.7 6.5 %collective-permute-start.10 = (f32[22,4,128]{2,1,0:T(4,128)S(1)}, f32[22,4,128]{2,1,0:T(4,128)S(1)}, u32[]{:S(2)}, u32[]{:S(2)}) collective-permute-start(f32[22,4,128]{2,1,0:T(4,128)S(1)} %get-tuple-element.27), channel_id=1, source_target_pairs={{8,0},{16,8},{24,16},{32,24},{40,32},{48,40},{56,48},{64,56},{72,6... | collective-permute-start | bytes 135176 | tf_op jit(solution)/shard_map/ppermute | solution.py:596
  69.2 6.0 %collective-permute-start.5 = (f32[4,48,128]{2,1,0:T(8,128)S(1)}, f32[4,48,128]{2,1,0:T(8,128)S(1)}, u32[]{:S(2)}, u32[]{:S(2)}) collective-permute-start(f32[4,48,128]{2,1,0:T(8,128)S(1)} %pad_maximum_fusion.1.mine_ref), channel_id=1, source_target_pairs={{0,1},{1,0},{2,3},{3,2},{4,5},{5,4},{6,7},{7,6},{8,9},{9,8},{10,11... | collective-permute-start | bytes 294920 | tf_op jit(solution)/shard_map/ppermute | solution.py:600
  79.4 2.0 %collective-permute-start.11 = (f32[1,16]{1,0:T(1,128)S(1)}, f32[1,16]{1,0:T(1,128)S(1)}, u32[]{:S(2)}, u32[]{:S(2)}) collective-permute-start(f32[1,16]{1,0:T(1,128)S(1)} %get-tuple-element.21), channel_id=1, source_target_pairs={{0,1},{1,0},{2,3},{3,2},{4,5},{5,4},{6,7},{7,6},{8,9},{9,8},{10,11... | collective-permute-start | bytes 200 | tf_op jit(solution)/shard_map/ppermute | solution.py:600

commit v6 on v5

--- a/solution.py
+++ b/solution.py
@@ -75,13 +75,18 @@
 
     def target(b):
         o = owner_ref[b]
-        return lax.rem(o, size_y) * (owners // size_y) + lax.div(o, size_y)
+        if size_y & (size_y - 1):
+            x, y = lax.div(o, size_y), lax.rem(o, size_y)
+        else:
+            x, y = lax.shift_right_logical(o, size_y.bit_length() - 1), o & (size_y - 1)
+        return y * (owners // size_y) + x
 
     for b in range(blocks):
         o = target(b)
         r = used_ref[o]
         used_ref[o] = r + 1
         rank_ref[b] = r
+        owner_ref[b] = o
         ids_ref[o * CAP + r] = patch_ref[b]
     spot = lax.broadcasted_iota(jnp.int32, (1, lanes), 1)
     for o in range(owners):
@@ -127,7 +132,7 @@
             total = jnp.where(choice == t + 1, product[:, lanes:], total)
     sums_ref[...] = total
     for b in range(blocks):
-        o, r = target(b), rank_ref[b]
+        o, r = owner_ref[b], rank_ref[b]
         for c in range(3):
             at = pl.multiple_of((r * 3 + c) * lanes, lanes)
             out_ref[o, :, pl.ds(at, lanes)] = sums_ref[c * blocks + b : c * blocks + b + 1, :]
@@ -260,43 +265,21 @@
 
 
 def powers_kernel(
-    sizes, layers, at_ref, depth_ref, beyond_ref, mine_ref, theirs_ref, stiff_ref,
-    tally_ref, zero_ref, one_ref, two_ref, three_ref, row_ref, flat, keep, diag, w1, w2, div1, div2, across1, across2,
+    layers, scalars_hbm, guide_ref, mine_ref, theirs_ref, stiff_ref,
+    tally_ref, zero_ref, one_ref, two_ref, three_ref, row_ref, scalars, sem, flat, keep, diag, w1, w2, div1, div2, across1, across2,
 ):
     rows, local_x = stiff_ref.shape[1], one_ref.shape[2]
-    size_x, size_y, size_z = sizes
-    at = at_ref[0]
-    at_z = lax.rem(at, size_z)
-    at_y = lax.rem(lax.div(at, size_z), size_y)
-    at_x = lax.div(at, size_z * size_y)
-    upper = at_z == 1
-    sign = jnp.where(upper, -1.0, 1.0).astype(F32)
     tall = mine_ref.shape[1]
-
-    def layer_of(z):
-        return jnp.where(upper, layers - 1 - z, z)
-
-    depths = [depth_ref[layer_of(z)] for z in range(layers)]
-    depths += [beyond_ref[layer_of(z)] for z in range(REACH + 2)]
-
-    def depth(z):
-        return depths[z] if z >= 0 else jnp.zeros((), F32)
-
-    lane = lax.broadcasted_iota(jnp.int32, (tall, LANES), 1)
-    line = lax.broadcasted_iota(jnp.int32, (tall, LANES), 0)
-    outside_x = ((line < EDGE) & (at_x == 0)) | ((line >= tall - EDGE) & (at_x == size_x - 1))
-    half = lane < LANES // 2
-    outside_y = (half & (at_y == size_y - 1)) | (jnp.logical_not(half) & (at_y == 0))
-    in0 = jnp.where(outside_x, 0.0, 1.0)
-    in1 = jnp.where(outside_x | outside_y, 0.0, 1.0)
-    inside = (in0, in1)
-
+    copy = pltpu.make_async_copy(scalars_hbm, scalars, sem)
+    copy.start()
+
+    inside = (guide_ref[0], guide_ref[1])
     edges = mine_ref[3] + theirs_ref[3]
 
     def tiles(c):
         own = mine_ref[c] + theirs_ref[c]
         side = pltpu.roll(edges, LANES - EDGE - 2 * EDGE * c, 1)
-        return jnp.where(outside_x, 0.0, own), jnp.where(outside_x | outside_y, 0.0, side)
+        return inside[0] * own, inside[1] * side
 
     def down(v):
         return pltpu.roll(v, tall - 1, 0)
@@ -304,7 +287,7 @@
     def up(v):
         return pltpu.roll(v, 1, 0)
 
-    s = [tiles(0), tiles(1), tuple(sign * v for v in tiles(2))]
+    s = [tiles(0), tiles(1), tuple(guide_ref[2] * v for v in tiles(2))]
     moved = [lane_steps(*v) for v in s]
     grad = tuple(
         inside[t] * 0.5 * (down(s[0][t]) - up(s[0][t]) + moved[1][0][t] - moved[1][1][t]) for t in range(2)
@@ -321,6 +304,19 @@
         flat[t, 6] = inside[t] * (-0.25) * (down(s[2][t]) - up(s[2][t]))
         flat[t, 7] = inside[t] * (-0.25) * (moved[2][0][t] - moved[2][1][t])
         flat[t, 8] = inside[t] * (-0.5) * grad[t]
+
+    copy.wait()
+    upper = scalars[2 * layers] > 0.5
+    sign = jnp.where(upper, -1.0, 1.0).astype(F32)
+
+    def layer_of(z):
+        return jnp.where(upper, layers - 1 - z, z)
+
+    depths = [scalars[layer_of(z)] for z in range(layers)]
+    depths += [scalars[layers + layer_of(z)] for z in range(REACH + 2)]
+
+    def depth(z):
+        return depths[z] if z >= 0 else jnp.zeros((), F32)
 
     first = EDGE - REACH
     body = pl.ds(EDGE, rows)
@@ -456,15 +452,14 @@
     row_ref[...] = row
 
 
-def powers(sizes, at, depth, beyond, mine, theirs, stiff, tally):
-    layers = depth.shape[0]
+def powers(layers, scalars, guide, mine, theirs, stiff, tally):
     _, rows, lanes = stiff.shape
     tall = mine.shape[1]
     local_x = tall - 2 * EDGE
     field = jax.ShapeDtypeStruct((3, layers, local_x, lanes), F32)
     deep = rows + 2 * EDGE
     return pl.pallas_call(
-        functools.partial(powers_kernel, sizes, layers),
+        functools.partial(powers_kernel, layers),
         out_shape=(
             field,
             field,
@@ -472,9 +467,11 @@
             field,
             jax.ShapeDtypeStruct((1, ROW), F32),
         ),
-        in_specs=[SMEM] * 3 + [VMEM] * 4,
+        in_specs=[ANY] + [VMEM] * 5,
         out_specs=(VMEM,) * 5,
         scratch_shapes=[
+            pltpu.SMEM(scalars.shape, F32),
+            pltpu.SemaphoreType.DMA,
             pltpu.VMEM((2, 9, tall, lanes), F32),
             pltpu.VMEM((2, tall, lanes), F32),
             pltpu.VMEM((layers + REACH, 2, rows, lanes), F32),
@@ -488,7 +485,7 @@
         compiler_params=pltpu.CompilerParams(vmem_limit_bytes=20 << 20),
         cost_estimate=pl.CostEstimate(flops=100_000_000, bytes_accessed=4 << 20, transcendentals=0),
         name="powers",
-    )(at, depth, beyond, mine, theirs, stiff, tally)
+    )(scalars, guide, mine, theirs, stiff, tally)
 
 
 def step_factors(nu):
@@ -621,7 +618,7 @@
     layers, local_x, local_y = stiffness.shape
     sizes = tuple(lax.axis_size(a) for a in ("gx", "gy", "gz"))
     owners = sizes[0] * sizes[1]
-    at = lax.axis_index(("gx", "gy", "gz")).astype(jnp.int32).reshape(1)
+    gx, gy = lax.axis_index("gx"), lax.axis_index("gy")
     upper = lax.axis_index("gz") == 1
 
     sums, tally = front(
@@ -640,6 +637,14 @@
     above = from_above(low, "gx")
     stiff = jnp.concatenate([below, stiff, above], axis=1)
 
+    scalars = jnp.concatenate([depth_kernel, depth_beyond, upper.astype(F32)[None]])
+    shape = (local_x + 2 * EDGE, local_y)
+    line, lane = (lax.broadcasted_iota(jnp.int32, shape, k) for k in range(2))
+    in_x = ((line >= EDGE) | (gx > 0)) & ((line < shape[0] - EDGE) | (gx < sizes[0] - 1))
+    in_y = jnp.where(lane < LANES // 2, gy < sizes[1] - 1, gy > 0)
+    sign = jnp.broadcast_to(jnp.where(upper, -1.0, 1.0), shape)
+    guide = jnp.stack([in_x.astype(F32), (in_x & in_y).astype(F32), sign.astype(F32)])
+
     part, edges = place(got[:, 0], local_x, local_y)
     side = beside(from_below(edges, "gy"), from_above(edges, "gy"), EDGE)
     mine = jnp.concatenate([part, side[None]])
@@ -647,7 +652,7 @@
         [from_below(mine[:, local_x - EDGE :, :], "gx"), mine, from_above(mine[:, :EDGE, :], "gx")], axis=1
     )
     zero, one, two, three, row = powers(
-        sizes, at, depth_kernel, depth_beyond, mine, from_partner(mine, "gz"), stiff, tally
+        layers, scalars, guide, mine, from_partner(mine, "gz"), stiff, tally
     )
     rows = jnp.broadcast_to(row + from_partner(row, "gz"), (owners, ROW))
     rows = lax.all_to_all(rows, ("gy", "gx"), split_axis=0, concat_axis=0, tiled=True)

time: 106 us -> 106 us (level)
  transfers between devices with their start and end apart: 13 -> 13, of which waited for: 5 -> 5; matrix products, arithmetic and copies ran while one was open for 0% -> 1% of each run, Pallas kernels for 1% -> 1%
where the time goes in v6:
time: 106 us; the launch traced here: 105 us
  starting transfers between devices  48.5 us (46%)
  waiting for transfers between devices  22.4 us (21%)
  blocking collectives  22.4 us (21%)
  Pallas kernels  10.3 us (10%)
    all_to_all x1, starting transfers between devices, per_device(): lax.all_to_all(sums, ('gy', 'gx'), split_axis=0, concat_axis=0, tiled=True)  29.6 us
    all_to_all x1, blocking collectives, per_device(): lax.all_to_all(rows, ('gy', 'gx'), split_axis=0, concat_axis=0, tiled=True)  22.4 us
    all_to_all x1, waiting for transfers between devices, per_device(): lax.all_to_all(sums, ('gy', 'gx'), split_axis=0, concat_axis=0, tiled=True)  18.9 us
    ppermute x4, starting transfers between devices, from_partner(): return lax.ppermute(value, axis, [(0, 1), (1, 0)])  7.36 us
    ppermute x4, starting transfers between devices, from_above(): lax.ppermute(value, axis, [((i + 1) % count, i) for i in range(count)])  5.92 us
    ppermute x4, starting transfers between devices, from_below(): lax.ppermute(value, axis, [(i, (i + 1) % count) for i in range(count)])  5.63 us
    pallas_call x1, Pallas kernels, powers(): pl.pallas_call(functools.partial(powers_kernel, layers), out_shape=(field...  4.06 us
    pallas_call x1, Pallas kernels, front(): pl.pallas_call(functools.partial(front_kernel, size_y), out_shape=(jax.Sh...  3.68 us
  transfers between devices with their start and end apart: 13, of which 5 were waited for; matrix products, arithmetic and copies ran while one was open for 1% of the time, Pallas kernels for 1%

profile of v6, /device:TPU:33, one launch (start us, length us, event | category | flops | bytes accessed | tf_op | source)
XLA Modules:
  0.0 105.2 jit_solution(7032551742456017126)
XLA Ops:
  0.6 0.0 copy-start
  0.6 0.0 copy-start.2
  0.7 3.7 %front.1 = (f32[64,1,1664]{2,1,0:T(1,128)}, f32[1,16]{1,0:T(1,128)}) custom-call(s32[64]{0:T(128)} %count_hbm.1, f32[4,3]{1,0:T(4,128)} %look_hbm.1, s32[64]{0:T(128)} %bitcast.13, s32[64]{0:T(128)} %patch_hbm.1, s32[64]{0:T(128)} %choice_hbm.1, f32[64,4,256]{2,1,0:T(4,128)} %observed_hbm.1, f32[64,4,256]{2,1,0:T(4,128)} %predicted_hbm.1, ...), custom_call_target="tpu_custom_call" | custom-call | flops 400000000 | bytes 4194304 | tf_op jit(solution)/shard_map/front/pallas_call | solution.py:144
  4.3 29.6 %all-to-all-start = ((f32[64,1,1664]{2,1,0:T(1,128)}), f32[64,1,1664]{2,1,0:T(1,128)S(1)}, u32[]{:S(2)}, u32[]{:S(2)}) async-start(f32[64,1,1664]{2,1,0:T(1,128)} %get-tuple-element.16), calls=%async_computation | async-start | bytes 851968 | tf_op jit(solution)/shard_map/all_to_all | solution.py:629
  33.9 0.0 copy-done.2
  34.0 0.0 copy-start.1
  34.0 1.0 collective-permute-start
  35.0 0.0 copy-done
  35.0 0.2 collective-permute-start.6
  35.2 0.1 pad.16.clone
  35.3 0.1 and_convert_fusion
  35.3 0.1 iota.38
  35.4 0.1 maximum_maximum_fusion.guide_ref
  35.5 0.9 collective-permute-done.6.far_ref
  36.4 0.1 pack.1
  36.5 0.5 collective-permute-start.8
  37.1 2.2 %collective-permute-start.7 = (f32[2,32,128]{2,1,0:T(8,128)S(1)}, f32[2,32,128]{2,1,0:T(8,128)S(1)}, u32[]{:S(2)}, u32[]{:S(2)}) collective-permute-start(f32[2,32,128]{2,1,0:T(8,128)S(1)} %pack.1), channel_id=1, source_target_pairs={{2,0},{4,2},{6,4},{0,6},{3,1},{5,3},{7,5},{1,7},{10,8},{12,10},{14... | collective-permute-start | bytes 98312 | tf_op jit(solution)/shard_map/ppermute | solution.py:593
  39.3 0.0 collective-permute-done
  39.3 0.1 pad_maximum_fusion.7.scalars_hbm
  39.4 18.9 %all-to-all-done = f32[64,1,1664]{2,1,0:T(1,128)S(1)} async-done(((f32[64,1,1664]{2,1,0:T(1,128)}), f32[64,1,1664]{2,1,0:T(1,128)S(1)}, u32[]{:S(2)}, u32[]{:S(2)}) %all-to-all-start) | async-done | bytes 426016 | tf_op jit(solution)/shard_map/all_to_all | solution.py:629
  58.3 0.8 place.1
  59.1 1.2 %collective-permute-start.2 = (f32[32,128]{1,0:T(8,128)S(1)}, f32[32,128]{1,0:T(8,128)S(1)}, u32[]{:S(2)}, u32[]{:S(2)}) collective-permute-start(f32[32,128]{1,0:T(8,128)S(1)} %get-tuple-element.18), channel_id=1, source_target_pairs={{0,2},{2,4},{4,6},{6,0},{1,3},{3,5},{5,7},{7,1},{8,10},{10,12},{12... | collective-permute-start | bytes 49160 | tf_op jit(solution)/shard_map/ppermute | solution.py:588
  60.3 2.0 %collective-permute-start.1 = (f32[32,128]{1,0:T(8,128)S(1)}, f32[32,128]{1,0:T(8,128)S(1)}, u32[]{:S(2)}, u32[]{:S(2)}) collective-permute-start(f32[32,128]{1,0:T(8,128)S(1)} %get-tuple-element.18), channel_id=1, source_target_pairs={{2,0},{4,2},{6,4},{0,6},{3,1},{5,3},{7,5},{1,7},{10,8},{12,10},{14... | collective-permute-start | bytes 49160 | tf_op jit(solution)/shard_map/ppermute | solution.py:593
  62.3 0.0 collective-permute-done.8
  62.3 0.0 collective-permute-done.7
  62.3 1.0 collective-permute-done.2
  63.3 0.0 collective-permute-done.1
  63.3 2.5 %collective-permute-start.3 = (f32[4,8,128]{2,1,0:T(8,128)S(1)}, f32[4,8,128]{2,1,0:T(8,128)S(1)}, u32[]{:S(2)}, u32[]{:S(2)}) collective-permute-start(f32[4,8,128]{2,1,0:T(8,128)S(1)} %get-tuple-element.30), channel_id=1, source_target_pairs={{0,8},{8,16},{16,24},{24,32},{32,40},{40,48},{48,56},{56,64},{64,7... | collective-permute-start | bytes 49160 | tf_op jit(solution)/shard_map/ppermute | solution.py:588
  65.8 0.3 collective-permute-start.4
  66.1 1.3 %collective-permute-start.9 = (f32[22,4,128]{2,1,0:T(4,128)S(1)}, f32[22,4,128]{2,1,0:T(4,128)S(1)}, u32[]{:S(2)}, u32[]{:S(2)}) collective-permute-start(f32[22,4,128]{2,1,0:T(4,128)S(1)} %get-tuple-element.28), channel_id=1, source_target_pairs={{0,8},{8,16},{16,24},{24,32},{32,40},{40,48},{48,56},{56,64},{64,7... | collective-permute-start | bytes 135176 | tf_op jit(solution)/shard_map/ppermute | solution.py:588
  67.4 1.5 %collective-permute-start.10 = (f32[22,4,128]{2,1,0:T(4,128)S(1)}, f32[22,4,128]{2,1,0:T(4,128)S(1)}, u32[]{:S(2)}, u32[]{:S(2)}) collective-permute-start(f32[22,4,128]{2,1,0:T(4,128)S(1)} %get-tuple-element.29), channel_id=1, source_target_pairs={{8,0},{16,8},{24,16},{32,24},{40,32},{48,40},{56,48},{64,56},{72,6... | collective-permute-start | bytes 135176 | tf_op jit(solution)/shard_map/ppermute | solution.py:593
  68.9 0.0 collective-permute-done.3
  68.9 0.0 collective-permute-done.4
  68.9 5.0 %collective-permute-start.5 = (f32[4,48,128]{2,1,0:T(8,128)S(1)}, f32[4,48,128]{2,1,0:T(8,128)S(1)}, u32[]{:S(2)}, u32[]{:S(2)}) collective-permute-start(f32[4,48,128]{2,1,0:T(8,128)S(1)} %pad_maximum_fusion.1.mine_ref), channel_id=1, source_target_pairs={{0,1},{1,0},{2,3},{3,2},{4,5},{5,4},{6,7},{7,6},{8,9},{9,8},{10,11... | collective-permute-start | bytes 294920 | tf_op jit(solution)/shard_map/ppermute | solution.py:597
  73.9 0.0 collective-permute-done.9
  73.9 0.0 collective-permute-done.10
  73.9 0.1 pad_maximum_fusion.stiff_ref
  74.0 0.9 collective-permute-done.5.theirs_ref
  74.9 0.0 copy-done.1
  74.9 4.1 %powers.1 = (f32[3,16,32,128]{3,2,1,0:T(8,128)S(1)}, f32[3,16,32,128]{3,2,1,0:T(8,128)S(1)}, f32[3,16,32,128]{3,2,1,0:T(8,128)S(1)}, f32[3,16,32,128]{3,2,1,0:T(8,128)S(1)}, f32[1,16]{1,0:T(1,128)S(1)}) custom-call(f32[33]{0:T(128)S(1)} %pad_maximum_fusion.7.scalars_hbm, f32[3,48,128]{2,1,0:T(8,128)S(1)} %maximum_maximum_fusion.guide_ref, ...), custom_call_target="tpu_custom_call" | custom-call | flops 100000000 | bytes 4194304 | tf_op jit(solution)/shard_map/powers/pallas_call | solution.py:461
  79.0 1.1 %collective-permute-start.11 = (f32[1,16]{1,0:T(1,128)S(1)}, f32[1,16]{1,0:T(1,128)S(1)}, u32[]{:S(2)}, u32[]{:S(2)}) collective-permute-start(f32[1,16]{1,0:T(1,128)S(1)} %get-tuple-element.21), channel_id=1, source_target_pairs={{0,1},{1,0},{2,3},{3,2},{4,5},{5,4},{6,7},{7,6},{8,9},{9,8},{10,11... | collective-permute-start | bytes 200 | tf_op jit(solution)/shard_map/ppermute | solution.py:597
  80.1 0.8 collective-permute-done.11
  81.0 22.4 %all_to_all.13 = f32[64,1,16]{2,1,0:T(1,128)S(1)} all-to-all(f32[64,1,16]{2,1,0:T(1,128)S(1)} %broadcast_in_dim.28), channel_id=1, replica_groups=mesh['grp'=2,'gx'=16,'gy'=4,'gz'=2] {'gy','gx'}, dimensions={0} | all-to-all | bytes 8192 | tf_op jit(solution)/shard_map/all_to_all | solution.py:658
  103.4 1.6 %finish.1 = (f32[3,16,32,128]{3,2,1,0:T(8,128)}, f32[3,16,32,128]{3,2,1,0:T(8,128)}) custom-call(f32[64,16]{1,0:T(8,128)S(1)} %bitcast.12, f32[3,16,32,128]{3,2,1,0:T(8,128)S(1)} %get-tuple-element.22.zero_ref, f32[3,16,32,128]{3,2,1,0:T(8,128)S(1)} %get-tuple-element.23.one_ref, f32[3,16,32,128]{3,2,1,0:T(8,128)S(1)} %get-tuple-element.24.two_ref, ...), custom_call_target="tpu_custom_call" | custom-call | flops 20000000 | bytes 4194304 | tf_op jit(solution)/shard_map/finish/pallas_call | solution.py:570
  (15 shorter events, 0.1 us)
Async XLA Ops:
  0.6 34.3 %copy-start = (f32[16,32,128]{2,1,0:T(8,128)S(1)}, f32[16,32,128]{2,1,0:T(8,128)}, u32[]{:S(2)}) copy-start(f32[16,32,128]{2,1,0:T(8,128)} %own_ref) | copy-start | bytes 786436
  0.6 33.3 %copy-start.2 = (f32[16]{0:T(128)S(1)}, f32[16]{0:T(128)}, u32[]{:S(2)}) copy-start(f32[16]{0:T(128)} %param.20) | copy-start | bytes 196
  4.3 53.9 %all-to-all-start = ((f32[64,1,1664]{2,1,0:T(1,128)}), f32[64,1,1664]{2,1,0:T(1,128)S(1)}, u32[]{:S(2)}, u32[]{:S(2)}) async-start(f32[64,1,1664]{2,1,0:T(1,128)} %get-tuple-element.16), calls=%async_computation | async-start | bytes 851968 | tf_op jit(solution)/shard_map/all_to_all | solution.py:629
  34.0 40.9 %copy-start.1 = (f32[1,16]{1,0:T(1,128)S(1)}, f32[1,16]{1,0:T(1,128)}, u32[]{:S(2)}) copy-start(f32[1,16]{1,0:T(1,128)} %get-tuple-element.20.tally_ref) | copy-start | bytes 196
  34.0 5.3 %collective-permute-start = (f32[16]{0:T(128)S(1)}, f32[16]{0:T(128)S(1)}, u32[]{:S(2)}, u32[]{:S(2)}) collective-permute-start(f32[16]{0:T(128)S(1)} %copy-done.2), channel_id=1, source_target_pairs={{0,1},{1,0},{2,3},{3,2},{4,5},{5,4},{6,7},{7,6},{8,9},{9,8},{10,11... | collective-permute-start | bytes 200 | tf_op jit(solution)/shard_map/ppermute | solution.py:597
  35.0 1.4 %collective-permute-start.6 = (f32[4,32,128]{2,1,0:T(8,128)S(1)}, f32[4,32,128]{2,1,0:T(8,128)S(1)}, u32[]{:S(2)}, u32[]{:S(2)}) collective-permute-start(f32[4,32,128]{2,1,0:T(8,128)S(1)} %slice_select_fusion), channel_id=1, source_target_pairs={{0,1},{1,0},{2,3},{3,2},{4,5},{5,4},{6,7},{7,6},{8,9},{9,8},{10,11... | collective-permute-start | bytes 196616 | tf_op jit(solution)/shard_map/ppermute | solution.py:597
  36.5 25.7 %collective-permute-start.8 = (f32[2,32,128]{2,1,0:T(8,128)S(1)}, f32[2,32,128]{2,1,0:T(8,128)S(1)}, u32[]{:S(2)}, u32[]{:S(2)}) collective-permute-start(f32[2,32,128]{2,1,0:T(8,128)S(1)} %pack.1), channel_id=1, source_target_pairs={{0,2},{2,4},{4,6},{6,0},{1,3},{3,5},{5,7},{7,1},{8,10},{10,12},{12... | collective-permute-start | bytes 98312 | tf_op jit(solution)/shard_map/ppermute | solution.py:588
  37.1 25.2 %collective-permute-start.7 = (f32[2,32,128]{2,1,0:T(8,128)S(1)}, f32[2,32,128]{2,1,0:T(8,128)S(1)}, u32[]{:S(2)}, u32[]{:S(2)}) collective-permute-start(f32[2,32,128]{2,1,0:T(8,128)S(1)} %pack.1), channel_id=1, source_target_pairs={{2,0},{4,2},{6,4},{0,6},{3,1},{5,3},{7,5},{1,7},{10,8},{12,10},{14... | collective-permute-start | bytes 98312 | tf_op jit(solution)/shard_map/ppermute | solution.py:593
  59.1 4.2 %collective-permute-start.2 = (f32[32,128]{1,0:T(8,128)S(1)}, f32[32,128]{1,0:T(8,128)S(1)}, u32[]{:S(2)}, u32[]{:S(2)}) collective-permute-start(f32[32,128]{1,0:T(8,128)S(1)} %get-tuple-element.18), channel_id=1, source_target_pairs={{0,2},{2,4},{4,6},{6,0},{1,3},{3,5},{5,7},{7,1},{8,10},{10,12},{12... | collective-permute-start | bytes 49160 | tf_op jit(solution)/shard_map/ppermute | solution.py:588
  60.3 3.0 %collective-permute-start.1 = (f32[32,128]{1,0:T(8,128)S(1)}, f32[32,128]{1,0:T(8,128)S(1)}, u32[]{:S(2)}, u32[]{:S(2)}) collective-permute-start(f32[32,128]{1,0:T(8,128)S(1)} %get-tuple-element.18), channel_id=1, source_target_pairs={{2,0},{4,2},{6,4},{0,6},{3,1},{5,3},{7,5},{1,7},{10,8},{12,10},{14... | collective-permute-start | bytes 49160 | tf_op jit(solution)/shard_map/ppermute | solution.py:593
  63.3 5.6 %collective-permute-start.3 = (f32[4,8,128]{2,1,0:T(8,128)S(1)}, f32[4,8,128]{2,1,0:T(8,128)S(1)}, u32[]{:S(2)}, u32[]{:S(2)}) collective-permute-start(f32[4,8,128]{2,1,0:T(8,128)S(1)} %get-tuple-element.30), channel_id=1, source_target_pairs={{0,8},{8,16},{16,24},{24,32},{32,40},{40,48},{48,56},{56,64},{64,7... | collective-permute-start | bytes 49160 | tf_op jit(solution)/shard_map/ppermute | solution.py:588
  65.8 3.1 %collective-permute-start.4 = (f32[4,8,128]{2,1,0:T(8,128)S(1)}, f32[4,8,128]{2,1,0:T(8,128)S(1)}, u32[]{:S(2)}, u32[]{:S(2)}) collective-permute-start(f32[4,8,128]{2,1,0:T(8,128)S(1)} %get-tuple-element.31), channel_id=1, source_target_pairs={{8,0},{16,8},{24,16},{32,24},{40,32},{48,40},{56,48},{64,56},{72,6... | collective-permute-start | bytes 49160 | tf_op jit(solution)/shard_map/ppermute | solution.py:593
  66.1 7.8 %collective-permute-start.9 = (f32[22,4,128]{2,1,0:T(4,128)S(1)}, f32[22,4,128]{2,1,0:T(4,128)S(1)}, u32[]{:S(2)}, u32[]{:S(2)}) collective-permute-start(f32[22,4,128]{2,1,0:T(4,128)S(1)} %get-tuple-element.28), channel_id=1, source_target_pairs={{0,8},{8,16},{16,24},{24,32},{32,40},{40,48},{48,56},{56,64},{64,7... | collective-permute-start | bytes 135176 | tf_op jit(solution)/shard_map/ppermute | solution.py:588
  67.4 6.5 %collective-permute-start.10 = (f32[22,4,128]{2,1,0:T(4,128)S(1)}, f32[22,4,128]{2,1,0:T(4,128)S(1)}, u32[]{:S(2)}, u32[]{:S(2)}) collective-permute-start(f32[22,4,128]{2,1,0:T(4,128)S(1)} %get-tuple-element.29), channel_id=1, source_target_pairs={{8,0},{16,8},{24,16},{32,24},{40,32},{48,40},{56,48},{64,56},{72,6... | collective-permute-start | bytes 135176 | tf_op jit(solution)/shard_map/ppermute | solution.py:593
  68.9 6.0 %collective-permute-start.5 = (f32[4,48,128]{2,1,0:T(8,128)S(1)}, f32[4,48,128]{2,1,0:T(8,128)S(1)}, u32[]{:S(2)}, u32[]{:S(2)}) collective-permute-start(f32[4,48,128]{2,1,0:T(8,128)S(1)} %pad_maximum_fusion.1.mine_ref), channel_id=1, source_target_pairs={{0,1},{1,0},{2,3},{3,2},{4,5},{5,4},{6,7},{7,6},{8,9},{9,8},{10,11... | collective-permute-start | bytes 294920 | tf_op jit(solution)/shard_map/ppermute | solution.py:597
  79.0 2.0 %collective-permute-start.11 = (f32[1,16]{1,0:T(1,128)S(1)}, f32[1,16]{1,0:T(1,128)S(1)}, u32[]{:S(2)}, u32[]{:S(2)}) collective-permute-start(f32[1,16]{1,0:T(1,128)S(1)} %get-tuple-element.21), channel_id=1, source_target_pairs={{0,1},{1,0},{2,3},{3,2},{4,5},{5,4},{6,7},{7,6},{8,9},{9,8},{10,11... | collective-permute-start | bytes 200 | tf_op jit(solution)/shard_map/ppermute | solution.py:597

commit v7 on v6

--- a/solution.py
+++ b/solution.py
@@ -219,14 +219,12 @@
     ids = got_ref[:, 3 * CAP * cells :]
     total = jnp.zeros((places, 3 * cells), F32)
     for r in range(CAP):
-        hot = (ids[:, r : r + 1] == place).astype(F32)
-        total += lax.dot_general(
-            hot,
-            got_ref[:, r * 3 * cells : (r + 1) * 3 * cells],
-            (((0,), (0,)), ((), ())),
-            precision=lax.Precision.HIGHEST,
-            preferred_element_type=F32,
-        )
+        hot = (ids[:, r : r + 1] == place).astype(jnp.bfloat16)
+        rest = got_ref[:, r * 3 * cells : (r + 1) * 3 * cells]
+        for _ in range(3):
+            piece = rest.astype(jnp.bfloat16)
+            rest = rest - piece.astype(F32)
+            total += lax.dot_general(hot, piece, (((0,), (0,)), ((), ())), preferred_element_type=F32)
     for c in range(3):
         for i in range(places_x):
             tile = total[i * places_y : (i + 1) * places_y, c * cells : (c + 1) * cells]
@@ -265,7 +263,7 @@
 
 
 def powers_kernel(
-    layers, scalars_hbm, guide_ref, mine_ref, theirs_ref, stiff_ref,
+    layers, scalars_hbm, guide_ref, mine_ref, stiff_ref,
     tally_ref, zero_ref, one_ref, two_ref, three_ref, row_ref, scalars, sem, flat, keep, diag, w1, w2, div1, div2, across1, across2,
 ):
     rows, local_x = stiff_ref.shape[1], one_ref.shape[2]
@@ -274,10 +272,10 @@
     copy.start()
 
     inside = (guide_ref[0], guide_ref[1])
-    edges = mine_ref[3] + theirs_ref[3]
+    edges = mine_ref[3]
 
     def tiles(c):
-        own = mine_ref[c] + theirs_ref[c]
+        own = mine_ref[c]
         side = pltpu.roll(edges, LANES - EDGE - 2 * EDGE * c, 1)
         return inside[0] * own, inside[1] * side
 
@@ -452,7 +450,7 @@
     row_ref[...] = row
 
 
-def powers(layers, scalars, guide, mine, theirs, stiff, tally):
+def powers(layers, scalars, guide, mine, stiff, tally):
     _, rows, lanes = stiff.shape
     tall = mine.shape[1]
     local_x = tall - 2 * EDGE
@@ -467,7 +465,7 @@
             field,
             jax.ShapeDtypeStruct((1, ROW), F32),
         ),
-        in_specs=[ANY] + [VMEM] * 5,
+        in_specs=[ANY] + [VMEM] * 4,
         out_specs=(VMEM,) * 5,
         scratch_shapes=[
             pltpu.SMEM(scalars.shape, F32),
@@ -485,7 +483,7 @@
         compiler_params=pltpu.CompilerParams(vmem_limit_bytes=20 << 20),
         cost_estimate=pl.CostEstimate(flops=100_000_000, bytes_accessed=4 << 20, transcendentals=0),
         name="powers",
-    )(scalars, guide, mine, theirs, stiff, tally)
+    )(scalars, guide, mine, stiff, tally)
 
 
 def step_factors(nu):
@@ -646,13 +644,16 @@
     guide = jnp.stack([in_x.astype(F32), (in_x & in_y).astype(F32), sign.astype(F32)])
 
     part, edges = place(got[:, 0], local_x, local_y)
+    part = jnp.concatenate([part, edges[None]])
+    part = part + from_partner(part, "gz")
+    part, edges = part[:3], part[3]
     side = beside(from_below(edges, "gy"), from_above(edges, "gy"), EDGE)
     mine = jnp.concatenate([part, side[None]])
     mine = jnp.concatenate(
         [from_below(mine[:, local_x - EDGE :, :], "gx"), mine, from_above(mine[:, :EDGE, :], "gx")], axis=1
     )
     zero, one, two, three, row = powers(
-        layers, scalars, guide, mine, from_partner(mine, "gz"), stiff, tally
+        layers, scalars, guide, mine, stiff, tally
     )
     rows = jnp.broadcast_to(row + from_partner(row, "gz"), (owners, ROW))
     rows = lax.all_to_all(rows, ("gy", "gx"), split_axis=0, concat_axis=0, tiled=True)

time: 106 us -> 104 us (0.981)
  blocking collectives: 22.4 us -> 21.3 us
    ppermute x4, starting transfers between devices: 5.92 us -> 9.02 us  [from_above(): lax.ppermute(value, axis, [((i + 1) % count, i) for i in range(count)])]
    ppermute x4, starting transfers between devices: 5.63 us -> 2.61 us  [from_below(): lax.ppermute(value, axis, [(i, (i + 1) % count) for i in range(count)])]
    all_to_all x1, blocking collectives: 22.4 us -> 21.3 us  [per_device(): lax.all_to_all(rows, ('gy', 'gx'), split_axis=0, concat_axis=0, tiled=True)]
  transfers between devices with their start and end apart: 13 -> 13, of which waited for: 5 -> 6; matrix products, arithmetic and copies ran while one was open for 1% -> 1% of each run, Pallas kernels for 1% -> 1%
where the time goes in v7:
time: 104 us; the launch traced here: 103 us
  starting transfers between devices  47.7 us (46%)
  waiting for transfers between devices  22.5 us (22%)
  blocking collectives  21.3 us (20%)
  Pallas kernels  10.1 us (10%)
    all_to_all x1, starting transfers between devices, per_device(): lax.all_to_all(sums, ('gy', 'gx'), split_axis=0, concat_axis=0, tiled=True)  29.6 us
    all_to_all x1, blocking collectives, per_device(): lax.all_to_all(rows, ('gy', 'gx'), split_axis=0, concat_axis=0, tiled=True)  21.3 us
    all_to_all x1, waiting for transfers between devices, per_device(): lax.all_to_all(sums, ('gy', 'gx'), split_axis=0, concat_axis=0, tiled=True)  19 us
    ppermute x4, starting transfers between devices, from_above(): lax.ppermute(value, axis, [((i + 1) % count, i) for i in range(count)])  9.02 us
    ppermute x4, starting transfers between devices, from_partner(): return lax.ppermute(value, axis, [(0, 1), (1, 0)])  6.44 us
    pallas_call x1, Pallas kernels, powers(): pl.pallas_call(functools.partial(powers_kernel, layers), out_shape=(field...  3.93 us
    pallas_call x1, Pallas kernels, front(): pl.pallas_call(functools.partial(front_kernel, size_y), out_shape=(jax.Sh...  3.68 us
    ppermute x4, starting transfers between devices, from_below(): lax.ppermute(value, axis, [(i, (i + 1) % count) for i in range(count)])  2.61 us
  transfers between devices with their start and end apart: 13, of which 6 were waited for; matrix products, arithmetic and copies ran while one was open for 1% of the time, Pallas kernels for 1%

profile of v7, /device:TPU:33, one launch (start us, length us, event | category | flops | bytes accessed | tf_op | source)
XLA Modules:
  0.0 103.1 jit_solution(16022727895019532137)
XLA Ops:
  0.6 0.0 copy-start
  0.6 0.0 copy-start.2
  0.7 3.7 %front.1 = (f32[64,1,1664]{2,1,0:T(1,128)}, f32[1,16]{1,0:T(1,128)}) custom-call(s32[64]{0:T(128)} %count_hbm.1, f32[4,3]{1,0:T(4,128)} %look_hbm.1, s32[64]{0:T(128)} %bitcast.18, s32[64]{0:T(128)} %patch_hbm.1, s32[64]{0:T(128)} %choice_hbm.1, f32[64,4,256]{2,1,0:T(4,128)} %observed_hbm.1, f32[64,4,256]{2,1,0:T(4,128)} %predicted_hbm.1, ...), custom_call_target="tpu_custom_call" | custom-call | flops 400000000 | bytes 4194304 | tf_op jit(solution)/shard_map/front/pallas_call | solution.py:144
  4.3 29.6 %all-to-all-start = ((f32[64,1,1664]{2,1,0:T(1,128)}), f32[64,1,1664]{2,1,0:T(1,128)S(1)}, u32[]{:S(2)}, u32[]{:S(2)}) async-start(f32[64,1,1664]{2,1,0:T(1,128)} %get-tuple-element.16), calls=%async_computation | async-start | bytes 851968 | tf_op jit(solution)/shard_map/all_to_all | solution.py:627
  33.9 0.0 copy-done.2
  34.0 1.0 collective-permute-start
  35.0 0.0 copy-done
  35.0 0.0 copy-start.1
  35.0 0.2 collective-permute-start.6
  35.2 0.1 pad.18.clone
  35.3 0.1 and_convert_fusion
  35.4 0.1 iota.38
  35.4 0.1 maximum_maximum_fusion.guide_ref
  35.5 0.3 collective-permute-done
  35.8 0.1 pad_maximum_fusion.8.scalars_hbm
  35.9 0.5 collective-permute-done.6.far_ref
  36.4 0.1 pack.1
  36.5 0.5 collective-permute-start.8
  37.1 2.2 %collective-permute-start.7 = (f32[2,32,128]{2,1,0:T(8,128)S(1)}, f32[2,32,128]{2,1,0:T(8,128)S(1)}, u32[]{:S(2)}, u32[]{:S(2)}) collective-permute-start(f32[2,32,128]{2,1,0:T(8,128)S(1)} %pack.1), channel_id=1, source_target_pairs={{2,0},{4,2},{6,4},{0,6},{3,1},{5,3},{7,5},{1,7},{10,8},{12,10},{14... | collective-permute-start | bytes 98312 | tf_op jit(solution)/shard_map/ppermute | solution.py:591
  39.3 19.0 %all-to-all-done = f32[64,1,1664]{2,1,0:T(1,128)S(1)} async-done(((f32[64,1,1664]{2,1,0:T(1,128)}), f32[64,1,1664]{2,1,0:T(1,128)S(1)}, u32[]{:S(2)}, u32[]{:S(2)}) %all-to-all-start) | async-done | bytes 426016 | tf_op jit(solution)/shard_map/all_to_all | solution.py:627
  58.3 0.7 place.1
  59.0 2.8 %collective-permute-start.1 = (f32[4,32,128]{2,1,0:T(8,128)S(1)}, f32[4,32,128]{2,1,0:T(8,128)S(1)}, u32[]{:S(2)}, u32[]{:S(2)}) collective-permute-start(f32[4,32,128]{2,1,0:T(8,128)S(1)} %pad_maximum_fusion.2), channel_id=1, source_target_pairs={{0,1},{1,0},{2,3},{3,2},{4,5},{5,4},{6,7},{7,6},{8,9},{9,8},{10,11... | collective-permute-start | bytes 196616 | tf_op jit(solution)/shard_map/ppermute | solution.py:595
  61.8 0.0 collective-permute-done.8
  61.8 0.0 collective-permute-done.7
  61.8 0.9 collective-permute-done.1
  62.7 1.3 %collective-permute-start.3 = (f32[32,128]{1,0:T(8,128)S(1)}, f32[32,128]{1,0:T(8,128)S(1)}, u32[]{:S(2)}, u32[]{:S(2)}) collective-permute-start(f32[32,128]{1,0:T(8,128)S(1)} %slice_bitcast_fusion), channel_id=1, source_target_pairs={{0,2},{2,4},{4,6},{6,0},{1,3},{3,5},{5,7},{7,1},{8,10},{10,12},{12... | collective-permute-start | bytes 49160 | tf_op jit(solution)/shard_map/ppermute | solution.py:586
  64.0 2.0 %collective-permute-start.2 = (f32[32,128]{1,0:T(8,128)S(1)}, f32[32,128]{1,0:T(8,128)S(1)}, u32[]{:S(2)}, u32[]{:S(2)}) collective-permute-start(f32[32,128]{1,0:T(8,128)S(1)} %slice_bitcast_fusion), channel_id=1, source_target_pairs={{2,0},{4,2},{6,4},{0,6},{3,1},{5,3},{7,5},{1,7},{10,8},{12,10},{14... | collective-permute-start | bytes 49160 | tf_op jit(solution)/shard_map/ppermute | solution.py:591
  66.0 0.6 collective-permute-start.9
  66.6 2.1 %collective-permute-start.10 = (f32[22,4,128]{2,1,0:T(4,128)S(1)}, f32[22,4,128]{2,1,0:T(4,128)S(1)}, u32[]{:S(2)}, u32[]{:S(2)}) collective-permute-start(f32[22,4,128]{2,1,0:T(4,128)S(1)} %get-tuple-element.29), channel_id=1, source_target_pairs={{8,0},{16,8},{24,16},{32,24},{40,32},{48,40},{56,48},{64,56},{72,6... | collective-permute-start | bytes 135176 | tf_op jit(solution)/shard_map/ppermute | solution.py:591
  68.8 0.0 collective-permute-done.3
  68.8 0.0 collective-permute-done.2
  68.8 0.1 collective-permute-start.4
  69.0 2.7 %collective-permute-start.5 = (f32[4,8,128]{2,1,0:T(8,128)S(1)}, f32[4,8,128]{2,1,0:T(8,128)S(1)}, u32[]{:S(2)}, u32[]{:S(2)}) collective-permute-start(f32[4,8,128]{2,1,0:T(8,128)S(1)} %get-tuple-element.31), channel_id=1, source_target_pairs={{8,0},{16,8},{24,16},{32,24},{40,32},{48,40},{56,48},{64,56},{72,6... | collective-permute-start | bytes 49160 | tf_op jit(solution)/shard_map/ppermute | solution.py:591
  71.6 0.0 collective-permute-done.9
  71.6 0.0 collective-permute-done.10
  71.6 0.1 pad_maximum_fusion.stiff_ref
  71.7 1.1 %collective-permute-done.4 = f32[4,8,128]{2,1,0:T(8,128)S(1)} collective-permute-done((f32[4,8,128]{2,1,0:T(8,128)S(1)}, f32[4,8,128]{2,1,0:T(8,128)S(1)}, u32[]{:S(2)}, u32[]{:S(2)}) %collective-permute-start.4) | collective-permute-done | bytes 16416 | tf_op jit(solution)/shard_map/ppermute | solution.py:586
  72.7 0.0 collective-permute-done.5
  72.7 0.0 copy-done.1
  72.8 3.9 %powers.1 = (f32[3,16,32,128]{3,2,1,0:T(8,128)S(1)}, f32[3,16,32,128]{3,2,1,0:T(8,128)S(1)}, f32[3,16,32,128]{3,2,1,0:T(8,128)S(1)}, f32[3,16,32,128]{3,2,1,0:T(8,128)S(1)}, f32[1,16]{1,0:T(1,128)S(1)}) custom-call(f32[33]{0:T(128)S(1)} %pad_maximum_fusion.8.scalars_hbm, f32[3,48,128]{2,1,0:T(8,128)S(1)} %maximum_maximum_fusion.guide_ref, ...), custom_call_target="tpu_custom_call" | custom-call | flops 100000000 | bytes 4194304 | tf_op jit(solution)/shard_map/powers/pallas_call | solution.py:459
  76.7 2.5 %collective-permute-start.11 = (f32[1,16]{1,0:T(1,128)S(1)}, f32[1,16]{1,0:T(1,128)S(1)}, u32[]{:S(2)}, u32[]{:S(2)}) collective-permute-start(f32[1,16]{1,0:T(1,128)S(1)} %get-tuple-element.21), channel_id=1, source_target_pairs={{0,1},{1,0},{2,3},{3,2},{4,5},{5,4},{6,7},{7,6},{8,9},{9,8},{10,11... | collective-permute-start | bytes 200 | tf_op jit(solution)/shard_map/ppermute | solution.py:595
  79.2 0.8 collective-permute-done.11
  80.0 21.3 %all_to_all.13 = f32[64,1,16]{2,1,0:T(1,128)S(1)} all-to-all(f32[64,1,16]{2,1,0:T(1,128)S(1)} %broadcast_in_dim.32), channel_id=1, replica_groups=mesh['grp'=2,'gx'=16,'gy'=4,'gz'=2] {'gy','gx'}, dimensions={0} | all-to-all | bytes 8192 | tf_op jit(solution)/shard_map/all_to_all | solution.py:659
  101.3 1.6 %finish.1 = (f32[3,16,32,128]{3,2,1,0:T(8,128)}, f32[3,16,32,128]{3,2,1,0:T(8,128)}) custom-call(f32[64,16]{1,0:T(8,128)S(1)} %bitcast.15, f32[3,16,32,128]{3,2,1,0:T(8,128)S(1)} %get-tuple-element.22.zero_ref, f32[3,16,32,128]{3,2,1,0:T(8,128)S(1)} %get-tuple-element.23.one_ref, f32[3,16,32,128]{3,2,1,0:T(8,128)S(1)} %get-tuple-element.24.two_ref, ...), custom_call_target="tpu_custom_call" | custom-call | flops 20000000 | bytes 4194304 | tf_op jit(solution)/shard_map/finish/pallas_call | solution.py:568
  (19 shorter events, 0.2 us)
Async XLA Ops:
  0.6 34.3 %copy-start = (f32[16,32,128]{2,1,0:T(8,128)S(1)}, f32[16,32,128]{2,1,0:T(8,128)}, u32[]{:S(2)}) copy-start(f32[16,32,128]{2,1,0:T(8,128)} %own_ref) | copy-start | bytes 786436
  0.6 33.3 %copy-start.2 = (f32[16]{0:T(128)S(1)}, f32[16]{0:T(128)}, u32[]{:S(2)}) copy-start(f32[16]{0:T(128)} %param.20) | copy-start | bytes 196
  4.3 53.9 %all-to-all-start = ((f32[64,1,1664]{2,1,0:T(1,128)}), f32[64,1,1664]{2,1,0:T(1,128)S(1)}, u32[]{:S(2)}, u32[]{:S(2)}) async-start(f32[64,1,1664]{2,1,0:T(1,128)} %get-tuple-element.16), calls=%async_computation | async-start | bytes 851968 | tf_op jit(solution)/shard_map/all_to_all | solution.py:627
  34.0 1.8 %collective-permute-start = (f32[16]{0:T(128)S(1)}, f32[16]{0:T(128)S(1)}, u32[]{:S(2)}, u32[]{:S(2)}) collective-permute-start(f32[16]{0:T(128)S(1)} %copy-done.2), channel_id=1, source_target_pairs={{0,1},{1,0},{2,3},{3,2},{4,5},{5,4},{6,7},{7,6},{8,9},{9,8},{10,11... | collective-permute-start | bytes 200 | tf_op jit(solution)/shard_map/ppermute | solution.py:595
  35.0 37.8 %copy-start.1 = (f32[1,16]{1,0:T(1,128)S(1)}, f32[1,16]{1,0:T(1,128)}, u32[]{:S(2)}) copy-start(f32[1,16]{1,0:T(1,128)} %get-tuple-element.20.tally_ref) | copy-start | bytes 196
  35.0 1.4 %collective-permute-start.6 = (f32[4,32,128]{2,1,0:T(8,128)S(1)}, f32[4,32,128]{2,1,0:T(8,128)S(1)}, u32[]{:S(2)}, u32[]{:S(2)}) collective-permute-start(f32[4,32,128]{2,1,0:T(8,128)S(1)} %slice_select_fusion), channel_id=1, source_target_pairs={{0,1},{1,0},{2,3},{3,2},{4,5},{5,4},{6,7},{7,6},{8,9},{9,8},{10,11... | collective-permute-start | bytes 196616 | tf_op jit(solution)/shard_map/ppermute | solution.py:595
  36.5 25.2 %collective-permute-start.8 = (f32[2,32,128]{2,1,0:T(8,128)S(1)}, f32[2,32,128]{2,1,0:T(8,128)S(1)}, u32[]{:S(2)}, u32[]{:S(2)}) collective-permute-start(f32[2,32,128]{2,1,0:T(8,128)S(1)} %pack.1), channel_id=1, source_target_pairs={{0,2},{2,4},{4,6},{6,0},{1,3},{3,5},{5,7},{7,1},{8,10},{10,12},{12... | collective-permute-start | bytes 98312 | tf_op jit(solution)/shard_map/ppermute | solution.py:586
  37.1 24.7 %collective-permute-start.7 = (f32[2,32,128]{2,1,0:T(8,128)S(1)}, f32[2,32,128]{2,1,0:T(8,128)S(1)}, u32[]{:S(2)}, u32[]{:S(2)}) collective-permute-start(f32[2,32,128]{2,1,0:T(8,128)S(1)} %pack.1), channel_id=1, source_target_pairs={{2,0},{4,2},{6,4},{0,6},{3,1},{5,3},{7,5},{1,7},{10,8},{12,10},{14... | collective-permute-start | bytes 98312 | tf_op jit(solution)/shard_map/ppermute | solution.py:591
  59.0 3.7 %collective-permute-start.1 = (f32[4,32,128]{2,1,0:T(8,128)S(1)}, f32[4,32,128]{2,1,0:T(8,128)S(1)}, u32[]{:S(2)}, u32[]{:S(2)}) collective-permute-start(f32[4,32,128]{2,1,0:T(8,128)S(1)} %pad_maximum_fusion.2), channel_id=1, source_target_pairs={{0,1},{1,0},{2,3},{3,2},{4,5},{5,4},{6,7},{7,6},{8,9},{9,8},{10,11... | collective-permute-start | bytes 196616 | tf_op jit(solution)/shard_map/ppermute | solution.py:595
  62.7 6.1 %collective-permute-start.3 = (f32[32,128]{1,0:T(8,128)S(1)}, f32[32,128]{1,0:T(8,128)S(1)}, u32[]{:S(2)}, u32[]{:S(2)}) collective-permute-start(f32[32,128]{1,0:T(8,128)S(1)} %slice_bitcast_fusion), channel_id=1, source_target_pairs={{0,2},{2,4},{4,6},{6,0},{1,3},{3,5},{5,7},{7,1},{8,10},{10,12},{12... | collective-permute-start | bytes 49160 | tf_op jit(solution)/shard_map/ppermute | solution.py:586
  64.0 4.8 %collective-permute-start.2 = (f32[32,128]{1,0:T(8,128)S(1)}, f32[32,128]{1,0:T(8,128)S(1)}, u32[]{:S(2)}, u32[]{:S(2)}) collective-permute-start(f32[32,128]{1,0:T(8,128)S(1)} %slice_bitcast_fusion), channel_id=1, source_target_pairs={{2,0},{4,2},{6,4},{0,6},{3,1},{5,3},{7,5},{1,7},{10,8},{12,10},{14... | collective-permute-start | bytes 49160 | tf_op jit(solution)/shard_map/ppermute | solution.py:591
  66.0 5.6 %collective-permute-start.9 = (f32[22,4,128]{2,1,0:T(4,128)S(1)}, f32[22,4,128]{2,1,0:T(4,128)S(1)}, u32[]{:S(2)}, u32[]{:S(2)}) collective-permute-start(f32[22,4,128]{2,1,0:T(4,128)S(1)} %get-tuple-element.28), channel_id=1, source_target_pairs={{0,8},{8,16},{16,24},{24,32},{32,40},{40,48},{48,56},{56,64},{64,7... | collective-permute-start | bytes 135176 | tf_op jit(solution)/shard_map/ppermute | solution.py:586
  66.6 5.0 %collective-permute-start.10 = (f32[22,4,128]{2,1,0:T(4,128)S(1)}, f32[22,4,128]{2,1,0:T(4,128)S(1)}, u32[]{:S(2)}, u32[]{:S(2)}) collective-permute-start(f32[22,4,128]{2,1,0:T(4,128)S(1)} %get-tuple-element.29), channel_id=1, source_target_pairs={{8,0},{16,8},{24,16},{32,24},{40,32},{48,40},{56,48},{64,56},{72,6... | collective-permute-start | bytes 135176 | tf_op jit(solution)/shard_map/ppermute | solution.py:591
  68.8 3.9 %collective-permute-start.4 = (f32[4,8,128]{2,1,0:T(8,128)S(1)}, f32[4,8,128]{2,1,0:T(8,128)S(1)}, u32[]{:S(2)}, u32[]{:S(2)}) collective-permute-start(f32[4,8,128]{2,1,0:T(8,128)S(1)} %get-tuple-element.30), channel_id=1, source_target_pairs={{0,8},{8,16},{16,24},{24,32},{32,40},{40,48},{48,56},{56,64},{64,7... | collective-permute-start | bytes 49160 | tf_op jit(solution)/shard_map/ppermute | solution.py:586
  69.0 3.8 %collective-permute-start.5 = (f32[4,8,128]{2,1,0:T(8,128)S(1)}, f32[4,8,128]{2,1,0:T(8,128)S(1)}, u32[]{:S(2)}, u32[]{:S(2)}) collective-permute-start(f32[4,8,128]{2,1,0:T(8,128)S(1)} %get-tuple-element.31), channel_id=1, source_target_pairs={{8,0},{16,8},{24,16},{32,24},{40,32},{48,40},{56,48},{64,56},{72,6... | collective-permute-start | bytes 49160 | tf_op jit(solution)/shard_map/ppermute | solution.py:591
  76.7 3.3 %collective-permute-start.11 = (f32[1,16]{1,0:T(1,128)S(1)}, f32[1,16]{1,0:T(1,128)S(1)}, u32[]{:S(2)}, u32[]{:S(2)}) collective-permute-start(f32[1,16]{1,0:T(1,128)S(1)} %get-tuple-element.21), channel_id=1, source_target_pairs={{0,1},{1,0},{2,3},{3,2},{4,5},{5,4},{6,7},{7,6},{8,9},{9,8},{10,11... | collective-permute-start | bytes 200 | tf_op jit(solution)/shard_map/ppermute | solution.py:595
